TPU v7x, 128 devices: a whole 4x4x4 slice. The times are simulated.
128 devices in a mesh: ma: 32 (over y, z, core), pb: 4 (over x).
Axes of the slice: x: 4, y: 4, z: 4, core: 2. Of those that a mesh axis runs over, the one named last changes fastest.
Arguments:
- coefs: float32 [512, 1056, 64], P('ma', 'pb'), may hold values from -6 to 6
- legendre: float32 [512, 1056, 4, 256], P('ma', None, 'pb'), may hold values from -0.25 to 0.25
- quad_weight: float32 [4, 256], P('pb'), may hold values from 0.3 to 3
- pair_of_slot: int32 [512], replicated, may hold values from 0 to 511, each once
- tracers: float32 [12, 2, 1024, 2048], P(None, None, ('ma', 'pb')), may hold values from 0 to 2
- heat_rate: float32 [12, 2], replicated, may hold values from -1.75 to 1.75
Outputs:
- spec_tendency: float32 [512, 1056, 64], P('ma', 'pb')
- tracers_new: float32 [12, 2, 1024, 2048], P(None, None, ('ma', 'pb'))
Inputs may be any that keep to these rules, and one draw needn't show every extreme that they name: Each pair number appears once; slot s holds the orders pair_of_slot[s] and 1023 - pair_of_slot[s].
All inputs are finite; a program needn't handle non-finite values.
Results may differ from a plain program's by a relative error of at most 0.00007.
Values sent between devices are 32-bit elements; how exact they have to be, the bound alone decides.
No kernel may reach another device: no remote copies, remote signals or barrier semaphores. Data moves between devices by JAX's collectives and lax.ppermute only.
A program may use at most 128 MiB of HBM per device.

v0:
```python
import math

import jax
import jax.numpy as jnp
from jax import lax
from jax.sharding import PartitionSpec as P

M = 1024
NLAT = 1024
NLON = 2048
LAYER_TOTAL = 8
NF = 4
NTR = 12
TLEV = 2
PAIRS = 512


COURANT = 0.15
DRAG_COEFFICIENT = 0.2
MOISTURE_SOURCE = 0.3
RAINFALL_FACTOR = 0.2
HIGHEST = lax.Precision.HIGHEST


def extended(array, sides, width):
    edges = {}
    for axis, dim in sides:
        count, length = (lax.axis_size(axis), array.shape[dim])
        up = [(i, (i + 1) % count) for i in range(count - 1)]
        last = lax.slice_in_dim(array, length - width, length, axis=dim)
        initial = lax.slice_in_dim(array, 0, width, axis=dim)
        edges[dim] = (
            lax.ppermute(last, axis, up),
            lax.ppermute(initial, axis, [(b, a) for a, b in up]),
        )
    done = []
    for _, dim in sides:
        low, high = edges[dim]
        around = [(width, width) if d in done else (0, 0) for d in range(array.ndim)]
        array = jnp.concatenate([jnp.pad(low, around), array, jnp.pad(high, around)], axis=dim)
        done.append(dim)
    return array


def order_tables(pair_of_slot):
    orders = jnp.stack([pair_of_slot, M - 1 - pair_of_slot], axis=1)
    points = jnp.arange(NLON, dtype=jnp.int32)
    phases = orders[:, :, None] * points[None, None, :] % NLON
    angles = phases.astype(jnp.float32) * (2.0 * math.pi / NLON)
    factor = 1.0 / math.sqrt(NLON)
    fourier_table = jnp.stack([jnp.cos(angles) * factor, -jnp.sin(angles) * factor], axis=0)
    weights = jnp.where(orders == 0, 1.0, 2.0).astype(jnp.float32)
    return (fourier_table, weights)


def row_masks(pair_ids, row_count):
    row_ids = jnp.arange(row_count, dtype=jnp.int32)
    bounds = (M - pair_ids)[:, None]
    low_rows = row_ids[None, :] < bounds
    high_rows = (row_ids[None, :] >= bounds) & (row_ids[None, :] <= M)
    return (low_rows, high_rows)


def advect(padded, zonal_wind, southward, first_row):
    middle = padded[:, :, 1:-1, :]
    east_face = 0.5 * (zonal_wind + jnp.roll(zonal_wind, -1, axis=-1))
    flux_east = jnp.maximum(east_face, 0.0) * middle + jnp.minimum(east_face, 0.0) * jnp.roll(
        middle, -1, axis=-1
    )
    across = 0.5 * (southward[:, :-1, :] + southward[:, 1:, :])
    flux_south = (
        jnp.maximum(across, 0.0) * padded[:, :, :-1, :]
        + jnp.minimum(across, 0.0) * padded[:, :, 1:, :]
    )
    upper_row = first_row - 1 + jnp.arange(across.shape[1], dtype=jnp.int32)
    inside = (upper_row >= 0) & (upper_row <= NLAT - 2)
    flux_south = jnp.where(inside[None, None, :, None], flux_south, 0.0)
    change = (
        flux_east
        - jnp.roll(flux_east, 1, axis=-1)
        + (flux_south[:, :, 1:, :] - flux_south[:, :, :-1, :])
    )
    return -COURANT * change


def shards(coefs, legendre, quad_weight, pair_of_slot, tracers, heat_rate):
    slot_count = coefs.shape[0]
    row_block = coefs.shape[1]
    columns = coefs.shape[2]
    quarter = legendre.shape[3]
    legendre_rows = legendre.reshape(slot_count, legendre.shape[1], quarter)
    own_pairs = lax.dynamic_slice_in_dim(
        pair_of_slot, lax.axis_index("ma") * slot_count, slot_count, 0
    )
    row_piece = lax.all_gather(coefs, "pb", axis=1, tiled=True)
    row_count = row_piece.shape[1]
    low_rows, high_rows = row_masks(own_pairs, row_count)
    masked = jnp.concatenate(
        [
            jnp.where(low_rows[:, :, None], row_piece, 0.0),
            jnp.where(high_rows[:, :, None], row_piece, 0.0),
        ],
        axis=2,
    )
    table_rows = legendre_rows
    legendre_sum = jnp.einsum("srl,src->slc", table_rows, masked, precision=HIGHEST)
    bands = lax.all_to_all(legendre_sum, "ma", split_axis=1, concat_axis=0, tiled=True)
    band_rows = bands.shape[1]
    fourier_table, weights = order_tables(pair_of_slot)
    spectral = (
        bands.reshape(PAIRS, band_rows, 2, 2, NF * LAYER_TOTAL) * weights[:, None, :, None, None]
    )
    physical_space_field = jnp.einsum("sjhpc,pshi->jci", spectral, fourier_table, precision=HIGHEST)
    zonal_wind = jnp.transpose(physical_space_field[:, 0:TLEV, :], (1, 0, 2))
    southward = -jnp.transpose(
        physical_space_field[:, LAYER_TOTAL : LAYER_TOTAL + TLEV, :], (1, 0, 2)
    )
    first_row = lax.axis_index(("ma", "pb")) * band_rows
    stacked = jnp.concatenate([tracers, zonal_wind[None], southward[None]], axis=0)
    widened = extended(stacked, ((("ma", "pb"), 2),), 3)
    anchor = widened[:NTR]
    zonal_ext = widened[NTR]
    south_ext = widened[NTR + 1]
    first_section = anchor[:, :, 1:-1] + advect(
        anchor, zonal_ext[:, 1:-1], south_ext, first_row - 2
    )
    second = 0.75 * anchor[:, :, 2:-2] + 0.25 * (
        first_section[:, :, 1:-1]
        + advect(first_section, zonal_ext[:, 2:-2], south_ext[:, 1:-1], first_row - 1)
    )
    new_tracers = tracers / 3.0 + 2.0 / 3.0 * (
        second[:, :, 1:-1] + advect(second, zonal_ext[:, 3:-3], south_ext[:, 2:-2], first_row)
    )
    heating = jnp.einsum("kl,klji->jli", heat_rate, new_tracers, precision=HIGHEST)
    eastward_finished = physical_space_field[:, 0:LAYER_TOTAL]
    northward_velocity = physical_space_field[:, LAYER_TOTAL : 2 * LAYER_TOTAL]
    thermal_state = physical_space_field[:, 2 * LAYER_TOTAL : 3 * LAYER_TOTAL]
    vapour_mixing_share = physical_space_field[:, 3 * LAYER_TOTAL : 4 * LAYER_TOTAL]
    flow_speed_norm = jnp.sqrt(
        eastward_finished * eastward_finished + northward_velocity * northward_velocity + 1.0
    )
    warming_finished = jnp.pad(heating, ((0, 0), (0, LAYER_TOTAL - TLEV), (0, 0)))
    rate_of_change_field = jnp.concatenate(
        [
            -DRAG_COEFFICIENT * flow_speed_norm * eastward_finished,
            -DRAG_COEFFICIENT * flow_speed_norm * northward_velocity,
            warming_finished - MOISTURE_SOURCE * thermal_state * vapour_mixing_share,
            MOISTURE_SOURCE * thermal_state * vapour_mixing_share
            - RAINFALL_FACTOR * flow_speed_norm * vapour_mixing_share,
        ],
        axis=1,
    )
    fourier = jnp.einsum(
        "jci,pshi->sjhpc", rate_of_change_field, fourier_table, precision=HIGHEST
    ).reshape(PAIRS, band_rows, 2 * columns)
    by_orders = lax.all_to_all(fourier, "ma", split_axis=0, concat_axis=1, tiled=True)
    weighted = by_orders * quad_weight.reshape(quarter)[None, :, None]
    table_rows = legendre_rows
    row_sums = jnp.einsum("srl,slc->rsc", table_rows, weighted, precision=HIGHEST)
    low_rows, high_rows = row_masks(own_pairs, row_block * lax.axis_size("pb"))
    summed = lax.psum_scatter(
        jnp.where(low_rows.T[:, :, None], row_sums[:, :, :columns], 0.0)
        + jnp.where(high_rows.T[:, :, None], row_sums[:, :, columns:], 0.0),
        "pb",
        scatter_dimension=0,
        tiled=True,
    )
    return (jnp.transpose(summed, (1, 0, 2)), new_tracers)


def solution(mesh):
    in_specs = (
        P("ma", "pb", None),
        P("ma", None, "pb", None),
        P("pb", None),
        P(),
        P(None, None, ("ma", "pb"), None),
        P(),
    )
    out_specs = (P("ma", "pb", None), P(None, None, ("ma", "pb"), None))
    return jax.shard_map(shards, mesh=mesh, in_specs=in_specs, out_specs=out_specs, check_vma=False)
```

profile of v0, /device:TPU:1, one launch (start us, length us, event | category | flops | bytes accessed | tf_op | source)
XLA Modules:
  0.0 511.0 jit_solution(13479577784716797474)
XLA Ops:
  7.2 2.9 copy.83
  10.3 0.6 copy-done.7
  11.0 87.7 %all-gather.2.cloned.1.call-done = f32[16,1056,64]{2,1,0:T(8,128)} async-done(((f32[16,264,64]{2,1,0:T(8,128)}), f32[16,1056,64]{2,1,0:T(8,128)}) %all-gather.2.cloned.1.call-update) | async-done | bytes 4325392 | tf_op jit(solution)/shard_map/all_gather | solution.py:95
  98.6 10.0 %broadcast_select_fusion.1 = (f32[16,1056,64]{2,1,0:T(8,128)}, f32[16,1056,64]{2,1,0:T(8,128)}) fusion(f32[16,1056,64]{2,1,0:T(8,128)} %all-gather.2.cloned.1.call-done, pred[16,1056]{1,0:T(8,128)(4,1)S(1)} %get-tuple-element.42, pred[16,1056]{1,0:T(8,128)(4,1)S(1)} %get-tuple-element.43), kind=kLoop, calls=%fused_computation.30 | loop fusion | flops 2162688 | bytes 13009920 | tf_op jit(solution)/shard_map/jit(_where)/select_n | solution.py:100
  108.7 26.4 %fusion.60 = f32[16,256,128]{1,2,0:T(8,128)S(1)} fusion(f32[16,1056,1,256]{3,2,1,0:T(1,128)} %param.7, f32[16,1056,64]{2,1,0:T(8,128)} %get-tuple-element.19, f32[16,1056,64]{2,1,0:T(8,128)} %get-tuple-element.18), kind=kOutput, calls=%fused_computation.87 | convolution fusion | flops 6645940224 | bytes 28049408 | tf_op jit(solution)/shard_map/srl,src->slc/dot_general | solution.py:106
  135.1 2.0 copy.84
  137.1 7.9 %all-to-all-start = ((f32[16,256,128]{2,0,1:T(8,128)}), f32[16,256,128]{2,0,1:T(8,128)}, u32[]{:S(2)}, u32[]{:S(2)}) async-start(f32[16,256,128]{2,0,1:T(8,128)} %copy.84), calls=%async_computation | async-start | bytes 4194304 | tf_op jit(solution)/shard_map/all_to_all | solution.py:107
  145.2 2.3 copy.89
  147.6 37.4 %cosine_multiply_fusion = (f32[1,512,2,2048]{3,1,0,2:T(8,128)}, f32[1,512,2,2048]{3,1,0,2:T(8,128)}) fusion(s32[512,2]{0,1:T(2,128)S(1)} %pad_add_fusion), kind=kLoop, calls=%fused_computation.24 | loop fusion | flops 35651584 | bytes 16781312 | tf_op jit(solution)/shard_map/mul | solution.py:51
  184.9 3.8 copy.86
  188.7 10.0 %reshape.233 = f32[512,8,2,2,32]{4,3,2,1,0:T(2,128)} reshape(f32[32,16,8,128]{3,2,1,0:T(8,128)} %copy.86) | data formatting | bytes 4194304 | tf_op jit(solution)/shard_map/reshape | solution.py:111
  198.7 5.6 %broadcast_multiply_fusion = f32[512,8,2,2,32]{4,3,2,1,0:T(2,128)S(1)} fusion(f32[512,8,2,2,32]{4,3,2,1,0:T(2,128)} %reshape.233, f32[512,2]{1,0:T(8,128)S(1)} %copy.87), kind=kLoop, calls=%fused_computation.31 | loop fusion | flops 524288 | bytes 4198400 | tf_op jit(solution)/shard_map/mul | solution.py:111
  204.4 73.6 %fusion.33 = f32[8,32,2048]{2,1,0:T(8,128)S(1)} fusion(f32[512,8,2,2,32]{4,3,2,1,0:T(2,128)S(1)} %broadcast_multiply_fusion, f32[1,512,2,2048]{3,1,0,2:T(8,128)} %get-tuple-element.39, f32[1,512,2,2048]{3,1,0,2:T(8,128)} %get-tuple-element.38), kind=kOutput, calls=%fused_computation.53 | convolution fusion | flops 12889096192 | bytes 20971520 | tf_op jit(solution)/shard_map/sjhpc,pshi->jci/dot_general | solution.py:113
  278.4 1.4 pad_maximum_fusion.7
  279.8 3.1 collective-permute-start
  282.9 3.7 collective-permute-start.1
  286.6 0.6 compare_and_fusion.1
  287.7 14.4 %collective-permute-done = f32[14,2,3,2048]{3,0,2,1:T(8,128)S(1)} collective-permute-done((f32[14,2,3,2048]{3,0,2,1:T(8,128)}, f32[14,2,3,2048]{3,0,2,1:T(8,128)S(1)}, u32[]{:S(2)}, u32[]{:S(2)}) %collective-permute-start) | collective-permute-done | bytes 688160 | tf_op jit(solution)/shard_map/ppermute | solution.py:33
  302.2 1.4 collective-permute-done.1
  303.6 1.8 pad_maximum_fusion.9
  305.8 0.9 slice.298
  306.6 0.7 slice.297
  307.3 0.6 slice.299
  309.0 1.6 pad_maximum_fusion
  310.7 0.9 slice.273
  311.5 2.4 fusion.30
  314.6 0.9 fusion.24
  315.5 1.5 fusion.27
  317.0 0.7 slice.286
  318.5 0.9 fusion.41
  319.7 0.7 fusion.32
  320.4 1.6 fusion.40
  322.1 0.6 slice.300
  323.2 0.6 fusion.49
  324.1 0.6 fusion.43
  324.7 0.8 copy-done.1
  325.5 2.2 fusion.48
  327.7 1.6 fusion.80
  329.9 17.4 %fusion.57 = f32[512,8,2,2,32]{0,4,1,2,3:T(8,128)S(1)} fusion(f32[8,8,2048]{2,1,0:T(8,128)S(1)} %get-tuple-element.25, f32[8,8,2048]{2,1,0:T(8,128)S(1)} %get-tuple-element.26, f32[8,8,2048]{2,1,0:T(8,128)S(1)} %get-tuple-element.27, f32[8,8,2048]{2,1,0:T(8,128)S(1)} %get-tuple-element.24, f32[1,512,2,2048]{3,1,0,2:T(8,128)} %get-tuple-element.39, ...), kind=kOutput, calls=%fused_computation.86 | convolution fusion | flops 12890669056 | bytes 20971520 | tf_op jit(solution)/shard_map/jci,pshi->sjhpc/dot_general | solution.py:153
  347.2 1.6 copy.109
  348.8 2.9 copy.110
  351.8 8.7 %all-to-all-start.1 = ((f32[512,8,128]{2,1,0:T(8,128)}), f32[512,8,128]{2,1,0:T(8,128)}, u32[]{:S(2)}, u32[]{:S(2)}) async-start(f32[512,8,128]{2,1,0:T(8,128)} %copy.110), calls=%async_computation.1 | async-start | bytes 4194304 | tf_op jit(solution)/shard_map/all_to_all | solution.py:156
  360.6 28.2 %all-to-all-done.1 = f32[512,8,128]{2,1,0:T(8,128)} async-done(((f32[512,8,128]{2,1,0:T(8,128)}), f32[512,8,128]{2,1,0:T(8,128)}, u32[]{:S(2)}, u32[]{:S(2)}) %all-to-all-start.1) | async-done | bytes 2097184 | tf_op jit(solution)/shard_map/all_to_all | solution.py:156
  388.8 21.9 %fusion.20 = f32[1056,16,128]{2,0,1:T(8,128)S(1)} fusion(f32[16,1056,1,256]{3,2,1,0:T(1,128)} %param.7, f32[16,32,8,128]{3,2,0,1:T(8,128)} %bitcast.26, f32[256]{0:T(256)S(1)} %bitcast.86), kind=kOutput, calls=%fused_computation.28 | convolution fusion | flops 6644301824 | bytes 28050432 | tf_op jit(solution)/shard_map/srl,slc->rsc/dot_general | solution.py:159
  410.7 9.5 %fusion.8 = f32[1056,16,64]{2,0,1:T(8,128)} fusion(f32[1056,16,128]{2,0,1:T(8,128)S(1)} %fusion.20, pred[1056,16]{0,1:T(8,128)(4,1)S(1)} %get-tuple-element.41, pred[1056,16]{0,1:T(8,128)(4,1)S(1)} %get-tuple-element.40), kind=kLoop, calls=%fused_computation.13 | loop fusion | flops 3244032 | bytes 13009920 | tf_op jit(solution)/shard_map/add | solution.py:162
  420.2 2.1 copy.113
  422.3 78.4 %reduce-scatter.2.cloned.1.call-done = f32[264,16,64]{2,0,1:T(8,128)} async-done(((f32[1056,16,64]{2,0,1:T(8,128)}), f32[264,16,64]{2,0,1:T(8,128)}) %reduce-scatter.2.cloned.1.call-update) | async-done | bytes 1081360 | tf_op jit(solution)/shard_map/reduce_scatter | solution.py:161
  500.6 3.0 copy.112
  (83 shorter events, 5.7 us)
Async XLA Ops:
  7.2 320.5 %copy-start = (f32[12,2]{0,1:T(2,128)S(1)}, f32[12,2]{0,1:T(2,128)}, u32[]{:S(2)}) copy-start(f32[12,2]{0,1:T(2,128)} %param.11) | copy-start | bytes 292
  7.2 3.0 copy-start.9
  7.2 91.5 %all-gather.2.cloned.1.call-start = ((), (), s32[]{:S(2)}) async-start(), calls=%async_computation.3 | async-start | bytes 10813440 | tf_op jit(solution)/shard_map/all_gather | solution.py:95
  10.3 98.4 %copy-start.10 = (s32[16]{0:T(128)}, s32[16]{0:T(128)S(1)}, u32[]{:S(2)}) copy-start(s32[16]{0:T(128)S(1)} %dynamic-slice_subtract_fusion) | copy-start | bytes 196
  10.3 0.6 copy-start.7
  137.1 47.8 %all-to-all-start = ((f32[16,256,128]{2,0,1:T(8,128)}), f32[16,256,128]{2,0,1:T(8,128)}, u32[]{:S(2)}, u32[]{:S(2)}) async-start(f32[16,256,128]{2,0,1:T(8,128)} %copy.84), calls=%async_computation | async-start | bytes 4194304 | tf_op jit(solution)/shard_map/all_to_all | solution.py:107
  278.0 1.8 copy-start.2
  279.8 22.4 %collective-permute-start = (f32[14,2,3,2048]{3,0,2,1:T(8,128)}, f32[14,2,3,2048]{3,0,2,1:T(8,128)S(1)}, u32[]{:S(2)}, u32[]{:S(2)}) collective-permute-start(f32[14,2,3,2048]{3,0,2,1:T(8,128)} %get-tuple-element.22), channel_id=1, source_target_pairs={{0,1},{1,2},{2,3},{3,4},{4,5},{5,6},{6,7},{7,8},{8,9},{9,10},{10,1... | collective-permute-start | bytes 2064392 | tf_op jit(solution)/shard_map/ppermute | solution.py:33
  282.9 20.7 %collective-permute-start.1 = (f32[14,2,3,2048]{3,0,2,1:T(8,128)}, f32[14,2,3,2048]{3,0,2,1:T(8,128)}, u32[]{:S(2)}, u32[]{:S(2)}) collective-permute-start(f32[14,2,3,2048]{3,0,2,1:T(8,128)} %get-tuple-element.23), channel_id=1, source_target_pairs={{1,0},{2,1},{3,2},{4,3},{5,4},{6,5},{7,6},{8,7},{9,8},{10,9},{11,1... | collective-permute-start | bytes 2064392 | tf_op jit(solution)/shard_map/ppermute | solution.py:34
  318.5 1.2 copy-start.14
  322.0 0.9 copy-start.4
  322.0 1.0 copy-start.6
  322.1 1.0 copy-start.5
  323.2 0.9 copy-start.13
  324.1 1.4 copy-start.1
  324.7 5.1 %slice-start = ((s8[8388608]{0:T(1024)(128)(4,1)}), s8[4194304]{0:T(1024)(128)(4,1)S(1)}, s32[]{:S(2)}) async-start(s8[8388608]{0:T(1024)(128)(4,1)} %bitcast.77), calls=%async_computation.5 | async-start | bytes 8388608
  325.5 4.3 slice-start.1
  327.7 1.8 copy-start.3
  351.7 8.7 %copy-start.8 = (pred[1056]{0:T(1024)(128)(4,1)S(1)}, pred[1056]{0:T(1024)(128)(4,1)}, u32[]{:S(2)}) copy-start(pred[1056]{0:T(1024)(128)(4,1)} %copy-done.7) | copy-start | bytes 3172
  351.7 8.8 %copy-start.11 = (s32[16]{0:T(128)S(1)}, s32[16]{0:T(128)}, u32[]{:S(2)}) copy-start(s32[16]{0:T(128)} %copy-done.10) | copy-start | bytes 196
  351.8 37.1 %copy-start.12 = (f32[1,256]{1,0:T(1,128)S(1)}, f32[1,256]{1,0:T(1,128)}, u32[]{:S(2)}) copy-start(f32[1,256]{1,0:T(1,128)} %param.8) | copy-start | bytes 3076
  351.8 37.1 %all-to-all-start.1 = ((f32[512,8,128]{2,1,0:T(8,128)}), f32[512,8,128]{2,1,0:T(8,128)}, u32[]{:S(2)}, u32[]{:S(2)}) async-start(f32[512,8,128]{2,1,0:T(8,128)} %copy.110), calls=%async_computation.1 | async-start | bytes 4194304 | tf_op jit(solution)/shard_map/all_to_all | solution.py:156
  360.4 140.2 %reduce-scatter.2.cloned.1.call-start = ((), (), s32[]{:S(2)}) async-start(), calls=%async_computation.4 | async-start | bytes 10813440 | tf_op jit(solution)/shard_map/reduce_scatter | solution.py:161
Sparse Core Ops, SparseCore 0:
  10.3 88.2 all-gather.1
  420.3 80.2 reduce-scatter.1
where the time goes:
time: 520 us; the launch traced here: 511 us
  waiting for transfers between devices  210 us (40%)
  matrix products  141 us (27%)
  other arithmetic  81.8 us (16%)
  local copies, waits for them, and re-layouts  39.5 us (8%)
  starting transfers between devices  23.4 us (4%)
  between operations  15.1 us (3%)
    all_gather x1, waiting for transfers between devices, shards(): row_piece = lax.all_gather(coefs, 'pb', axis=1, tiled=True)  87.7 us
    reduce_scatter x1, waiting for transfers between devices, shards(): lax.psum_scatter(jnp.where(low_rows.T[:, :, None], row_sums[:, :, :column...  78.4 us
    dot_general x1, matrix products, shards(): jnp.einsum('sjhpc,pshi->jci', spectral, fourier_table, precision=HIGHEST)  73.6 us
    mul x1, other arithmetic, order_tables(): jnp.cos(angles) * factor  37.4 us
    all_to_all x1, waiting for transfers between devices, shards(): lax.all_to_all(fourier, 'ma', split_axis=0, concat_axis=1, tiled=True)  28.2 us
    dot_general x1, matrix products, shards(): jnp.einsum('srl,src->slc', table_rows, masked, precision=HIGHEST)  26.4 us
    dot_general x1, matrix products, shards(): jnp.einsum('srl,slc->rsc', table_rows, weighted, precision=HIGHEST)  21.9 us
    dot_general x1, matrix products, shards(): jnp.einsum('jci,pshi->sjhpc', rate_of_change_field, fourier_table, precis...  17.4 us
  transfers between devices with their start and end apart: 6, of which 5 were waited for; matrix products, arithmetic and copies ran while one was open for 8% of the time, Pallas kernels for 0%

commit v1 on v0

v1 whole, which is shorter than its diff:
```python
import math

import jax
import jax.numpy as jnp
from jax import lax
from jax.experimental import pallas as pl
from jax.experimental.pallas import tpu as pltpu
from jax.sharding import PartitionSpec as P

M = 1024
NLAT = 1024
NLON = 2048
HALF = NLON // 2
NTR = 12
TLEV = 2
SLOTS = 16
ROWS = 264
ALL_ROWS = 1056
QLAT = 256

COURANT = 0.15
DRAG_COEFFICIENT = 0.2
MOISTURE_SOURCE = 0.3
RAINFALL_FACTOR = 0.2

BF16 = jnp.bfloat16
F32 = jnp.float32
VMEM_LIMIT = 56 * 1024 * 1024


def params(**kw):
    return pltpu.CompilerParams(vmem_limit_bytes=VMEM_LIMIT, **kw)


def cost(us):
    return pl.CostEstimate(flops=int(us * 2.5e8), bytes_accessed=1 << 20, transcendentals=0)


def split(x):
    hi = x.astype(BF16)
    return hi, (x - hi.astype(F32)).astype(BF16)


def mm(a, b):
    return lax.dot_general(a, b, (((1,), (0,)), ((), ())), preferred_element_type=F32)


def mm_t(a, b):
    return lax.dot_general(a, b, (((1,), (1,)), ((), ())), preferred_element_type=F32)


def pack_kernel(c_ref, a_ref, b_ref, scr):
    for ch, out in ((0, a_ref), (1, b_ref)):
        for g in range(4):
            for s in range(4):
                for p in range(2):
                    r0 = s * 32 + p * 16
                    c0 = p * 32 + ch * 16
                    scr[r0 : r0 + 16, 0:ROWS] = c_ref[4 * g + s, c0 : c0 + 16, :]
            out[g] = scr[...].T[0:ROWS]


def pack(coefs_t):
    shape = jax.ShapeDtypeStruct((4, ROWS, 128), F32)
    return pl.pallas_call(
        pack_kernel,
        out_shape=(shape, shape),
        scratch_shapes=[pltpu.VMEM((128, 384), F32)],
        compiler_params=params(),
        cost_estimate=cost(3),
        name="pack",
    )(coefs_t)


def legendre_kernel(
    pairs, place, own, right, left, far_a, far_b, hi_hbm, lo_hbm,
    out, rows, cols, leg_hi, leg_lo, sem,
):
    step = pl.program_id(0)
    d = place[0]

    def put(k, value):
        start = pl.multiple_of(((d + k) % 4) * ROWS, 8)
        rows[pl.ds(start, ROWS), :] = value

    put(0, own[0])
    put(3, right[0])
    put(1, left[0])
    put(2, jnp.where(step < 2, far_a[0], far_b[0]))
    cols[...] = rows[...].T
    fetch(step, hi_hbm, lo_hbm, leg_hi, leg_lo, sem)
    sums = []
    for q in range(4):
        n = 4 * step + q
        lo_order = pairs[n]
        odd = lo_order % 2
        x = cols[32 * q : 32 * q + 32, 0:M]
        r = lax.broadcasted_iota(jnp.int32, (1, M), 1)
        low = (r < M - lo_order).astype(jnp.int32)
        weight = jnp.where((low == 1) & (lo_order == 0), 1.0, 2.0)
        in_even = low != odd
        x = x * weight
        lhs = jnp.concatenate([jnp.where(in_even, x, 0.0), jnp.where(in_even, 0.0, x)], axis=0)
        hi, lo = split(lhs)
        both = jnp.concatenate([hi, lo], axis=0)
        last = 2.0 * cols[32 * q : 32 * q + 32, M : M + 128][:, 0:1]
        row = leg_hi[n, M : M + 16, :].astype(F32)[0:1] + leg_lo[n, M : M + 16, :].astype(F32)[0:1]
        outer = last * row
        first = mm(both, leg_hi[n, 0:M, :])
        acc = first[0:64] + first[64:128] + mm(hi, leg_lo[n, 0:M, :])
        sums.append(
            acc
            + jnp.concatenate(
                [jnp.where(odd == 1, outer, 0.0), jnp.where(odd == 1, 0.0, outer)], axis=0
            )
        )
    for p in range(2):
        out[:, p] = jnp.concatenate(sums[2 * p : 2 * p + 2], axis=0).T.reshape(32, 8, 128)


def prepare_kernel(leg, hi_out, lo_out, raw, hi_buf, lo_buf, sem):
    step = pl.program_id(0)

    def load(n):
        return pltpu.make_async_copy(leg.at[n], raw.at[n], sem.at[0, n])

    def store(n):
        return (
            pltpu.make_async_copy(hi_buf.at[n], hi_out.at[n], sem.at[1, n]),
            pltpu.make_async_copy(lo_buf.at[n], lo_out.at[n], sem.at[2, n]),
        )

    @pl.when(step == 0)
    def _():
        for n in range(SLOTS):
            load(n).start()

    load(step).wait()
    for t in range(2):
        hi, lo = split(raw[step, pl.ds(t, ALL_ROWS, stride=2), :])
        hi_buf[step, :, 128 * t : 128 * t + 128] = hi
        lo_buf[step, :, 128 * t : 128 * t + 128] = lo
    for copy in store(step):
        copy.start()

    @pl.when(step == SLOTS - 1)
    def _():
        for n in range(SLOTS):
            for copy in store(n):
                copy.wait()


ANY = pl.BlockSpec(memory_space=pl.ANY)


def prepare(leg):
    shape = jax.ShapeDtypeStruct((SLOTS, ALL_ROWS, QLAT), BF16)
    buffer = pltpu.VMEM((SLOTS, ALL_ROWS, QLAT), BF16)
    return pl.pallas_call(
        prepare_kernel,
        grid=(SLOTS,),
        in_specs=[ANY],
        out_specs=(ANY, ANY),
        out_shape=(shape, shape),
        scratch_shapes=[
            pltpu.VMEM((SLOTS, 2 * ALL_ROWS, 128), F32),
            buffer,
            buffer,
            pltpu.SemaphoreType.DMA((3, SLOTS)),
        ],
        compiler_params=params(dimension_semantics=("arbitrary",)),
        cost_estimate=cost(11),
        name="prepare",
    )(leg)


LEG_SCRATCH = [
    pltpu.VMEM((SLOTS, ALL_ROWS, QLAT), BF16),
    pltpu.VMEM((SLOTS, ALL_ROWS, QLAT), BF16),
    pltpu.SemaphoreType.DMA((2, SLOTS)),
]


def fetch(step, hi_hbm, lo_hbm, leg_hi, leg_lo, sem):
    def loads(group):
        return [
            pltpu.make_async_copy(src.at[4 * group + n], dst.at[4 * group + n], sem.at[i, 4 * group + n])
            for n in range(4)
            for i, (src, dst) in enumerate(((hi_hbm, leg_hi), (lo_hbm, leg_lo)))
        ]

    @pl.when(step == 0)
    def _():
        for copy in loads(0):
            copy.start()

    for copy in loads(step):
        copy.wait()

    @pl.when(step == 0)
    def _():
        for copy in loads(1):
            copy.start()

    @pl.when(step < 2)
    def _():
        for copy in loads(step + 2):
            copy.start()


def legendre_sums(pairs, place, own, right, left, far_a, far_b, leg_hi, leg_lo):
    def group(i, *_):
        return (i, 0, 0)

    block = (1, ROWS, 128)
    return pl.pallas_call(
        legendre_kernel,
        grid_spec=pltpu.PrefetchScalarGridSpec(
            num_scalar_prefetch=2,
            grid=(4,),
            in_specs=[
                pl.BlockSpec(block, group),
                pl.BlockSpec(block, group),
                pl.BlockSpec(block, group),
                pl.BlockSpec(block, lambda i, *_: (jnp.minimum(i, 1), 0, 0)),
                pl.BlockSpec(block, lambda i, *_: (jnp.maximum(i - 2, 0), 0, 0)),
                ANY,
                ANY,
            ],
            out_specs=pl.BlockSpec((32, 2, 8, 128), lambda i, *_: (0, i, 0, 0)),
            scratch_shapes=[pltpu.VMEM((1152, 128), F32), pltpu.VMEM((128, 1152), F32)]
            + LEG_SCRATCH,
        ),
        out_shape=jax.ShapeDtypeStruct((32, 8, 8, 128), F32),
        compiler_params=params(dimension_semantics=("arbitrary",)),
        cost_estimate=cost(10),
        name="legendre_sums",
    )(pairs, place, own, right, left, far_a, far_b, leg_hi, leg_lo)


def cos_sin(phase):
    quadrant = (phase + NLON // 8) // (NLON // 4)
    x = (phase - quadrant * (NLON // 4)).astype(F32) * (2.0 * math.pi / NLON)
    y = x * x
    s = x * (1.0 + y * (-1 / 6 + y * (1 / 120 + y * (-1 / 5040 + y * (1 / 362880)))))
    c = 1.0 + y * (-1 / 2 + y * (1 / 24 + y * (-1 / 720 + y * (1 / 40320 + y * (-1 / 3628800)))))
    swap = quadrant % 2 == 1
    cos = jnp.where(swap, s, c)
    sin = jnp.where(swap, c, s)
    cos = jnp.where((quadrant + 1) % 4 >= 2, -cos, cos)
    return cos, jnp.where(quadrant % 4 >= 2, -sin, sin)


def table_kernel(orders, hi_ref, lo_ref):
    m = orders[0]
    product = m * lax.broadcasted_iota(jnp.int32, (1, 128), 1)
    cb, sb = cos_sin(product % NLON)
    factor = 1.0 / math.sqrt(NLON)
    cb, sb = cb * factor, sb * factor
    ca, sa = cos_sin(product % 16 * 128)
    for a in range(8):
        c1, s1 = ca[:, a : a + 1], sa[:, a : a + 1]
        for part, value in ((0, c1 * cb - s1 * sb), (1, -(s1 * cb + c1 * sb))):
            hi, lo = split(value)
            hi_ref[part, :, 128 * a : 128 * a + 128] = hi
            lo_ref[part, :, 128 * a : 128 * a + 128] = lo


def fourier_tables(pair_of_slot):
    first = pair_of_slot
    second = M - 1 - pair_of_slot
    flip = first % 2 == 1
    even = jnp.where(flip, second, first)
    odd = jnp.where(flip, first, second)
    orders = jnp.stack([even, odd], 0).reshape(2, QLAT, 2).transpose(0, 2, 1).reshape(4, QLAT, 1)
    orders = jnp.broadcast_to(orders, (4, QLAT, 128))
    shape = jax.ShapeDtypeStruct((8, QLAT, HALF), BF16)
    out = pl.BlockSpec((2, QLAT, HALF), lambda i: (i, 0, 0))
    return pl.pallas_call(
        table_kernel,
        grid=(4,),
        in_specs=[pl.BlockSpec((1, QLAT, 128), lambda i: (i, 0, 0))],
        out_specs=(out, out),
        out_shape=(shape, shape),
        compiler_params=params(dimension_semantics=("arbitrary",)),
        cost_estimate=cost(5),
        name="tables",
    )(orders)


def to_grid(recv, t_hi, t_lo, z):
    for j in range(8):
        hi, lo = split(recv[:, j, :].T)
        for n in range(8):
            z[n, 16 * j : 16 * j + 16, :] = hi[16 * n : 16 * n + 16]
            z[n, 128 + 16 * j : 128 + 16 * j + 16, :] = lo[16 * n : 16 * n + 16]

    def block(nb):
        cols = slice(256 * nb, 256 * nb + 256)
        res = []
        for par in range(2):
            wide = jnp.zeros((256, 256), F32)
            narrow = jnp.zeros((128, 256), F32)
            for s in range(2):
                for p in range(2):
                    lhs = z[s * 4 + par * 2 + p]
                    n = par * 4 + s * 2 + p
                    wide = wide + mm(lhs, t_hi[n, :, cols])
                    narrow = narrow + mm(lhs[0:128], t_lo[n, :, cols])
            res.append(wide[0:128] + wide[128:256] + narrow)
        return res[0] + res[1], res[0] - res[1]

    return block


def fold(west, east, d, nb):
    cols = slice(256 * nb, 256 * nb + 256)
    for par, value in ((0, west + east), (1, west - east)):
        hi, lo = split(value)
        d[par, 0:128, cols] = hi
        d[par, 128:256, cols] = lo


def from_grid(d, t_hi, t_lo, res, out):
    for par in range(2):
        for s in range(2):
            for p in range(2):
                n = par * 4 + s * 2 + p
                wide = mm_t(d[par], t_hi[n])
                narrow = mm_t(d[par, 0:128], t_lo[n])
                res[s * 4 + par * 2 + p] = wide[0:128] + wide[128:256] + narrow
    for j in range(8):
        rows = jnp.concatenate([res[n, 16 * j : 16 * j + 16, :] for n in range(8)], axis=0)
        out[:, j, :] = rows.T


def wind_kernel(recv, t_hi, t_lo, out, wind, last, first, speed_ref, z, d, res, g):
    block = to_grid(recv, t_hi, t_lo, z)
    for nb in range(4):
        tend = []
        for side, value in enumerate(block(nb)):
            cols = slice(HALF * side + 256 * nb, HALF * side + 256 * nb + 256)
            for t in range(2):
                g[8 * side + 2 * nb + t] = value[:, 128 * t : 128 * t + 128]
            both = value.reshape(8, 16, 256)
            u, v = both[:, 0:8], both[:, 8:16]
            speed = jnp.sqrt(u * u + v * v + 1.0)
            speed_ref[:, cols] = speed.reshape(64, 256)
            drag = -DRAG_COEFFICIENT * speed
            tend.append(jnp.concatenate([drag * u, drag * v], axis=1).reshape(128, 256))
        fold(tend[0], tend[1], d, nb)
    for t in range(16):
        for l in range(TLEV):
            cols = slice(128 * t, 128 * t + 128)
            for n, value in (
                (l, g[t, pl.ds(l, 8, stride=16), :]),
                (TLEV + l, -g[t, pl.ds(8 + l, 8, stride=16), :]),
            ):
                wind[n, :, cols] = value
                last[n, :, cols] = value[4:8]
                first[n, :, cols] = value[0:4]
    from_grid(d, t_hi, t_lo, res, out)


def moist_kernel(recv, t_hi, t_lo, speed_ref, heat_ref, out, z, d, res):
    block = to_grid(recv, t_hi, t_lo, z)
    for nb in range(4):
        tend = []
        for side, value in enumerate(block(nb)):
            cols = slice(HALF * side + 256 * nb, HALF * side + 256 * nb + 256)
            both = value.reshape(8, 16, 256)
            t, q = both[:, 0:8], both[:, 8:16]
            speed = speed_ref[:, cols].reshape(8, 8, 256)
            n = 8 * side + 2 * nb
            heat = jnp.concatenate([heat_ref[n], heat_ref[n + 1]], axis=1).reshape(8, 8, 256)
            source = MOISTURE_SOURCE * t * q
            tend.append(
                jnp.concatenate(
                    [heat - source, source - RAINFALL_FACTOR * speed * q], axis=1
                ).reshape(128, 256)
            )
        fold(tend[0], tend[1], d, nb)
    from_grid(d, t_hi, t_lo, res, out)


FOURIER_SCRATCH = [
    pltpu.VMEM((8, 256, 256), BF16),
    pltpu.VMEM((2, 256, HALF), BF16),
    pltpu.VMEM((8, 128, 256), F32),
]


def wind_stage(recv, t_hi, t_lo):
    return pl.pallas_call(
        wind_kernel,
        out_shape=(
            jax.ShapeDtypeStruct((QLAT, 8, 128), F32),
            jax.ShapeDtypeStruct((2 * TLEV, 8, NLON), F32),
            jax.ShapeDtypeStruct((2 * TLEV, 4, NLON), F32),
            jax.ShapeDtypeStruct((2 * TLEV, 4, NLON), F32),
            jax.ShapeDtypeStruct((64, NLON), F32),
        ),
        scratch_shapes=FOURIER_SCRATCH + [pltpu.VMEM((16, 128, 128), F32)],
        compiler_params=params(),
        cost_estimate=cost(10),
        name="wind_stage",
    )(recv, t_hi, t_lo)


def moist_stage(recv, t_hi, t_lo, speed, heat):
    return pl.pallas_call(
        moist_kernel,
        out_shape=jax.ShapeDtypeStruct((QLAT, 8, 128), F32),
        scratch_shapes=FOURIER_SCRATCH,
        compiler_params=params(),
        cost_estimate=cost(10),
        name="moist_stage",
    )(recv, t_hi, t_lo, speed, heat)


def halo_of(above, below):
    return jnp.concatenate([below, above], axis=0)


def vertical(middle, halo, row):
    up_m, up_h = pltpu.roll(middle, 7, 0), pltpu.roll(halo, 7, 0)
    down_m, down_h = pltpu.roll(middle, 1, 0), pltpu.roll(halo, 1, 0)
    end, start = row == 7, row == 0
    return (
        (jnp.where(end, up_h, up_m), jnp.where(start, down_h, down_m)),
        (jnp.where(end, up_m, up_h), jnp.where(start, down_m, down_h)),
    )


def advect_kernel(
    rate, band, tracer, above, below, wind, wind_above, wind_below, out, heat, coef, total
):
    k = pl.program_id(0)
    row = lax.broadcasted_iota(jnp.int32, (8, 1), 0)

    @pl.when(k == 0)
    def _():
        for l in range(TLEV):
            m = TLEV + l
            u = (wind[l], halo_of(wind_above[l], wind_below[l]))
            w = (wind[m], halo_of(wind_above[m], wind_below[m]))
            moved = vertical(*w, row)
            faces = []
            for n, offset in ((0, row), (1, jnp.where(row < 4, row + 8, row - 8))):
                upper = band[0] * 8 + offset
                inside = (upper >= 0) & (upper <= NLAT - 2)
                faces.append(jnp.where(inside, 0.5 * (w[n] + moved[n][0]), 0.0))
            above_faces = vertical(*faces, row)
            for n in range(2):
                east = 0.5 * (u[n] + pltpu.roll(u[n], NLON - 1, 1))
                west = pltpu.roll(east, 1, 1)
                south, north = faces[n], above_faces[n][1]
                here = (
                    jnp.maximum(east, 0.0) - jnp.minimum(west, 0.0)
                    + jnp.maximum(south, 0.0) - jnp.minimum(north, 0.0)
                )
                stencil = (
                    -COURANT * here,
                    -COURANT * jnp.minimum(east, 0.0),
                    COURANT * jnp.maximum(west, 0.0),
                    -COURANT * jnp.minimum(south, 0.0),
                    COURANT * jnp.maximum(north, 0.0),
                )
                for c, value in enumerate(stencil):
                    coef[l, n, c] = value
        total[...] = jnp.zeros(total.shape, F32)

    def advect(field, l, parts):
        moved = vertical(*field, row)
        done = []
        for n in range(parts):
            q = field[n]
            south, north = moved[n]
            done.append(
                coef[l, n, 0] * q
                + coef[l, n, 1] * pltpu.roll(q, NLON - 1, 1)
                + coef[l, n, 2] * pltpu.roll(q, 1, 1)
                + coef[l, n, 3] * south
                + coef[l, n, 4] * north
            )
        return done

    for l in range(TLEV):
        q = (tracer[0, l], halo_of(above[0, l], below[0, l]))
        first = [a + b for a, b in zip(q, advect(q, l, 2))]
        second = [
            0.75 * a + 0.25 * (b + c) for a, b, c in zip(q, first, advect(first, l, 2))
        ]
        new = q[0] / 3.0 + 2.0 / 3.0 * (second[0] + advect(second, l, 1)[0])
        out[0, l] = new
        total[l] = total[l] + rate[k, l] * new

    @pl.when(k == NTR - 1)
    def _():
        heat[...] = jnp.zeros(heat.shape, F32)
        for t in range(16):
            for l in range(TLEV):
                heat[t, pl.ds(l, 8, stride=8), :] = total[l, :, 128 * t : 128 * t + 128]


def transport(rate, band, tracers, above, below, wind, wind_above, wind_below):
    block = pl.BlockSpec((1, TLEV, 8, NLON), lambda k, *_: (k, 0, 0, 0))
    edge = pl.BlockSpec((1, TLEV, 4, NLON), lambda k, *_: (k, 0, 0, 0))
    whole = pl.BlockSpec((2 * TLEV, 8, NLON), lambda k, *_: (0, 0, 0))
    side = pl.BlockSpec((2 * TLEV, 4, NLON), lambda k, *_: (0, 0, 0))
    return pl.pallas_call(
        advect_kernel,
        grid_spec=pltpu.PrefetchScalarGridSpec(
            num_scalar_prefetch=2,
            grid=(NTR,),
            in_specs=[block, edge, edge, whole, side, side],
            out_specs=(block, pl.BlockSpec((16, 64, 128), lambda k, *_: (0, 0, 0))),
            scratch_shapes=[
                pltpu.VMEM((TLEV, 2, 5, 8, NLON), F32),
                pltpu.VMEM((TLEV, 8, NLON), F32),
            ],
        ),
        out_shape=(
            jax.ShapeDtypeStruct((NTR, TLEV, 8, NLON), F32),
            jax.ShapeDtypeStruct((16, 64, 128), F32),
        ),
        compiler_params=params(dimension_semantics=("arbitrary",)),
        cost_estimate=cost(10),
        name="transport",
    )(rate, band, tracers, above, below, wind, wind_above, wind_below)


PART_ROWS = ALL_ROWS // 2


def tendency_kernel(
    pairs, place, recv, weight, hi_hbm, lo_hbm,
    own, ahead, far_a, far_b, behind, res, leg_hi, leg_lo, sem,
):
    step = pl.program_id(0)
    d = place[0]
    fetch(step, hi_hbm, lo_hbm, leg_hi, leg_lo, sem)
    lane = lax.broadcasted_iota(jnp.int32, (1, 128), 1)
    rhs = []
    bound = jnp.zeros((1, 128), jnp.int32)
    for b in range(4):
        lo_order = pairs[4 * step + b]
        f = recv[:, b // 2].reshape(QLAT, 128) * weight[...]
        even = pltpu.roll(f, (32 * b - 64 * (b % 2)) % 128, 1)
        odd = pltpu.roll(f, (32 * b - 64 * (b % 2) - 32) % 128, 1)
        here = lane // 32 == b
        flip = lo_order % 2 == 1
        low = jnp.where(here, jnp.where(flip, odd, even), 0.0)
        high = jnp.where(here, jnp.where(flip, even, odd), 0.0)
        rhs.append(split(jnp.concatenate([low, high], axis=1)))
        bound = jnp.where(here, M - lo_order, bound)
    rhs = jnp.concatenate([x for hi, lo in rhs for x in (hi, lo, hi)], axis=0)
    for part in range(2):
        rows = slice(PART_ROWS * part, PART_ROWS * (part + 1))
        lhs = []
        for b in range(4):
            hi = leg_hi[4 * step + b, rows, :]
            lhs += [hi, hi, leg_lo[4 * step + b, rows, :]]
        both = mm(jnp.concatenate(lhs, axis=1), rhs)
        r = PART_ROWS * part + lax.broadcasted_iota(jnp.int32, (PART_ROWS, 1), 0)
        value = jnp.where(r < bound, both[:, 0:128], both[:, 128:256])
        res[rows, :] = jnp.where(r <= M, value, 0.0)

    def get(k):
        return res[pl.ds(pl.multiple_of(((d + k) % 4) * ROWS, 8), ROWS), :]

    own[0] = get(0)
    ahead[0] = get(1)
    behind[0] = get(3)

    @pl.when(step < 2)
    def _():
        far_a[0] = get(2)

    @pl.when(step >= 2)
    def _():
        far_b[0] = get(2)


def tendency_sums(pairs, place, recv, weight, leg_hi, leg_lo):
    size = (1, ROWS, 128)
    block = pl.BlockSpec(size, lambda i, *_: (i, 0, 0))
    full = jax.ShapeDtypeStruct((4, ROWS, 128), F32)
    part = jax.ShapeDtypeStruct((2, ROWS, 128), F32)
    return pl.pallas_call(
        tendency_kernel,
        grid_spec=pltpu.PrefetchScalarGridSpec(
            num_scalar_prefetch=2,
            grid=(4,),
            in_specs=[
                pl.BlockSpec((32, 2, 8, 128), lambda i, *_: (0, i, 0, 0)),
                pl.BlockSpec((QLAT, 128), lambda i, *_: (0, 0)),
                ANY,
                ANY,
            ],
            out_specs=(
                block,
                block,
                pl.BlockSpec(size, lambda i, *_: (jnp.minimum(i, 1), 0, 0)),
                pl.BlockSpec(size, lambda i, *_: (jnp.maximum(i - 2, 0), 0, 0)),
                block,
            ),
            scratch_shapes=[pltpu.VMEM((ALL_ROWS, 128), F32)] + LEG_SCRATCH,
        ),
        out_shape=(full, full, part, part, full),
        compiler_params=params(dimension_semantics=("arbitrary",)),
        cost_estimate=cost(10),
        name="tendency_sums",
    )(pairs, place, recv, weight, leg_hi, leg_lo)


def unpack_kernel(a0, a1, a2, b0, b1, b2, out, scr):
    for ch, refs in ((0, (a0, a1, a2)), (1, (b0, b1, b2))):
        for g in range(4):
            scr[0:ROWS, :] = refs[0][g] + refs[1][g] + refs[2][g]
            value = scr[...].T
            for s in range(4):
                for p in range(2):
                    r0 = s * 32 + p * 16
                    c0 = p * 32 + ch * 16
                    out[4 * g + s, c0 : c0 + 16, :] = value[r0 : r0 + 16, 0:ROWS]


def unpack(pieces):
    return pl.pallas_call(
        unpack_kernel,
        out_shape=jax.ShapeDtypeStruct((SLOTS, 64, ROWS), F32),
        scratch_shapes=[pltpu.VMEM((384, 128), F32)],
        compiler_params=params(),
        cost_estimate=cost(4),
        name="unpack",
    )(*pieces)


def shift(x, axis, by):
    n = lax.axis_size(axis)
    return lax.ppermute(x, axis, [(i, (i + by) % n) for i in range(n)])


def neighbours(last, first):
    axes = ("ma", "pb")
    n = lax.axis_size("ma") * lax.axis_size("pb")
    down = [(i, i + 1) for i in range(n - 1)]
    return (
        lax.ppermute(last, axes, down),
        lax.ppermute(first, axes, [(b, a) for a, b in down]),
    )


def gather_rows(x):
    right = shift(x, "pb", 1)
    left = shift(x, "pb", -1)
    return right, left, shift(right[0:2], "pb", 1), shift(left[2:4], "pb", -1)


def scatter_rows(own, ahead, far_a, far_b, behind):
    via_a = shift(far_a, "pb", 1)
    via_b = shift(far_b, "pb", -1)
    ahead = jnp.concatenate([ahead[0:2] + via_a, ahead[2:4]], axis=0)
    behind = jnp.concatenate([behind[0:2], behind[2:4] + via_b], axis=0)
    return own, shift(ahead, "pb", 1), shift(behind, "pb", -1)


def exchange(x):
    return lax.all_to_all(x, "ma", 0, 0, tiled=True)


def shards(coefs, legendre, quad_weight, pair_of_slot, tracers, heat_rate):
    ma = lax.axis_index("ma")
    pb = lax.axis_index("pb")
    pairs = lax.dynamic_slice_in_dim(pair_of_slot, ma * SLOTS, SLOTS, 0)
    place = pb.reshape(1).astype(jnp.int32)
    band = (ma * lax.axis_size("pb") + pb).reshape(1).astype(jnp.int32)
    leg = legendre.reshape(SLOTS, 2 * ALL_ROWS, 128)
    weight = jnp.broadcast_to(quad_weight.reshape(QLAT, 1), (QLAT, 128))

    rows_a, rows_b = pack(jnp.transpose(coefs, (0, 2, 1)))
    got_a = gather_rows(rows_a)
    rows_b, near_a = lax.optimization_barrier((rows_b, got_a[0:2]))
    got_a = (*near_a, *got_a[2:])
    got_b = gather_rows(rows_b)
    t_hi, t_lo = fourier_tables(pair_of_slot)
    leg_hi, leg_lo = prepare(leg)
    sums_a = legendre_sums(pairs, place, rows_a, *got_a, leg_hi, leg_lo)
    sent_a = exchange(sums_a)
    above, below = neighbours(tracers[:, :, 4:8, :], tracers[:, :, 0:4, :])
    sums_b = legendre_sums(pairs, place, rows_b, *got_b, leg_hi, leg_lo)
    sent_b = exchange(sums_b)

    back_a, wind, last, first, speed = wind_stage(sent_a.reshape(QLAT, 8, 128), t_hi, t_lo)
    wind_above, wind_below = neighbours(last, first)
    back_a = exchange(back_a.reshape(32, 8, 8, 128))
    new_tracers, heat = transport(
        heat_rate, band, tracers, above, below, wind, wind_above, wind_below
    )
    back_b = moist_stage(sent_b.reshape(QLAT, 8, 128), t_hi, t_lo, speed, heat)
    back_b = exchange(back_b.reshape(32, 8, 8, 128))
    sums_a = tendency_sums(pairs, place, back_a, weight, leg_hi, leg_lo)
    sums_a = scatter_rows(*sums_a)
    sums_b = tendency_sums(pairs, place, back_b, weight, leg_hi, leg_lo)
    sums_b = scatter_rows(*sums_b)
    summed = unpack((*sums_a, *sums_b))
    return (jnp.transpose(summed, (0, 2, 1)), new_tracers)


def solution(mesh):
    in_specs = (
        P("ma", "pb", None),
        P("ma", None, "pb", None),
        P("pb", None),
        P(),
        P(None, None, ("ma", "pb"), None),
        P(),
    )
    out_specs = (P("ma", "pb", None), P(None, None, ("ma", "pb"), None))
    return jax.shard_map(shards, mesh=mesh, in_specs=in_specs, out_specs=out_specs, check_vma=False)
```

time: 520 us -> 257 us (0.49); the launches traced: 511 us -> 254 us
  waiting for transfers between devices: 210 us -> 53.8 us
  matrix products: 141 us -> 0 us
  Pallas kernels: 0 us -> 111 us
  other arithmetic: 81.8 us -> 2.42 us
  starting transfers between devices: 23.4 us -> 73.4 us
  local copies, waits for them, and re-layouts: 39.5 us -> 12.1 us
  between operations: 15.1 us -> 1.11 us
    dot_general x5 -> x0, matrix products: 141 us -> none  [the longest x1 73.6 us: shards(): jnp.einsum('sjhpc,pshi->jci', spectral, fourier_table, precision=HIGHEST)]
    pallas_call x0 -> x11, Pallas kernels: none -> 111 us  [the longest x2 26.8 us: tendency_sums(): pl.pallas_call(tendency_kernel, grid_spec=pltpu.PrefetchScalarGridSpec(nu...]
    all_gather x1 -> x0, waiting for transfers between devices: 87.7 us -> none  [shards(): row_piece = lax.all_gather(coefs, 'pb', axis=1, tiled=True)]
    reduce_scatter x1 -> x0, waiting for transfers between devices: 78.4 us -> none  [shards(): lax.psum_scatter(jnp.where(low_rows.T[:, :, None], row_sums[:, :, :column...]
    mul x3 -> x0, other arithmetic: 43.3 us -> none  [the longest x1 37.4 us: order_tables(): jnp.cos(angles) * factor]
    ppermute x2 -> x20, waiting for transfers between devices: 15.8 us -> 53.7 us  [the longest x16 52 us: shift(): return lax.ppermute(x, axis, [(i, (i + by) % n) for i in range(n)])]
    ppermute x2 -> x20, starting transfers between devices: 6.76 us -> 37.6 us  [the longest x16 23.7 us: shift(): return lax.ppermute(x, axis, [(i, (i + by) % n) for i in range(n)])]
    all_to_all x2 -> x4, waiting for transfers between devices: 28.2 us -> 0.01 us  [exchange(): return lax.all_to_all(x, 'ma', 0, 0, tiled=True)]
  transfers between devices with their start and end apart: 6 -> 24, of which waited for: 5 -> 8; matrix products, arithmetic and copies ran while one was open for 8% -> 4% of each run, Pallas kernels for 0% -> 41%
where the time goes in v1:
time: 257 us; the launch traced here: 254 us
  Pallas kernels  111 us (43%)
  starting transfers between devices  73.4 us (29%)
  waiting for transfers between devices  53.8 us (21%)
  local copies, waits for them, and re-layouts  12.1 us (5%)
    ppermute x16, waiting for transfers between devices, shift(): return lax.ppermute(x, axis, [(i, (i + by) % n) for i in range(n)])  52 us
    all_to_all x4, starting transfers between devices, exchange(): return lax.all_to_all(x, 'ma', 0, 0, tiled=True)  35.8 us
    pallas_call x2, Pallas kernels, tendency_sums(): pl.pallas_call(tendency_kernel, grid_spec=pltpu.PrefetchScalarGridSpec(nu...  26.8 us
    ppermute x16, starting transfers between devices, shift(): return lax.ppermute(x, axis, [(i, (i + by) % n) for i in range(n)])  23.7 us
    pallas_call x2, Pallas kernels, legendre_sums(): pl.pallas_call(legendre_kernel, grid_spec=pltpu.PrefetchScalarGridSpec(nu...  23.1 us
    pallas_call x1, Pallas kernels, prepare(): pl.pallas_call(prepare_kernel, grid=(SLOTS,), in_specs=[ANY], out_specs=(...  12.6 us
    pallas_call x1, Pallas kernels, transport(): pl.pallas_call(advect_kernel, grid_spec=pltpu.PrefetchScalarGridSpec(num_...  12.6 us
    pallas_call x1, Pallas kernels, wind_stage(): pl.pallas_call(wind_kernel, out_shape=(jax.ShapeDtypeStruct((QLAT, 8, 128...  10.6 us
  transfers between devices with their start and end apart: 24, of which 8 were waited for; matrix products, arithmetic and copies ran while one was open for 4% of the time, Pallas kernels for 41%

profile of v1, /device:TPU:1, one launch (start us, length us, event | category | flops | bytes accessed | tf_op | source)
XLA Modules:
  0.0 254.3 jit_solution(14708793893732780271)
XLA Ops:
  0.6 2.7 %pack.1 = (f32[4,264,128]{2,1,0:T(8,128)}, f32[4,264,128]{2,1,0:T(8,128)}) custom-call(f32[16,64,264]{2,1,0:T(8,128)} %bitcast.19), custom_call_target="tpu_custom_call" | custom-call | flops 750000000 | bytes 1048576 | tf_op jit(solution)/shard_map/pack/pallas_call | solution.py:65
  3.3 2.0 collective-permute-start
  5.4 1.3 collective-permute-start.1
  6.6 11.8 %collective-permute-done.right = f32[4,264,128]{2,1,0:T(8,128)S(1)} collective-permute-done((f32[4,264,128]{2,1,0:T(8,128)}, f32[4,264,128]{2,1,0:T(8,128)S(1)}, u32[]{:S(2)}, u32[]{:S(2)}) %collective-permute-start) | collective-permute-done | bytes 540704 | tf_op jit(solution)/shard_map/ppermute | solution.py:642
  18.9 2.5 collective-permute-start.3
  21.3 1.3 dynamic_slice.3.pairs
  22.6 12.6 %prepare.1 = (bf16[16,1056,256]{2,1,0:T(8,128)(2,1)}, bf16[16,1056,256]{2,1,0:T(8,128)(2,1)}) custom-call(f32[16,2112,128]{2,1,0:T(8,128)} %bitcast.12), custom_call_target="tpu_custom_call" | custom-call | flops 2750000128 | bytes 1048576 | tf_op jit(solution)/shard_map/prepare/pallas_call | solution.py:159
  35.4 2.7 %collective-permute-start.9 = (f32[4,264,128]{2,1,0:T(8,128)S(1)}, f32[4,264,128]{2,1,0:T(8,128)S(1)}, u32[]{:S(2)}, u32[]{:S(2)}) collective-permute-start(f32[4,264,128]{2,1,0:T(8,128)S(1)} %copy-done.8), channel_id=1, source_target_pairs={{0,3},{1,0},{2,1},{3,2},{4,7},{5,4},{6,5},{7,6},{8,11},{9,8},{10,9... | collective-permute-start | bytes 1622024 | tf_op jit(solution)/shard_map/ppermute | solution.py:642
  38.1 0.7 copy-done.15
  38.8 11.5 %legendre_sums.2 = f32[32,8,8,128]{3,2,1,0:T(8,128)} custom-call(s32[16]{0:T(128)} %dynamic_slice.3.pairs, s32[1]{0:T(128)} %bitcast.place, f32[4,264,128]{2,1,0:T(8,128)} %get-tuple-element.28.own, f32[4,264,128]{2,1,0:T(8,128)} %copy-done.4, f32[4,264,128]{2,1,0:T(8,128)} %copy-done.5, f32[2,264,128]{2,1,0:T(8,128)} %copy-done.15, ...), custom_call_target="tpu_custom_call" | custom-call | flops 2500000000 | bytes 1048576 | tf_op jit(solution)/shard_map/legendre_sums/pallas_call | solution.py:216
  50.4 11.0 %all-to-all-start = ((f32[32,8,8,128]{3,2,1,0:T(8,128)}), f32[32,8,8,128]{3,2,1,0:T(8,128)S(1)}, u32[]{:S(2)}, u32[]{:S(2)}) async-start(f32[32,8,8,128]{3,2,1,0:T(8,128)} %legendre_sums.2), calls=%async_computation | async-start | bytes 2097152 | tf_op jit(solution)/shard_map/all_to_all | solution.py:670
  61.6 2.7 %collective-permute-start.11 = (f32[2,264,128]{2,1,0:T(8,128)S(1)}, f32[2,264,128]{2,1,0:T(8,128)S(1)}, u32[]{:S(2)}, u32[]{:S(2)}) collective-permute-start(f32[2,264,128]{2,1,0:T(8,128)S(1)} %slice.59), channel_id=1, source_target_pairs={{0,3},{1,0},{2,1},{3,2},{4,7},{5,4},{6,5},{7,6},{8,11},{9,8},{10,9... | collective-permute-start | bytes 811016 | tf_op jit(solution)/shard_map/ppermute | solution.py:642
  64.3 6.2 %collective-permute-done.10.far_a = f32[2,264,128]{2,1,0:T(8,128)S(1)} collective-permute-done((f32[2,264,128]{2,1,0:T(8,128)S(1)}, f32[2,264,128]{2,1,0:T(8,128)S(1)}, u32[]{:S(2)}, u32[]{:S(2)}) %collective-permute-start.10) | collective-permute-done | bytes 270368 | tf_op jit(solution)/shard_map/ppermute | solution.py:642
  70.6 0.7 copy-done.17
  71.3 0.7 copy-done.18
  72.0 11.5 %legendre_sums.3 = f32[32,8,8,128]{3,2,1,0:T(8,128)} custom-call(s32[16]{0:T(128)} %dynamic_slice.3.pairs, s32[1]{0:T(128)} %bitcast.place, f32[4,264,128]{2,1,0:T(8,128)} %get-tuple-element.42.own, f32[4,264,128]{2,1,0:T(8,128)} %copy-done.6, f32[4,264,128]{2,1,0:T(8,128)} %copy-done.7, f32[2,264,128]{2,1,0:T(8,128)} %copy-done.17, ...), custom_call_target="tpu_custom_call" | custom-call | flops 2500000000 | bytes 1048576 | tf_op jit(solution)/shard_map/legendre_sums/pallas_call | solution.py:216
  83.6 8.1 %all-to-all-start.2 = ((f32[32,8,8,128]{3,2,1,0:T(8,128)}), f32[32,8,8,128]{3,2,1,0:T(8,128)S(1)}, u32[]{:S(2)}, u32[]{:S(2)}) async-start(f32[32,8,8,128]{3,2,1,0:T(8,128)} %legendre_sums.3), calls=%async_computation.2 | async-start | bytes 2097152 | tf_op jit(solution)/shard_map/all_to_all | solution.py:670
  91.7 3.2 %fusion.2 = (f32[12,2,4,2048]{3,2,1,0:T(4,128)S(1)}, f32[12,2,4,2048]{3,2,1,0:T(4,128)}) fusion(f32[12,2,8,2048]{3,2,1,0:T(8,128)} %tracer.1), kind=kLoop, calls=%fused_computation.16 | loop fusion | bytes 3145728 | tf_op jit(solution)/shard_map/slice | solution.py:691
  94.9 1.9 collective-permute-start.12
  96.8 5.0 %collective-permute-start.13 = (f32[12,2,4,2048]{3,2,1,0:T(4,128)S(1)}, f32[12,2,4,2048]{3,2,1,0:T(4,128)}, u32[]{:S(2)}, u32[]{:S(2)}) collective-permute-start(f32[12,2,4,2048]{3,2,1,0:T(4,128)S(1)} %get-tuple-element.54), channel_id=1, source_target_pairs={{1,0},{2,1},{3,2},{4,3},{5,4},{6,5},{7,6},{8,7},{9,8},{10,9},{11,1... | collective-permute-start | bytes 2359304 | tf_op jit(solution)/shard_map/ppermute | solution.py:651
  102.4 1.0 broadcast_in_dim.15.orders
  103.4 9.1 %tables.1 = (bf16[8,256,1024]{2,1,0:T(8,128)(2,1)}, bf16[8,256,1024]{2,1,0:T(8,128)(2,1)}) custom-call(s32[4,256,128]{2,1,0:T(8,128)} %broadcast_in_dim.15.orders), custom_call_target="tpu_custom_call" | custom-call | flops 1250000000 | bytes 1048576 | tf_op jit(solution)/shard_map/tables/pallas_call | solution.py:279
  112.5 10.6 %wind_stage.1 = (f32[256,8,128]{2,1,0:T(8,128)}, f32[4,8,2048]{2,1,0:T(8,128)}, f32[4,4,2048]{2,1,0:T(4,128)}, f32[4,4,2048]{2,1,0:T(4,128)}, f32[64,2048]{1,0:T(8,128)}) custom-call(f32[256,8,128]{2,1,0:T(8,128)} %bitcast.13, bf16[8,256,1024]{2,1,0:T(8,128)(2,1)} %get-tuple-element.34.t_hi, bf16[8,256,1024]{2,1,0:T(8,128)(2,1)} %get-tuple-element.35.t_lo), custom_call_target="tpu_custom_call" | custom-call | flops 2500000000 | bytes 1048576 | tf_op jit(solution)/shard_map/wind_stage/pallas_call | solution.py:394
  123.1 8.3 %all-to-all-start.1 = ((f32[32,8,8,128]{3,2,1,0:T(8,128)}), f32[32,8,8,128]{3,2,1,0:T(8,128)S(1)}, u32[]{:S(2)}, u32[]{:S(2)}) async-start(f32[32,8,8,128]{3,2,1,0:T(8,128)} %bitcast.17), calls=%async_computation.1 | async-start | bytes 2097152 | tf_op jit(solution)/shard_map/all_to_all | solution.py:670
  131.4 1.9 collective-permute-start.14
  133.3 5.1 %collective-permute-start.15 = (f32[4,4,2048]{2,1,0:T(4,128)}, f32[4,4,2048]{2,1,0:T(4,128)S(1)}, u32[]{:S(2)}, u32[]{:S(2)}) collective-permute-start(f32[4,4,2048]{2,1,0:T(4,128)} %get-tuple-element.46), channel_id=1, source_target_pairs={{1,0},{2,1},{3,2},{4,3},{5,4},{6,5},{7,6},{8,7},{9,8},{10,9},{11,1... | collective-permute-start | bytes 393224 | tf_op jit(solution)/shard_map/ppermute | solution.py:651
  138.4 0.7 copy.14.rate
  139.1 0.9 collective-permute-done.14.wind_above
  140.0 0.8 collective-permute-done.15.wind_below
  141.5 12.6 %transport.1 = (f32[12,2,8,2048]{3,2,1,0:T(8,128)}, f32[16,64,128]{2,1,0:T(8,128)}) custom-call(f32[12,2]{1,0:T(8,128)} %copy.14.rate, s32[1]{0:T(128)} %bitcast.8.band, f32[12,2,8,2048]{3,2,1,0:T(8,128)} %tracer.1, f32[12,2,4,2048]{3,2,1,0:T(4,128)} %collective-permute-done.12.above, f32[12,2,4,2048]{3,2,1,0:T(4,128)} %collective-permute-done.13.below, ...), custom_call_target="tpu_custom_call" | custom-call | flops 2500000000 | bytes 1048576 | tf_op jit(solution)/shard_map/transport/pallas_call | solution.py:511
  154.1 10.4 %moist_stage.1 = f32[256,8,128]{2,1,0:T(8,128)} custom-call(f32[256,8,128]{2,1,0:T(8,128)} %bitcast.14, bf16[8,256,1024]{2,1,0:T(8,128)(2,1)} %get-tuple-element.34.t_hi, bf16[8,256,1024]{2,1,0:T(8,128)(2,1)} %get-tuple-element.35.t_lo, f32[64,2048]{1,0:T(8,128)} %get-tuple-element.43.speed_ref, f32[16,64,128]{2,1,0:T(8,128)} %get-tuple-element.47.heat_ref), custom_call_target="tpu_custom_call" | custom-call | flops 2500000000 | bytes 1048576 | tf_op jit(solution)/shard_map/moist_stage/pallas_call | solution.py:411
  164.5 8.4 %all-to-all-start.3 = ((f32[32,8,8,128]{3,2,1,0:T(8,128)}), f32[32,8,8,128]{3,2,1,0:T(8,128)S(1)}, u32[]{:S(2)}, u32[]{:S(2)}) async-start(f32[32,8,8,128]{3,2,1,0:T(8,128)} %bitcast.15), calls=%async_computation.3 | async-start | bytes 2097152 | tf_op jit(solution)/shard_map/all_to_all | solution.py:670
  172.9 0.8 broadcast_in_dim.17.weight
  173.7 13.4 %tendency_sums.2 = (f32[4,264,128]{2,1,0:T(8,128)}, f32[4,264,128]{2,1,0:T(8,128)}, f32[2,264,128]{2,1,0:T(8,128)}, f32[2,264,128]{2,1,0:T(8,128)}, f32[4,264,128]{2,1,0:T(8,128)}) custom-call(s32[16]{0:T(128)} %dynamic_slice.3.pairs, s32[1]{0:T(128)} %bitcast.place, f32[32,8,8,128]{3,2,1,0:T(8,128)} %copy-done.1, f32[256,128]{1,0:T(8,128)} %broadcast_in_dim.17.weight, ...), custom_call_target="tpu_custom_call" | custom-call | flops 2500000000 | bytes 1048576 | tf_op jit(solution)/shard_map/tendency_sums/pallas_call | solution.py:590
  187.1 5.4 %collective-permute-start.6 = (f32[2,264,128]{2,1,0:T(8,128)}, f32[2,264,128]{2,1,0:T(8,128)S(1)}, u32[]{:S(2)}, u32[]{:S(2)}) collective-permute-start(f32[2,264,128]{2,1,0:T(8,128)} %get-tuple-element.41), channel_id=1, source_target_pairs={{0,3},{1,0},{2,1},{3,2},{4,7},{5,4},{6,5},{7,6},{8,11},{9,8},{10,9... | collective-permute-start | bytes 811016 | tf_op jit(solution)/shard_map/ppermute | solution.py:642
  192.5 5.9 %collective-permute-done.6 = f32[2,264,128]{2,1,0:T(8,128)S(1)} collective-permute-done((f32[2,264,128]{2,1,0:T(8,128)}, f32[2,264,128]{2,1,0:T(8,128)S(1)}, u32[]{:S(2)}, u32[]{:S(2)}) %collective-permute-start.6) | collective-permute-done | bytes 270368 | tf_op jit(solution)/shard_map/ppermute | solution.py:642
  198.4 1.1 fusion.4
  199.5 3.4 %collective-permute-start.7 = (f32[4,264,128]{2,1,0:T(8,128)S(1)}, f32[4,264,128]{2,1,0:T(8,128)S(1)}, u32[]{:S(2)}, u32[]{:S(2)}) collective-permute-start(f32[4,264,128]{2,1,0:T(8,128)S(1)} %pad_maximum_fusion.1), channel_id=1, source_target_pairs={{0,3},{1,0},{2,1},{3,2},{4,7},{5,4},{6,5},{7,6},{8,11},{9,8},{10,9... | collective-permute-start | bytes 1622024 | tf_op jit(solution)/shard_map/ppermute | solution.py:642
  202.9 1.0 copy-done.2
  203.9 13.4 %tendency_sums.3 = (f32[4,264,128]{2,1,0:T(8,128)}, f32[4,264,128]{2,1,0:T(8,128)}, f32[2,264,128]{2,1,0:T(8,128)}, f32[2,264,128]{2,1,0:T(8,128)}, f32[4,264,128]{2,1,0:T(8,128)}) custom-call(s32[16]{0:T(128)} %dynamic_slice.3.pairs, s32[1]{0:T(128)} %bitcast.place, f32[32,8,8,128]{3,2,1,0:T(8,128)} %copy-done.2, f32[256,128]{1,0:T(8,128)} %broadcast_in_dim.17.weight, ...), custom_call_target="tpu_custom_call" | custom-call | flops 2500000000 | bytes 1048576 | tf_op jit(solution)/shard_map/tendency_sums/pallas_call | solution.py:590
  217.5 1.5 collective-permute-start.5
  219.1 5.2 %collective-permute-done.18 = f32[2,264,128]{2,1,0:T(8,128)S(1)} collective-permute-done((f32[2,264,128]{2,1,0:T(8,128)}, f32[2,264,128]{2,1,0:T(8,128)S(1)}, u32[]{:S(2)}, u32[]{:S(2)}) %collective-permute-start.18) | collective-permute-done | bytes 270368 | tf_op jit(solution)/shard_map/ppermute | solution.py:642
  224.2 1.1 fusion.3
  225.3 1.6 collective-permute-start.19
  226.9 10.1 %collective-permute-done.16 = f32[2,264,128]{2,1,0:T(8,128)S(1)} collective-permute-done((f32[2,264,128]{2,1,0:T(8,128)}, f32[2,264,128]{2,1,0:T(8,128)S(1)}, u32[]{:S(2)}, u32[]{:S(2)}) %collective-permute-start.16) | collective-permute-done | bytes 270368 | tf_op jit(solution)/shard_map/ppermute | solution.py:642
  237.2 12.7 %collective-permute-done.17.b1 = f32[4,264,128]{2,1,0:T(8,128)S(1)} collective-permute-done((f32[4,264,128]{2,1,0:T(8,128)S(1)}, f32[4,264,128]{2,1,0:T(8,128)S(1)}, u32[]{:S(2)}, u32[]{:S(2)}) %collective-permute-start.17) | collective-permute-done | bytes 540704 | tf_op jit(solution)/shard_map/ppermute | solution.py:642
  250.0 0.8 copy-done.12
  250.8 3.5 %unpack.1 = f32[16,64,264]{2,1,0:T(8,128)} custom-call(f32[4,264,128]{2,1,0:T(8,128)} %get-tuple-element.37.a0, f32[4,264,128]{2,1,0:T(8,128)} %copy-done.10, f32[4,264,128]{2,1,0:T(8,128)} %copy-done.9, f32[4,264,128]{2,1,0:T(8,128)} %get-tuple-element.48.b0, f32[4,264,128]{2,1,0:T(8,128)} %copy-done.12, f32[4,264,128]{2,1,0:T(8,128)} %copy-done.11), custom_call_target="tpu_custom_call" | custom-call | flops 1000000000 | bytes 1048576 | tf_op jit(solution)/shard_map/unpack/pallas_call | solution.py:630
  (83 shorter events, 2.4 us)
Async XLA Ops:
  3.3 15.1 %collective-permute-start = (f32[4,264,128]{2,1,0:T(8,128)}, f32[4,264,128]{2,1,0:T(8,128)S(1)}, u32[]{:S(2)}, u32[]{:S(2)}) collective-permute-start(f32[4,264,128]{2,1,0:T(8,128)} %get-tuple-element.28.own), channel_id=1, source_target_pairs={{0,1},{1,2},{2,3},{3,0},{4,5},{5,6},{6,7},{7,4},{8,9},{9,10},{10,1... | collective-permute-start | bytes 1622024 | tf_op jit(solution)/shard_map/ppermute | solution.py:642
  5.4 13.5 %collective-permute-start.1 = (f32[4,264,128]{2,1,0:T(8,128)}, f32[4,264,128]{2,1,0:T(8,128)S(1)}, u32[]{:S(2)}, u32[]{:S(2)}) collective-permute-start(f32[4,264,128]{2,1,0:T(8,128)} %get-tuple-element.28.own), channel_id=1, source_target_pairs={{0,3},{1,0},{2,1},{3,2},{4,7},{5,4},{6,5},{7,6},{8,11},{9,8},{10,9... | collective-permute-start | bytes 1622024 | tf_op jit(solution)/shard_map/ppermute | solution.py:642
  18.5 16.8 %copy-start.4 = (f32[4,264,128]{2,1,0:T(8,128)}, f32[4,264,128]{2,1,0:T(8,128)S(1)}, u32[]{:S(2)}) copy-start(f32[4,264,128]{2,1,0:T(8,128)S(1)} %collective-permute-done.right) | copy-start | bytes 1622020
  18.5 19.6 %collective-permute-start.2 = (f32[2,264,128]{2,1,0:T(8,128)S(1)}, f32[2,264,128]{2,1,0:T(8,128)S(1)}, u32[]{:S(2)}, u32[]{:S(2)}) collective-permute-start(f32[2,264,128]{2,1,0:T(8,128)S(1)} %slice.56), channel_id=1, source_target_pairs={{0,1},{1,2},{2,3},{3,0},{4,5},{5,6},{6,7},{7,4},{8,9},{9,10},{10,1... | collective-permute-start | bytes 811016 | tf_op jit(solution)/shard_map/ppermute | solution.py:642
  18.8 16.4 %copy-start.5 = (f32[4,264,128]{2,1,0:T(8,128)}, f32[4,264,128]{2,1,0:T(8,128)S(1)}, u32[]{:S(2)}) copy-start(f32[4,264,128]{2,1,0:T(8,128)S(1)} %collective-permute-done.1.left) | copy-start | bytes 1622020
  18.9 19.2 %collective-permute-start.3 = (f32[2,264,128]{2,1,0:T(8,128)S(1)}, f32[2,264,128]{2,1,0:T(8,128)S(1)}, u32[]{:S(2)}, u32[]{:S(2)}) collective-permute-start(f32[2,264,128]{2,1,0:T(8,128)S(1)} %slice.57), channel_id=1, source_target_pairs={{0,3},{1,0},{2,1},{3,2},{4,7},{5,4},{6,5},{7,6},{8,11},{9,8},{10,9... | collective-permute-start | bytes 811016 | tf_op jit(solution)/shard_map/ppermute | solution.py:642
  22.6 12.7 %copy-start.8 = (f32[4,264,128]{2,1,0:T(8,128)S(1)}, f32[4,264,128]{2,1,0:T(8,128)}, u32[]{:S(2)}) copy-start(f32[4,264,128]{2,1,0:T(8,128)} %get-tuple-element.42.own) | copy-start | bytes 1622020
  35.3 26.2 %collective-permute-start.8 = (f32[4,264,128]{2,1,0:T(8,128)S(1)}, f32[4,264,128]{2,1,0:T(8,128)S(1)}, u32[]{:S(2)}, u32[]{:S(2)}) collective-permute-start(f32[4,264,128]{2,1,0:T(8,128)S(1)} %copy-done.8), channel_id=1, source_target_pairs={{0,1},{1,2},{2,3},{3,0},{4,5},{5,6},{6,7},{7,4},{8,9},{9,10},{10,1... | collective-permute-start | bytes 1622024 | tf_op jit(solution)/shard_map/ppermute | solution.py:642
  35.4 26.2 %collective-permute-start.9 = (f32[4,264,128]{2,1,0:T(8,128)S(1)}, f32[4,264,128]{2,1,0:T(8,128)S(1)}, u32[]{:S(2)}, u32[]{:S(2)}) collective-permute-start(f32[4,264,128]{2,1,0:T(8,128)S(1)} %copy-done.8), channel_id=1, source_target_pairs={{0,3},{1,0},{2,1},{3,2},{4,7},{5,4},{6,5},{7,6},{8,11},{9,8},{10,9... | collective-permute-start | bytes 1622024 | tf_op jit(solution)/shard_map/ppermute | solution.py:642
  38.0 0.7 copy-start.15
  38.0 0.8 copy-start.16
  50.4 33.2 %all-to-all-start = ((f32[32,8,8,128]{3,2,1,0:T(8,128)}), f32[32,8,8,128]{3,2,1,0:T(8,128)S(1)}, u32[]{:S(2)}, u32[]{:S(2)}) async-start(f32[32,8,8,128]{3,2,1,0:T(8,128)} %legendre_sums.2), calls=%async_computation | async-start | bytes 2097152 | tf_op jit(solution)/shard_map/all_to_all | solution.py:670
  61.4 9.1 %copy-start.6 = (f32[4,264,128]{2,1,0:T(8,128)}, f32[4,264,128]{2,1,0:T(8,128)S(1)}, u32[]{:S(2)}) copy-start(f32[4,264,128]{2,1,0:T(8,128)S(1)} %collective-permute-done.8.right) | copy-start | bytes 1622020
  61.5 9.1 %collective-permute-start.10 = (f32[2,264,128]{2,1,0:T(8,128)S(1)}, f32[2,264,128]{2,1,0:T(8,128)S(1)}, u32[]{:S(2)}, u32[]{:S(2)}) collective-permute-start(f32[2,264,128]{2,1,0:T(8,128)S(1)} %slice.58), channel_id=1, source_target_pairs={{0,1},{1,2},{2,3},{3,0},{4,5},{5,6},{6,7},{7,4},{8,9},{9,10},{10,1... | collective-permute-start | bytes 811016 | tf_op jit(solution)/shard_map/ppermute | solution.py:642
  61.6 9.0 %copy-start.7 = (f32[4,264,128]{2,1,0:T(8,128)}, f32[4,264,128]{2,1,0:T(8,128)S(1)}, u32[]{:S(2)}) copy-start(f32[4,264,128]{2,1,0:T(8,128)S(1)} %collective-permute-done.9.left) | copy-start | bytes 1622020
  61.6 9.0 %collective-permute-start.11 = (f32[2,264,128]{2,1,0:T(8,128)S(1)}, f32[2,264,128]{2,1,0:T(8,128)S(1)}, u32[]{:S(2)}, u32[]{:S(2)}) collective-permute-start(f32[2,264,128]{2,1,0:T(8,128)S(1)} %slice.59), channel_id=1, source_target_pairs={{0,3},{1,0},{2,1},{3,2},{4,7},{5,4},{6,5},{7,6},{8,11},{9,8},{10,9... | collective-permute-start | bytes 811016 | tf_op jit(solution)/shard_map/ppermute | solution.py:642
  70.6 0.7 copy-start.17
  71.3 0.7 copy-start.18
  83.5 18.3 %copy-start.19 = (s32[512]{0:T(512)S(1)}, s32[512]{0:T(512)}, u32[]{:S(2)}) copy-start(s32[512]{0:T(512)} %param.9) | copy-start | bytes 6148
  83.6 28.9 %copy-start = (f32[32,8,8,128]{3,2,1,0:T(8,128)}, f32[32,8,8,128]{3,2,1,0:T(8,128)S(1)}, u32[]{:S(2)}) copy-start(f32[32,8,8,128]{3,2,1,0:T(8,128)S(1)} %all-to-all-done) | copy-start | bytes 3145732
  83.6 39.5 %all-to-all-start.2 = ((f32[32,8,8,128]{3,2,1,0:T(8,128)}), f32[32,8,8,128]{3,2,1,0:T(8,128)S(1)}, u32[]{:S(2)}, u32[]{:S(2)}) async-start(f32[32,8,8,128]{3,2,1,0:T(8,128)} %legendre_sums.3), calls=%async_computation.2 | async-start | bytes 2097152 | tf_op jit(solution)/shard_map/all_to_all | solution.py:670
  94.9 44.2 %collective-permute-start.12 = (f32[12,2,4,2048]{3,2,1,0:T(4,128)}, f32[12,2,4,2048]{3,2,1,0:T(4,128)}, u32[]{:S(2)}, u32[]{:S(2)}) collective-permute-start(f32[12,2,4,2048]{3,2,1,0:T(4,128)} %get-tuple-element.55), channel_id=1, source_target_pairs={{0,1},{1,2},{2,3},{3,4},{4,5},{5,6},{6,7},{7,8},{8,9},{9,10},{10,1... | collective-permute-start | bytes 2359304 | tf_op jit(solution)/shard_map/ppermute | solution.py:650
  96.8 42.3 %collective-permute-start.13 = (f32[12,2,4,2048]{3,2,1,0:T(4,128)S(1)}, f32[12,2,4,2048]{3,2,1,0:T(4,128)}, u32[]{:S(2)}, u32[]{:S(2)}) collective-permute-start(f32[12,2,4,2048]{3,2,1,0:T(4,128)S(1)} %get-tuple-element.54), channel_id=1, source_target_pairs={{1,0},{2,1},{3,2},{4,3},{5,4},{6,5},{7,6},{8,7},{9,8},{10,9},{11,1... | collective-permute-start | bytes 2359304 | tf_op jit(solution)/shard_map/ppermute | solution.py:651
  112.5 25.9 %copy-start.21 = (f32[12,2]{0,1:T(2,128)S(1)}, f32[12,2]{0,1:T(2,128)}, u32[]{:S(2)}) copy-start(f32[12,2]{0,1:T(2,128)} %param.11) | copy-start | bytes 292
  123.1 31.0 %copy-start.3 = (f32[32,8,8,128]{3,2,1,0:T(8,128)}, f32[32,8,8,128]{3,2,1,0:T(8,128)S(1)}, u32[]{:S(2)}) copy-start(f32[32,8,8,128]{3,2,1,0:T(8,128)S(1)} %all-to-all-done.2) | copy-start | bytes 3145732
  123.1 41.4 %all-to-all-start.1 = ((f32[32,8,8,128]{3,2,1,0:T(8,128)}), f32[32,8,8,128]{3,2,1,0:T(8,128)S(1)}, u32[]{:S(2)}, u32[]{:S(2)}) async-start(f32[32,8,8,128]{3,2,1,0:T(8,128)} %bitcast.17), calls=%async_computation.1 | async-start | bytes 2097152 | tf_op jit(solution)/shard_map/all_to_all | solution.py:670
  131.4 8.6 %collective-permute-start.14 = (f32[4,4,2048]{2,1,0:T(4,128)}, f32[4,4,2048]{2,1,0:T(4,128)S(1)}, u32[]{:S(2)}, u32[]{:S(2)}) collective-permute-start(f32[4,4,2048]{2,1,0:T(4,128)} %get-tuple-element.45), channel_id=1, source_target_pairs={{0,1},{1,2},{2,3},{3,4},{4,5},{5,6},{6,7},{7,8},{8,9},{9,10},{10,1... | collective-permute-start | bytes 393224 | tf_op jit(solution)/shard_map/ppermute | solution.py:650
  133.3 7.5 %collective-permute-start.15 = (f32[4,4,2048]{2,1,0:T(4,128)}, f32[4,4,2048]{2,1,0:T(4,128)S(1)}, u32[]{:S(2)}, u32[]{:S(2)}) collective-permute-start(f32[4,4,2048]{2,1,0:T(4,128)} %get-tuple-element.46), channel_id=1, source_target_pairs={{1,0},{2,1},{3,2},{4,3},{5,4},{6,5},{7,6},{8,7},{9,8},{10,9},{11,1... | collective-permute-start | bytes 393224 | tf_op jit(solution)/shard_map/ppermute | solution.py:651
  140.0 0.8 copy-start.22
  140.9 0.7 copy-start.23
  154.1 18.8 %copy-start.20 = (f32[1,256]{1,0:T(1,128)S(1)}, f32[1,256]{1,0:T(1,128)}, u32[]{:S(2)}) copy-start(f32[1,256]{1,0:T(1,128)} %param.8) | copy-start | bytes 3076
  164.5 9.2 %copy-start.1 = (f32[32,8,8,128]{3,2,1,0:T(8,128)}, f32[32,8,8,128]{3,2,1,0:T(8,128)S(1)}, u32[]{:S(2)}) copy-start(f32[32,8,8,128]{3,2,1,0:T(8,128)S(1)} %all-to-all-done.1.recv) | copy-start | bytes 3145732
  164.5 38.4 %all-to-all-start.3 = ((f32[32,8,8,128]{3,2,1,0:T(8,128)}), f32[32,8,8,128]{3,2,1,0:T(8,128)S(1)}, u32[]{:S(2)}, u32[]{:S(2)}) async-start(f32[32,8,8,128]{3,2,1,0:T(8,128)} %bitcast.15), calls=%async_computation.3 | async-start | bytes 2097152 | tf_op jit(solution)/shard_map/all_to_all | solution.py:670
  187.1 11.3 %collective-permute-start.6 = (f32[2,264,128]{2,1,0:T(8,128)}, f32[2,264,128]{2,1,0:T(8,128)S(1)}, u32[]{:S(2)}, u32[]{:S(2)}) collective-permute-start(f32[2,264,128]{2,1,0:T(8,128)} %get-tuple-element.41), channel_id=1, source_target_pairs={{0,3},{1,0},{2,1},{3,2},{4,7},{5,4},{6,5},{7,6},{8,11},{9,8},{10,9... | collective-permute-start | bytes 811016 | tf_op jit(solution)/shard_map/ppermute | solution.py:642
  192.5 24.9 %collective-permute-start.4 = (f32[2,264,128]{2,1,0:T(8,128)}, f32[2,264,128]{2,1,0:T(8,128)S(1)}, u32[]{:S(2)}, u32[]{:S(2)}) collective-permute-start(f32[2,264,128]{2,1,0:T(8,128)} %get-tuple-element.39), channel_id=1, source_target_pairs={{0,1},{1,2},{2,3},{3,0},{4,5},{5,6},{6,7},{7,4},{8,9},{9,10},{10,1... | collective-permute-start | bytes 811016 | tf_op jit(solution)/shard_map/ppermute | solution.py:642
  199.5 17.8 %copy-start.14 = (f32[4,264,128]{2,1,0:T(8,128)S(1)}, f32[4,264,128]{2,1,0:T(8,128)}, u32[]{:S(2)}) copy-start(f32[4,264,128]{2,1,0:T(8,128)} %get-tuple-element.38) | copy-start | bytes 1622020
  199.5 37.7 %collective-permute-start.7 = (f32[4,264,128]{2,1,0:T(8,128)S(1)}, f32[4,264,128]{2,1,0:T(8,128)S(1)}, u32[]{:S(2)}, u32[]{:S(2)}) collective-permute-start(f32[4,264,128]{2,1,0:T(8,128)S(1)} %pad_maximum_fusion.1), channel_id=1, source_target_pairs={{0,3},{1,0},{2,1},{3,2},{4,7},{5,4},{6,5},{7,6},{8,11},{9,8},{10,9... | collective-permute-start | bytes 1622024 | tf_op jit(solution)/shard_map/ppermute | solution.py:642
  202.9 1.0 copy-start.2
  217.3 19.8 %copy-start.13 = (f32[4,264,128]{2,1,0:T(8,128)S(1)}, f32[4,264,128]{2,1,0:T(8,128)}, u32[]{:S(2)}) copy-start(f32[4,264,128]{2,1,0:T(8,128)} %get-tuple-element.49) | copy-start | bytes 1622020
  217.3 6.9 %collective-permute-start.18 = (f32[2,264,128]{2,1,0:T(8,128)}, f32[2,264,128]{2,1,0:T(8,128)S(1)}, u32[]{:S(2)}, u32[]{:S(2)}) collective-permute-start(f32[2,264,128]{2,1,0:T(8,128)} %get-tuple-element.52), channel_id=1, source_target_pairs={{0,3},{1,0},{2,1},{3,2},{4,7},{5,4},{6,5},{7,6},{8,11},{9,8},{10,9... | collective-permute-start | bytes 811016 | tf_op jit(solution)/shard_map/ppermute | solution.py:642
  217.5 19.7 %collective-permute-start.5 = (f32[4,264,128]{2,1,0:T(8,128)S(1)}, f32[4,264,128]{2,1,0:T(8,128)S(1)}, u32[]{:S(2)}, u32[]{:S(2)}) collective-permute-start(f32[4,264,128]{2,1,0:T(8,128)S(1)} %pad_maximum_fusion), channel_id=1, source_target_pairs={{0,1},{1,2},{2,3},{3,0},{4,5},{5,6},{6,7},{7,4},{8,9},{9,10},{10,1... | collective-permute-start | bytes 1622024 | tf_op jit(solution)/shard_map/ppermute | solution.py:642
  219.0 18.0 %collective-permute-start.16 = (f32[2,264,128]{2,1,0:T(8,128)}, f32[2,264,128]{2,1,0:T(8,128)S(1)}, u32[]{:S(2)}, u32[]{:S(2)}) collective-permute-start(f32[2,264,128]{2,1,0:T(8,128)} %get-tuple-element.50), channel_id=1, source_target_pairs={{0,1},{1,2},{2,3},{3,0},{4,5},{5,6},{6,7},{7,4},{8,9},{9,10},{10,1... | collective-permute-start | bytes 811016 | tf_op jit(solution)/shard_map/ppermute | solution.py:642
  225.3 11.9 %collective-permute-start.19 = (f32[4,264,128]{2,1,0:T(8,128)S(1)}, f32[4,264,128]{2,1,0:T(8,128)S(1)}, u32[]{:S(2)}, u32[]{:S(2)}) collective-permute-start(f32[4,264,128]{2,1,0:T(8,128)S(1)} %pad_maximum_fusion.3), channel_id=1, source_target_pairs={{0,3},{1,0},{2,1},{3,2},{4,7},{5,4},{6,5},{7,6},{8,11},{9,8},{10,9... | collective-permute-start | bytes 1622024 | tf_op jit(solution)/shard_map/ppermute | solution.py:642
  237.1 12.9 %collective-permute-start.17 = (f32[4,264,128]{2,1,0:T(8,128)S(1)}, f32[4,264,128]{2,1,0:T(8,128)S(1)}, u32[]{:S(2)}, u32[]{:S(2)}) collective-permute-start(f32[4,264,128]{2,1,0:T(8,128)S(1)} %pad_maximum_fusion.2), channel_id=1, source_target_pairs={{0,1},{1,2},{2,3},{3,0},{4,5},{5,6},{6,7},{7,4},{8,9},{9,10},{10,1... | collective-permute-start | bytes 1622024 | tf_op jit(solution)/shard_map/ppermute | solution.py:642
  237.2 12.8 %copy-start.9 = (f32[4,264,128]{2,1,0:T(8,128)}, f32[4,264,128]{2,1,0:T(8,128)S(1)}, u32[]{:S(2)}) copy-start(f32[4,264,128]{2,1,0:T(8,128)S(1)} %collective-permute-done.7.a2) | copy-start | bytes 1622020
  237.2 12.8 %copy-start.10 = (f32[4,264,128]{2,1,0:T(8,128)}, f32[4,264,128]{2,1,0:T(8,128)S(1)}, u32[]{:S(2)}) copy-start(f32[4,264,128]{2,1,0:T(8,128)S(1)} %collective-permute-done.5.a1) | copy-start | bytes 1622020
  237.2 12.8 %copy-start.11 = (f32[4,264,128]{2,1,0:T(8,128)}, f32[4,264,128]{2,1,0:T(8,128)S(1)}, u32[]{:S(2)}) copy-start(f32[4,264,128]{2,1,0:T(8,128)S(1)} %collective-permute-done.19.b2) | copy-start | bytes 1622020
  250.0 0.8 copy-start.12

commit v2 on v1

--- a/solution.py
+++ b/solution.py
@@ -25,7 +25,7 @@
 
 BF16 = jnp.bfloat16
 F32 = jnp.float32
-VMEM_LIMIT = 56 * 1024 * 1024
+VMEM_LIMIT = 28 * 1024 * 1024
 
 
 def params(**kw):
@@ -76,23 +76,39 @@
     pairs, place, own, right, left, far_a, far_b, hi_hbm, lo_hbm,
     out, rows, cols, leg_hi, leg_lo, sem,
 ):
-    step = pl.program_id(0)
+    tables = (hi_hbm, lo_hbm, leg_hi, leg_lo, sem)
+    start_tables(*tables)
+
+    def body(step, carry):
+        legendre_group(
+            step, pairs, place, own, right, left, far_a, far_b, tables, out, rows, cols
+        )
+        return carry
+
+    lax.fori_loop(0, 4, body, 0)
+
+
+def legendre_group(
+    step, pairs, place, own, right, left, far_a, far_b, tables, out, rows, cols
+):
+    _, _, leg_hi, leg_lo, _ = tables
     d = place[0]
 
     def put(k, value):
         start = pl.multiple_of(((d + k) % 4) * ROWS, 8)
         rows[pl.ds(start, ROWS), :] = value
 
-    put(0, own[0])
-    put(3, right[0])
-    put(1, left[0])
-    put(2, jnp.where(step < 2, far_a[0], far_b[0]))
+    put(0, own[step])
+    put(3, right[step])
+    put(1, left[step])
+    put(2, jnp.where(step < 2, far_a[jnp.minimum(step, 1)], far_b[jnp.maximum(step - 2, 0)]))
     cols[...] = rows[...].T
-    fetch(step, hi_hbm, lo_hbm, leg_hi, leg_lo, sem)
+    for q in range(4):
+        next_tables(4 * step + q, *tables)
     sums = []
     for q in range(4):
-        n = 4 * step + q
-        lo_order = pairs[n]
+        lo_order = pairs[4 * step + q]
+        n = (4 * step + q) % RING
         odd = lo_order % 2
         x = cols[32 * q : 32 * q + 32, 0:M]
         r = lax.broadcasted_iota(jnp.int32, (1, M), 1)
@@ -115,155 +131,180 @@
             )
         )
     for p in range(2):
-        out[:, p] = jnp.concatenate(sums[2 * p : 2 * p + 2], axis=0).T.reshape(32, 8, 128)
-
-
-def prepare_kernel(leg, hi_out, lo_out, raw, hi_buf, lo_buf, sem):
-    step = pl.program_id(0)
-
+        out[:, 2 * step + p] = jnp.concatenate(sums[2 * p : 2 * p + 2], axis=0).T.reshape(32, 8, 128)
+
+
+DEPTH = 4
+
+
+def prepare_kernel(leg, hi_out, lo_out, raw, hi_buf, lo_buf, load_sem, store_sem):
     def load(n):
-        return pltpu.make_async_copy(leg.at[n], raw.at[n], sem.at[0, n])
+        slot = n % DEPTH
+        return pltpu.make_async_copy(leg.at[n], raw.at[slot], load_sem.at[slot])
 
     def store(n):
+        slot = n % DEPTH
         return (
-            pltpu.make_async_copy(hi_buf.at[n], hi_out.at[n], sem.at[1, n]),
-            pltpu.make_async_copy(lo_buf.at[n], lo_out.at[n], sem.at[2, n]),
+            pltpu.make_async_copy(hi_buf.at[slot], hi_out.at[n], store_sem.at[0, slot]),
+            pltpu.make_async_copy(lo_buf.at[slot], lo_out.at[n], store_sem.at[1, slot]),
         )
 
-    @pl.when(step == 0)
-    def _():
-        for n in range(SLOTS):
-            load(n).start()
-
-    load(step).wait()
-    for t in range(2):
-        hi, lo = split(raw[step, pl.ds(t, ALL_ROWS, stride=2), :])
-        hi_buf[step, :, 128 * t : 128 * t + 128] = hi
-        lo_buf[step, :, 128 * t : 128 * t + 128] = lo
-    for copy in store(step):
-        copy.start()
-
-    @pl.when(step == SLOTS - 1)
-    def _():
-        for n in range(SLOTS):
-            for copy in store(n):
+    for n in range(DEPTH):
+        load(n).start()
+
+    def body(n, carry):
+        load(n).wait()
+
+        @pl.when(n >= DEPTH)
+        def _():
+            for copy in store(n - DEPTH):
                 copy.wait()
 
+        slot = n % DEPTH
+        for t in range(2):
+            hi, lo = split(raw[slot, pl.ds(t, ALL_ROWS, stride=2), :])
+            hi_buf[slot, :, 128 * t : 128 * t + 128] = hi
+            lo_buf[slot, :, 128 * t : 128 * t + 128] = lo
+        for copy in store(n):
+            copy.start()
+
+        @pl.when(n + DEPTH < SLOTS)
+        def _():
+            load(n + DEPTH).start()
+
+        return carry
+
+    lax.fori_loop(0, SLOTS, body, 0)
+    for n in range(SLOTS - DEPTH, SLOTS):
+        for copy in store(n):
+            copy.wait()
+
 
 ANY = pl.BlockSpec(memory_space=pl.ANY)
+ON_CHIP = pl.BlockSpec(memory_space=pltpu.VMEM)
+SCALARS = pl.BlockSpec(memory_space=pltpu.SMEM)
 
 
 def prepare(leg):
-    shape = jax.ShapeDtypeStruct((SLOTS, ALL_ROWS, QLAT), BF16)
-    buffer = pltpu.VMEM((SLOTS, ALL_ROWS, QLAT), BF16)
+    shape = pltpu.HBM((SLOTS, ALL_ROWS, QLAT), BF16)
+    buffer = pltpu.VMEM((DEPTH, ALL_ROWS, QLAT), BF16)
     return pl.pallas_call(
         prepare_kernel,
-        grid=(SLOTS,),
         in_specs=[ANY],
         out_specs=(ANY, ANY),
         out_shape=(shape, shape),
         scratch_shapes=[
-            pltpu.VMEM((SLOTS, 2 * ALL_ROWS, 128), F32),
+            pltpu.VMEM((DEPTH, 2 * ALL_ROWS, 128), F32),
             buffer,
             buffer,
-            pltpu.SemaphoreType.DMA((3, SLOTS)),
+            pltpu.SemaphoreType.DMA((DEPTH,)),
+            pltpu.SemaphoreType.DMA((2, DEPTH)),
         ],
-        compiler_params=params(dimension_semantics=("arbitrary",)),
+        compiler_params=params(),
         cost_estimate=cost(11),
         name="prepare",
-    )(leg)
-
-
+    )(in_hbm(leg))
+
+
+def in_hbm(x):
+    return pltpu.with_memory_space_constraint(x, pltpu.HBM)
+
+
+RING = 12
+AHEAD = 8
 LEG_SCRATCH = [
-    pltpu.VMEM((SLOTS, ALL_ROWS, QLAT), BF16),
-    pltpu.VMEM((SLOTS, ALL_ROWS, QLAT), BF16),
-    pltpu.SemaphoreType.DMA((2, SLOTS)),
+    pltpu.VMEM((RING, ALL_ROWS, QLAT), BF16),
+    pltpu.VMEM((RING, ALL_ROWS, QLAT), BF16),
+    pltpu.SemaphoreType.DMA((2, RING)),
 ]
 
 
-def fetch(step, hi_hbm, lo_hbm, leg_hi, leg_lo, sem):
-    def loads(group):
-        return [
-            pltpu.make_async_copy(src.at[4 * group + n], dst.at[4 * group + n], sem.at[i, 4 * group + n])
-            for n in range(4)
-            for i, (src, dst) in enumerate(((hi_hbm, leg_hi), (lo_hbm, leg_lo)))
-        ]
-
-    @pl.when(step == 0)
+def slot_tables(n, hi_hbm, lo_hbm, leg_hi, leg_lo, sem):
+    slot = n % RING
+    return (
+        pltpu.make_async_copy(hi_hbm.at[n], leg_hi.at[slot], sem.at[0, slot]),
+        pltpu.make_async_copy(lo_hbm.at[n], leg_lo.at[slot], sem.at[1, slot]),
+    )
+
+
+def start_tables(*refs):
+    for n in range(AHEAD):
+        for copy in slot_tables(n, *refs):
+            copy.start()
+
+
+def next_tables(n, *refs):
+    for copy in slot_tables(n, *refs):
+        copy.wait()
+
+    @pl.when(n + AHEAD < SLOTS)
     def _():
-        for copy in loads(0):
+        for copy in slot_tables(n + AHEAD, *refs):
             copy.start()
 
-    for copy in loads(step):
-        copy.wait()
-
-    @pl.when(step == 0)
-    def _():
-        for copy in loads(1):
-            copy.start()
-
-    @pl.when(step < 2)
-    def _():
-        for copy in loads(step + 2):
-            copy.start()
-
 
 def legendre_sums(pairs, place, own, right, left, far_a, far_b, leg_hi, leg_lo):
-    def group(i, *_):
-        return (i, 0, 0)
-
-    block = (1, ROWS, 128)
     return pl.pallas_call(
         legendre_kernel,
-        grid_spec=pltpu.PrefetchScalarGridSpec(
-            num_scalar_prefetch=2,
-            grid=(4,),
-            in_specs=[
-                pl.BlockSpec(block, group),
-                pl.BlockSpec(block, group),
-                pl.BlockSpec(block, group),
-                pl.BlockSpec(block, lambda i, *_: (jnp.minimum(i, 1), 0, 0)),
-                pl.BlockSpec(block, lambda i, *_: (jnp.maximum(i - 2, 0), 0, 0)),
-                ANY,
-                ANY,
-            ],
-            out_specs=pl.BlockSpec((32, 2, 8, 128), lambda i, *_: (0, i, 0, 0)),
-            scratch_shapes=[pltpu.VMEM((1152, 128), F32), pltpu.VMEM((128, 1152), F32)]
-            + LEG_SCRATCH,
-        ),
+        in_specs=[SCALARS] * 2 + [ON_CHIP] * 5 + [ANY] * 2,
+        out_specs=ON_CHIP,
         out_shape=jax.ShapeDtypeStruct((32, 8, 8, 128), F32),
-        compiler_params=params(dimension_semantics=("arbitrary",)),
+        scratch_shapes=[pltpu.VMEM((1152, 128), F32), pltpu.VMEM((128, 1152), F32)] + LEG_SCRATCH,
+        compiler_params=params(),
         cost_estimate=cost(10),
         name="legendre_sums",
-    )(pairs, place, own, right, left, far_a, far_b, leg_hi, leg_lo)
+    )(pairs, place, own, right, left, far_a, far_b, in_hbm(leg_hi), in_hbm(leg_lo))
 
 
 def cos_sin(phase):
-    quadrant = (phase + NLON // 8) // (NLON // 4)
-    x = (phase - quadrant * (NLON // 4)).astype(F32) * (2.0 * math.pi / NLON)
+    quadrant = (phase + NLON // 8) >> 9
+    x = (phase - (quadrant << 9)).astype(F32) * (2.0 * math.pi / NLON)
     y = x * x
     s = x * (1.0 + y * (-1 / 6 + y * (1 / 120 + y * (-1 / 5040 + y * (1 / 362880)))))
     c = 1.0 + y * (-1 / 2 + y * (1 / 24 + y * (-1 / 720 + y * (1 / 40320 + y * (-1 / 3628800)))))
-    swap = quadrant % 2 == 1
+    swap = (quadrant & 1) == 1
     cos = jnp.where(swap, s, c)
     sin = jnp.where(swap, c, s)
-    cos = jnp.where((quadrant + 1) % 4 >= 2, -cos, cos)
-    return cos, jnp.where(quadrant % 4 >= 2, -sin, sin)
-
-
-def table_kernel(orders, hi_ref, lo_ref):
-    m = orders[0]
+    cos = jnp.where(((quadrant + 1) & 2) != 0, -cos, cos)
+    return cos, jnp.where((quadrant & 2) != 0, -sin, sin)
+
+
+def table_kernel(orders, hi_out, lo_out, hi_buf, lo_buf, sem):
+    def stores(n):
+        rows = pl.ds(2 * n, 2)
+        return (
+            pltpu.make_async_copy(hi_buf.at[rows], hi_out.at[rows], sem.at[0, n]),
+            pltpu.make_async_copy(lo_buf.at[rows], lo_out.at[rows], sem.at[1, n]),
+        )
+
+    def body(n, carry):
+        table_pair(n, orders, hi_buf, lo_buf)
+        for copy in stores(n):
+            copy.start()
+        return carry
+
+    lax.fori_loop(0, 4, body, 0)
+    for n in range(4):
+        for copy in stores(n):
+            copy.wait()
+
+
+TABLE = pltpu.VMEM((8, QLAT, HALF), BF16)
+
+
+def table_pair(n, orders, hi_ref, lo_ref):
+    m = orders[n]
     product = m * lax.broadcasted_iota(jnp.int32, (1, 128), 1)
-    cb, sb = cos_sin(product % NLON)
+    cb, sb = cos_sin(product & (NLON - 1))
     factor = 1.0 / math.sqrt(NLON)
     cb, sb = cb * factor, sb * factor
-    ca, sa = cos_sin(product % 16 * 128)
+    ca, sa = cos_sin((product & 15) << 7)
     for a in range(8):
         c1, s1 = ca[:, a : a + 1], sa[:, a : a + 1]
         for part, value in ((0, c1 * cb - s1 * sb), (1, -(s1 * cb + c1 * sb))):
             hi, lo = split(value)
-            hi_ref[part, :, 128 * a : 128 * a + 128] = hi
-            lo_ref[part, :, 128 * a : 128 * a + 128] = lo
+            hi_ref[2 * n + part, :, 128 * a : 128 * a + 128] = hi
+            lo_ref[2 * n + part, :, 128 * a : 128 * a + 128] = lo
 
 
 def fourier_tables(pair_of_slot):
@@ -274,21 +315,31 @@
     odd = jnp.where(flip, first, second)
     orders = jnp.stack([even, odd], 0).reshape(2, QLAT, 2).transpose(0, 2, 1).reshape(4, QLAT, 1)
     orders = jnp.broadcast_to(orders, (4, QLAT, 128))
-    shape = jax.ShapeDtypeStruct((8, QLAT, HALF), BF16)
-    out = pl.BlockSpec((2, QLAT, HALF), lambda i: (i, 0, 0))
+    shape = pltpu.HBM((8, QLAT, HALF), BF16)
     return pl.pallas_call(
         table_kernel,
-        grid=(4,),
-        in_specs=[pl.BlockSpec((1, QLAT, 128), lambda i: (i, 0, 0))],
-        out_specs=(out, out),
+        in_specs=[ON_CHIP],
+        out_specs=(ANY, ANY),
         out_shape=(shape, shape),
-        compiler_params=params(dimension_semantics=("arbitrary",)),
+        scratch_shapes=[TABLE, TABLE, pltpu.SemaphoreType.DMA((2, 4))],
+        compiler_params=params(),
         cost_estimate=cost(5),
         name="tables",
     )(orders)
 
 
-def to_grid(recv, t_hi, t_lo, z):
+def table_loads(hi_hbm, lo_hbm, t_hi, t_lo, sem, nb):
+    cols = pl.ds(256 * nb, 256)
+    return (
+        pltpu.make_async_copy(hi_hbm.at[:, :, cols], t_hi.at[:, :, cols], sem.at[0, nb]),
+        pltpu.make_async_copy(lo_hbm.at[:, :, cols], t_lo.at[:, :, cols], sem.at[1, nb]),
+    )
+
+
+def to_grid(recv, hi_hbm, lo_hbm, t_hi, t_lo, sem, z):
+    for nb in range(4):
+        for copy in table_loads(hi_hbm, lo_hbm, t_hi, t_lo, sem, nb):
+            copy.start()
     for j in range(8):
         hi, lo = split(recv[:, j, :].T)
         for n in range(8):
@@ -297,6 +348,8 @@
 
     def block(nb):
         cols = slice(256 * nb, 256 * nb + 256)
+        for copy in table_loads(hi_hbm, lo_hbm, t_hi, t_lo, sem, nb):
+            copy.wait()
         res = []
         for par in range(2):
             wide = jnp.zeros((256, 256), F32)
@@ -334,8 +387,10 @@
         out[:, j, :] = rows.T
 
 
-def wind_kernel(recv, t_hi, t_lo, out, wind, last, first, speed_ref, z, d, res, g):
-    block = to_grid(recv, t_hi, t_lo, z)
+def wind_kernel(
+    recv, hi_hbm, lo_hbm, out, wind, last, first, speed_ref, z, d, res, t_hi, t_lo, sem, g
+):
+    block = to_grid(recv, hi_hbm, lo_hbm, t_hi, t_lo, sem, z)
     for nb in range(4):
         tend = []
         for side, value in enumerate(block(nb)):
@@ -362,8 +417,10 @@
     from_grid(d, t_hi, t_lo, res, out)
 
 
-def moist_kernel(recv, t_hi, t_lo, speed_ref, heat_ref, out, z, d, res):
-    block = to_grid(recv, t_hi, t_lo, z)
+def moist_kernel(
+    recv, hi_hbm, lo_hbm, speed_ref, heat_ref, out, z, d, res, t_hi, t_lo, sem
+):
+    block = to_grid(recv, hi_hbm, lo_hbm, t_hi, t_lo, sem, z)
     for nb in range(4):
         tend = []
         for side, value in enumerate(block(nb)):
@@ -387,12 +444,16 @@
     pltpu.VMEM((8, 256, 256), BF16),
     pltpu.VMEM((2, 256, HALF), BF16),
     pltpu.VMEM((8, 128, 256), F32),
+    TABLE,
+    TABLE,
+    pltpu.SemaphoreType.DMA((2, 4)),
 ]
 
 
 def wind_stage(recv, t_hi, t_lo):
     return pl.pallas_call(
         wind_kernel,
+        in_specs=[ON_CHIP, ANY, ANY],
         out_shape=(
             jax.ShapeDtypeStruct((QLAT, 8, 128), F32),
             jax.ShapeDtypeStruct((2 * TLEV, 8, NLON), F32),
@@ -404,18 +465,19 @@
         compiler_params=params(),
         cost_estimate=cost(10),
         name="wind_stage",
-    )(recv, t_hi, t_lo)
+    )(recv, in_hbm(t_hi), in_hbm(t_lo))
 
 
 def moist_stage(recv, t_hi, t_lo, speed, heat):
     return pl.pallas_call(
         moist_kernel,
+        in_specs=[ON_CHIP, ANY, ANY, ON_CHIP, ON_CHIP],
         out_shape=jax.ShapeDtypeStruct((QLAT, 8, 128), F32),
         scratch_shapes=FOURIER_SCRATCH,
         compiler_params=params(),
         cost_estimate=cost(10),
         name="moist_stage",
-    )(recv, t_hi, t_lo, speed, heat)
+    )(recv, in_hbm(t_hi), in_hbm(t_lo), speed, heat)
 
 
 def halo_of(above, below):
@@ -537,15 +599,29 @@
     pairs, place, recv, weight, hi_hbm, lo_hbm,
     own, ahead, far_a, far_b, behind, res, leg_hi, leg_lo, sem,
 ):
-    step = pl.program_id(0)
+    tables = (hi_hbm, lo_hbm, leg_hi, leg_lo, sem)
+    start_tables(*tables)
+
+    def body(step, carry):
+        tendency_group(
+            step, pairs, place, recv, weight, tables, own, ahead, far_a, far_b, behind, res
+        )
+        return carry
+
+    lax.fori_loop(0, 4, body, 0)
+
+
+def tendency_group(
+    step, pairs, place, recv, weight, tables, own, ahead, far_a, far_b, behind, res
+):
+    _, _, leg_hi, leg_lo, _ = tables
     d = place[0]
-    fetch(step, hi_hbm, lo_hbm, leg_hi, leg_lo, sem)
     lane = lax.broadcasted_iota(jnp.int32, (1, 128), 1)
     rhs = []
     bound = jnp.zeros((1, 128), jnp.int32)
     for b in range(4):
         lo_order = pairs[4 * step + b]
-        f = recv[:, b // 2].reshape(QLAT, 128) * weight[...]
+        f = recv[:, 2 * step + b // 2].reshape(QLAT, 128) * weight[...]
         even = pltpu.roll(f, (32 * b - 64 * (b % 2)) % 128, 1)
         odd = pltpu.roll(f, (32 * b - 64 * (b % 2) - 32) % 128, 1)
         here = lane // 32 == b
@@ -555,12 +631,15 @@
         rhs.append(split(jnp.concatenate([low, high], axis=1)))
         bound = jnp.where(here, M - lo_order, bound)
     rhs = jnp.concatenate([x for hi, lo in rhs for x in (hi, lo, hi)], axis=0)
+    for b in range(4):
+        next_tables(4 * step + b, *tables)
     for part in range(2):
         rows = slice(PART_ROWS * part, PART_ROWS * (part + 1))
         lhs = []
         for b in range(4):
-            hi = leg_hi[4 * step + b, rows, :]
-            lhs += [hi, hi, leg_lo[4 * step + b, rows, :]]
+            n = (4 * step + b) % RING
+            hi = leg_hi[n, rows, :]
+            lhs += [hi, hi, leg_lo[n, rows, :]]
         both = mm(jnp.concatenate(lhs, axis=1), rhs)
         r = PART_ROWS * part + lax.broadcasted_iota(jnp.int32, (PART_ROWS, 1), 0)
         value = jnp.where(r < bound, both[:, 0:128], both[:, 128:256])
@@ -569,49 +648,32 @@
     def get(k):
         return res[pl.ds(pl.multiple_of(((d + k) % 4) * ROWS, 8), ROWS), :]
 
-    own[0] = get(0)
-    ahead[0] = get(1)
-    behind[0] = get(3)
+    own[step] = get(0)
+    ahead[step] = get(1)
+    behind[step] = get(3)
 
     @pl.when(step < 2)
     def _():
-        far_a[0] = get(2)
+        far_a[step] = get(2)
 
     @pl.when(step >= 2)
     def _():
-        far_b[0] = get(2)
+        far_b[step - 2] = get(2)
 
 
 def tendency_sums(pairs, place, recv, weight, leg_hi, leg_lo):
-    size = (1, ROWS, 128)
-    block = pl.BlockSpec(size, lambda i, *_: (i, 0, 0))
     full = jax.ShapeDtypeStruct((4, ROWS, 128), F32)
     part = jax.ShapeDtypeStruct((2, ROWS, 128), F32)
     return pl.pallas_call(
         tendency_kernel,
-        grid_spec=pltpu.PrefetchScalarGridSpec(
-            num_scalar_prefetch=2,
-            grid=(4,),
-            in_specs=[
-                pl.BlockSpec((32, 2, 8, 128), lambda i, *_: (0, i, 0, 0)),
-                pl.BlockSpec((QLAT, 128), lambda i, *_: (0, 0)),
-                ANY,
-                ANY,
-            ],
-            out_specs=(
-                block,
-                block,
-                pl.BlockSpec(size, lambda i, *_: (jnp.minimum(i, 1), 0, 0)),
-                pl.BlockSpec(size, lambda i, *_: (jnp.maximum(i - 2, 0), 0, 0)),
-                block,
-            ),
-            scratch_shapes=[pltpu.VMEM((ALL_ROWS, 128), F32)] + LEG_SCRATCH,
-        ),
+        in_specs=[SCALARS] * 2 + [ON_CHIP] * 2 + [ANY] * 2,
+        out_specs=(ON_CHIP,) * 5,
         out_shape=(full, full, part, part, full),
-        compiler_params=params(dimension_semantics=("arbitrary",)),
+        scratch_shapes=[pltpu.VMEM((ALL_ROWS, 128), F32)] + LEG_SCRATCH,
+        compiler_params=params(),
         cost_estimate=cost(10),
         name="tendency_sums",
-    )(pairs, place, recv, weight, leg_hi, leg_lo)
+    )(pairs, place, recv, weight, in_hbm(leg_hi), in_hbm(leg_lo))
 
 
 def unpack_kernel(a0, a1, a2, b0, b1, b2, out, scr):

time: 257 us -> 239 us (0.930)
  Pallas kernels: 111 us -> 92.7 us
    pallas_call x8, Pallas kernels: 92.6 us -> 78.4 us  [the longest x2 23.7 us: tendency_sums(): pl.pallas_call(tendency_kernel, in_specs=[SCALARS] * 2 + [ON_CHIP] * 2 +...]
    unnamed x49 -> x19, local copies, waits for them, and re-layouts: 5.35 us -> 5.85 us
  transfers between devices with their start and end apart: 24 -> 24, of which waited for: 8 -> 8; matrix products, arithmetic and copies ran while one was open for 4% -> 3% of each run, Pallas kernels for 41% -> 38%
where the time goes in v2:
time: 239 us; the launch traced here: 236 us
  Pallas kernels  92.7 us (39%)
  starting transfers between devices  74.5 us (31%)
  waiting for transfers between devices  54 us (23%)
  local copies, waits for them, and re-layouts  12.3 us (5%)
    ppermute x16, waiting for transfers between devices, shift(): return lax.ppermute(x, axis, [(i, (i + by) % n) for i in range(n)])  52.1 us
    all_to_all x4, starting transfers between devices, exchange(): return lax.all_to_all(x, 'ma', 0, 0, tiled=True)  36.3 us
    ppermute x16, starting transfers between devices, shift(): return lax.ppermute(x, axis, [(i, (i + by) % n) for i in range(n)])  24.3 us
    pallas_call x2, Pallas kernels, tendency_sums(): pl.pallas_call(tendency_kernel, in_specs=[SCALARS] * 2 + [ON_CHIP] * 2 +...  23.7 us
    pallas_call x2, Pallas kernels, legendre_sums(): pl.pallas_call(legendre_kernel, in_specs=[SCALARS] * 2 + [ON_CHIP] * 5 +...  17.9 us
    pallas_call x1, Pallas kernels, prepare(): pl.pallas_call(prepare_kernel, in_specs=[ANY], out_specs=(ANY, ANY), out_...  12.6 us
    pallas_call x1, Pallas kernels, transport(): pl.pallas_call(advect_kernel, grid_spec=pltpu.PrefetchScalarGridSpec(num_...  11.4 us
    ppermute x2, starting transfers between devices, neighbours(): lax.ppermute(first, axes, [(b, a) for a, b in down])  10.1 us
  transfers between devices with their start and end apart: 24, of which 8 were waited for; matrix products, arithmetic and copies ran while one was open for 3% of the time, Pallas kernels for 38%

profile of v2, /device:TPU:1, one launch (start us, length us, event | category | flops | bytes accessed | tf_op | source)
XLA Modules:
  0.0 235.7 jit_solution(4206239570941395237)
XLA Ops:
  0.6 1.4 copy-done.1
  2.0 1.3 pack.1
  3.4 2.0 collective-permute-start
  5.4 1.3 collective-permute-start.1
  6.7 11.6 %collective-permute-done.right = f32[4,264,128]{2,1,0:T(8,128)S(1)} collective-permute-done((f32[4,264,128]{2,1,0:T(8,128)S(1)}, f32[4,264,128]{2,1,0:T(8,128)S(1)}, u32[]{:S(2)}, u32[]{:S(2)}) %collective-permute-start) | collective-permute-done | bytes 540704 | tf_op jit(solution)/shard_map/ppermute | solution.py:704
  18.3 0.7 slice.56
  19.0 0.3 collective-permute-start.2
  19.3 0.7 slice.57
  20.0 2.4 %collective-permute-start.3 = (f32[2,264,128]{2,1,0:T(8,128)}, f32[2,264,128]{2,1,0:T(8,128)S(1)}, u32[]{:S(2)}, u32[]{:S(2)}) collective-permute-start(f32[2,264,128]{2,1,0:T(8,128)} %slice.57), channel_id=1, source_target_pairs={{0,3},{1,0},{2,1},{3,2},{4,7},{5,4},{6,5},{7,6},{8,11},{9,8},{10,9... | collective-permute-start | bytes 811016 | tf_op jit(solution)/shard_map/ppermute | solution.py:704
  22.4 0.8 dynamic_slice.3.pairs
  23.1 12.6 %prepare.1 = (bf16[16,1056,256]{2,1,0:T(8,128)(2,1)}, bf16[16,1056,256]{2,1,0:T(8,128)(2,1)}) custom-call(f32[16,2112,128]{2,1,0:T(8,128)} %bitcast.15), custom_call_target="tpu_custom_call" | custom-call | flops 2750000128 | bytes 1048576 | tf_op jit(solution)/shard_map/prepare/pallas_call | solution.py:191
  35.8 2.7 %collective-permute-start.9 = (f32[4,264,128]{2,1,0:T(8,128)}, f32[4,264,128]{2,1,0:T(8,128)S(1)}, u32[]{:S(2)}, u32[]{:S(2)}) collective-permute-start(f32[4,264,128]{2,1,0:T(8,128)} %get-tuple-element.42.own), channel_id=1, source_target_pairs={{0,3},{1,0},{2,1},{3,2},{4,7},{5,4},{6,5},{7,6},{8,11},{9,8},{10,9... | collective-permute-start | bytes 1622024 | tf_op jit(solution)/shard_map/ppermute | solution.py:704
  38.5 8.7 %legendre_sums.2 = f32[32,8,8,128]{3,2,1,0:T(8,128)} custom-call(s32[16]{0:T(128)S(1)} %dynamic_slice.3.pairs, s32[1]{0:T(128)} %bitcast.place, f32[4,264,128]{2,1,0:T(8,128)S(1)} %get-tuple-element.28.own, f32[4,264,128]{2,1,0:T(8,128)S(1)} %collective-permute-done.right, f32[4,264,128]{2,1,0:T(8,128)S(1)} %collective-permute-done.1.left, ...), custom_call_target="tpu_custom_call" | custom-call | flops 2500000000 | bytes 1048576 | tf_op jit(solution)/shard_map/legendre_sums/pallas_call | solution.py:247
  47.2 11.0 %all-to-all-start = ((f32[32,8,8,128]{3,2,1,0:T(8,128)}), f32[32,8,8,128]{3,2,1,0:T(8,128)S(1)}, u32[]{:S(2)}, u32[]{:S(2)}) async-start(f32[32,8,8,128]{3,2,1,0:T(8,128)} %legendre_sums.2), calls=%async_computation | async-start | bytes 2097152 | tf_op jit(solution)/shard_map/all_to_all | solution.py:732
  58.4 2.7 %collective-permute-start.11 = (f32[2,264,128]{2,1,0:T(8,128)S(1)}, f32[2,264,128]{2,1,0:T(8,128)S(1)}, u32[]{:S(2)}, u32[]{:S(2)}) collective-permute-start(f32[2,264,128]{2,1,0:T(8,128)S(1)} %slice.59), channel_id=1, source_target_pairs={{0,3},{1,0},{2,1},{3,2},{4,7},{5,4},{6,5},{7,6},{8,11},{9,8},{10,9... | collective-permute-start | bytes 811016 | tf_op jit(solution)/shard_map/ppermute | solution.py:704
  61.1 6.2 %collective-permute-done.10.far_a = f32[2,264,128]{2,1,0:T(8,128)S(1)} collective-permute-done((f32[2,264,128]{2,1,0:T(8,128)S(1)}, f32[2,264,128]{2,1,0:T(8,128)S(1)}, u32[]{:S(2)}, u32[]{:S(2)}) %collective-permute-start.10) | collective-permute-done | bytes 270368 | tf_op jit(solution)/shard_map/ppermute | solution.py:704
  67.3 9.2 %legendre_sums.3 = f32[32,8,8,128]{3,2,1,0:T(8,128)} custom-call(s32[16]{0:T(128)S(1)} %dynamic_slice.3.pairs, s32[1]{0:T(128)} %bitcast.place, f32[4,264,128]{2,1,0:T(8,128)} %get-tuple-element.42.own, f32[4,264,128]{2,1,0:T(8,128)S(1)} %collective-permute-done.8.right, f32[4,264,128]{2,1,0:T(8,128)S(1)} %collective-permute-done.9.left, ...), custom_call_target="tpu_custom_call" | custom-call | flops 2500000000 | bytes 1048576 | tf_op jit(solution)/shard_map/legendre_sums/pallas_call | solution.py:247
  76.6 8.1 %all-to-all-start.2 = ((f32[32,8,8,128]{3,2,1,0:T(8,128)}), f32[32,8,8,128]{3,2,1,0:T(8,128)S(1)}, u32[]{:S(2)}, u32[]{:S(2)}) async-start(f32[32,8,8,128]{3,2,1,0:T(8,128)} %legendre_sums.3), calls=%async_computation.2 | async-start | bytes 2097152 | tf_op jit(solution)/shard_map/all_to_all | solution.py:732
  84.7 3.5 %fusion.2 = (f32[12,2,4,2048]{3,2,1,0:T(4,128)}, f32[12,2,4,2048]{3,2,1,0:T(4,128)}) fusion(f32[12,2,8,2048]{3,2,1,0:T(8,128)} %tracer.1), kind=kLoop, calls=%fused_computation.16 | loop fusion | bytes 3145728 | tf_op jit(solution)/shard_map/slice | solution.py:753
  88.1 1.9 collective-permute-start.12
  90.1 5.0 %collective-permute-start.13 = (f32[12,2,4,2048]{3,2,1,0:T(4,128)}, f32[12,2,4,2048]{3,2,1,0:T(4,128)}, u32[]{:S(2)}, u32[]{:S(2)}) collective-permute-start(f32[12,2,4,2048]{3,2,1,0:T(4,128)} %get-tuple-element.54), channel_id=1, source_target_pairs={{1,0},{2,1},{3,2},{4,3},{5,4},{6,5},{7,6},{8,7},{9,8},{10,9},{11,1... | collective-permute-start | bytes 2359304 | tf_op jit(solution)/shard_map/ppermute | solution.py:713
  95.8 6.4 %tables.1 = (bf16[8,256,1024]{2,1,0:T(8,128)(2,1)}, bf16[8,256,1024]{2,1,0:T(8,128)(2,1)}) custom-call(s32[4,256,128]{2,1,0:T(8,128)S(1)} %broadcast_in_dim.15.orders), custom_call_target="tpu_custom_call" | custom-call | flops 1250000000 | bytes 1048576 | tf_op jit(solution)/shard_map/tables/pallas_call | solution.py:319
  102.3 9.0 %wind_stage.1 = (f32[256,8,128]{2,1,0:T(8,128)}, f32[4,8,2048]{2,1,0:T(8,128)S(1)}, f32[4,4,2048]{2,1,0:T(4,128)S(1)}, f32[4,4,2048]{2,1,0:T(4,128)S(1)}, f32[64,2048]{1,0:T(8,128)S(1)}) custom-call(f32[256,8,128]{2,1,0:T(8,128)S(1)} %bitcast.12, bf16[8,256,1024]{2,1,0:T(8,128)(2,1)} %get-tuple-element.34.hi_hbm, bf16[8,256,1024]{2,1,0:T(8,128)(2,1)} %get-tuple-element.35.lo_hbm), custom_call_target="tpu_custom_call" | custom-call | flops 2500000000 | bytes 1048576 | tf_op jit(solution)/shard_map/wind_stage/pallas_call | solution.py:454
  111.3 0.7 copy-done.2
  112.0 0.6 copy-done.4
  112.7 0.6 copy-done.5
  113.3 8.3 %all-to-all-start.1 = ((f32[32,8,8,128]{3,2,1,0:T(8,128)}), f32[32,8,8,128]{3,2,1,0:T(8,128)S(1)}, u32[]{:S(2)}, u32[]{:S(2)}) async-start(f32[32,8,8,128]{3,2,1,0:T(8,128)} %bitcast.5), calls=%async_computation.1 | async-start | bytes 2097152 | tf_op jit(solution)/shard_map/all_to_all | solution.py:732
  121.6 1.9 collective-permute-start.14
  123.5 5.1 %collective-permute-start.15 = (f32[4,4,2048]{2,1,0:T(4,128)}, f32[4,4,2048]{2,1,0:T(4,128)}, u32[]{:S(2)}, u32[]{:S(2)}) collective-permute-start(f32[4,4,2048]{2,1,0:T(4,128)} %copy-done.4), channel_id=1, source_target_pairs={{1,0},{2,1},{3,2},{4,3},{5,4},{6,5},{7,6},{8,7},{9,8},{10,9},{11,1... | collective-permute-start | bytes 393224 | tf_op jit(solution)/shard_map/ppermute | solution.py:713
  128.7 1.5 collective-permute-done.14.wind_above
  130.2 0.4 collective-permute-done.15.wind_below
  130.6 1.4 copy-done
  132.0 0.9 copy-done.3
  133.0 11.4 %transport.1 = (f32[12,2,8,2048]{3,2,1,0:T(8,128)}, f32[16,64,128]{2,1,0:T(8,128)S(1)}) custom-call(f32[12,2]{1,0:T(8,128)S(1)} %copy.14.rate, s32[1]{0:T(128)} %bitcast.8.band, f32[12,2,8,2048]{3,2,1,0:T(8,128)S(1)} %copy-done, f32[12,2,4,2048]{3,2,1,0:T(4,128)S(1)} %collective-permute-done.12.above, f32[12,2,4,2048]{3,2,1,0:T(4,128)} %collective-permute-done.13.below, ...), custom_call_target="tpu_custom_call" | custom-call | flops 2500000000 | bytes 1048576 | tf_op jit(solution)/shard_map/transport/pallas_call | solution.py:573
  144.4 8.7 %moist_stage.1 = f32[256,8,128]{2,1,0:T(8,128)} custom-call(f32[256,8,128]{2,1,0:T(8,128)S(1)} %bitcast.13, bf16[8,256,1024]{2,1,0:T(8,128)(2,1)} %get-tuple-element.34.hi_hbm, bf16[8,256,1024]{2,1,0:T(8,128)(2,1)} %get-tuple-element.35.lo_hbm, f32[64,2048]{1,0:T(8,128)S(1)} %get-tuple-element.43.speed_ref, f32[16,64,128]{2,1,0:T(8,128)S(1)} %get-tuple-element.47.heat_ref), custom_call_target="tpu_custom_call" | custom-call | flops 2500000000 | bytes 1048576 | tf_op jit(solution)/shard_map/moist_stage/pallas_call | solution.py:472
  153.2 8.9 %all-to-all-start.3 = ((f32[32,8,8,128]{3,2,1,0:T(8,128)}), f32[32,8,8,128]{3,2,1,0:T(8,128)S(1)}, u32[]{:S(2)}, u32[]{:S(2)}) async-start(f32[32,8,8,128]{3,2,1,0:T(8,128)} %bitcast.9), calls=%async_computation.3 | async-start | bytes 2097152 | tf_op jit(solution)/shard_map/all_to_all | solution.py:732
  162.1 12.2 %tendency_sums.2 = (f32[4,264,128]{2,1,0:T(8,128)S(1)}, f32[4,264,128]{2,1,0:T(8,128)S(1)}, f32[2,264,128]{2,1,0:T(8,128)}, f32[2,264,128]{2,1,0:T(8,128)S(1)}, f32[4,264,128]{2,1,0:T(8,128)S(1)}) custom-call(s32[16]{0:T(128)S(1)} %dynamic_slice.3.pairs, s32[1]{0:T(128)} %bitcast.place, f32[32,8,8,128]{3,2,1,0:T(8,128)S(1)} %all-to-all-done.1.recv, ...), custom_call_target="tpu_custom_call" | custom-call | flops 2500000000 | bytes 1048576 | tf_op jit(solution)/shard_map/tendency_sums/pallas_call | solution.py:667
  174.4 5.6 %collective-permute-start.6 = (f32[2,264,128]{2,1,0:T(8,128)S(1)}, f32[2,264,128]{2,1,0:T(8,128)S(1)}, u32[]{:S(2)}, u32[]{:S(2)}) collective-permute-start(f32[2,264,128]{2,1,0:T(8,128)S(1)} %get-tuple-element.41), channel_id=1, source_target_pairs={{0,3},{1,0},{2,1},{3,2},{4,7},{5,4},{6,5},{7,6},{8,11},{9,8},{10,9... | collective-permute-start | bytes 811016 | tf_op jit(solution)/shard_map/ppermute | solution.py:704
  180.0 5.6 %collective-permute-done.6 = f32[2,264,128]{2,1,0:T(8,128)S(1)} collective-permute-done((f32[2,264,128]{2,1,0:T(8,128)S(1)}, f32[2,264,128]{2,1,0:T(8,128)S(1)}, u32[]{:S(2)}, u32[]{:S(2)}) %collective-permute-start.6) | collective-permute-done | bytes 270368 | tf_op jit(solution)/shard_map/ppermute | solution.py:704
  185.7 0.8 pad_maximum_fusion.1
  186.5 3.4 %collective-permute-start.7 = (f32[4,264,128]{2,1,0:T(8,128)}, f32[4,264,128]{2,1,0:T(8,128)S(1)}, u32[]{:S(2)}, u32[]{:S(2)}) collective-permute-start(f32[4,264,128]{2,1,0:T(8,128)} %pad_maximum_fusion.1), channel_id=1, source_target_pairs={{0,3},{1,0},{2,1},{3,2},{4,7},{5,4},{6,5},{7,6},{8,11},{9,8},{10,9... | collective-permute-start | bytes 1622024 | tf_op jit(solution)/shard_map/ppermute | solution.py:704
  189.9 11.5 %tendency_sums.3 = (f32[4,264,128]{2,1,0:T(8,128)S(1)}, f32[4,264,128]{2,1,0:T(8,128)S(1)}, f32[2,264,128]{2,1,0:T(8,128)S(1)}, f32[2,264,128]{2,1,0:T(8,128)S(1)}, f32[4,264,128]{2,1,0:T(8,128)S(1)}) custom-call(s32[16]{0:T(128)S(1)} %dynamic_slice.3.pairs, s32[1]{0:T(128)} %bitcast.place, f32[32,8,8,128]{3,2,1,0:T(8,128)S(1)} %all-to-all-done.3.recv, ...), custom_call_target="tpu_custom_call" | custom-call | flops 2500000000 | bytes 1048576 | tf_op jit(solution)/shard_map/tendency_sums/pallas_call | solution.py:667
  201.6 1.5 collective-permute-start.5
  203.2 5.0 %collective-permute-done.18 = f32[2,264,128]{2,1,0:T(8,128)S(1)} collective-permute-done((f32[2,264,128]{2,1,0:T(8,128)S(1)}, f32[2,264,128]{2,1,0:T(8,128)S(1)}, u32[]{:S(2)}, u32[]{:S(2)}) %collective-permute-start.18) | collective-permute-done | bytes 270368 | tf_op jit(solution)/shard_map/ppermute | solution.py:704
  208.2 2.0 collective-permute-start.19
  210.3 10.9 %collective-permute-done.16 = f32[2,264,128]{2,1,0:T(8,128)S(1)} collective-permute-done((f32[2,264,128]{2,1,0:T(8,128)S(1)}, f32[2,264,128]{2,1,0:T(8,128)S(1)}, u32[]{:S(2)}, u32[]{:S(2)}) %collective-permute-start.16) | collective-permute-done | bytes 270368 | tf_op jit(solution)/shard_map/ppermute | solution.py:704
  221.4 12.8 %collective-permute-done.17.b1 = f32[4,264,128]{2,1,0:T(8,128)S(1)} collective-permute-done((f32[4,264,128]{2,1,0:T(8,128)S(1)}, f32[4,264,128]{2,1,0:T(8,128)S(1)}, u32[]{:S(2)}, u32[]{:S(2)}) %collective-permute-start.17) | collective-permute-done | bytes 540704 | tf_op jit(solution)/shard_map/ppermute | solution.py:704
  234.1 1.6 unpack.1
  (53 shorter events, 1.7 us)
Async XLA Ops:
  0.6 1.4 copy-start.1
  3.4 14.9 %collective-permute-start = (f32[4,264,128]{2,1,0:T(8,128)S(1)}, f32[4,264,128]{2,1,0:T(8,128)S(1)}, u32[]{:S(2)}, u32[]{:S(2)}) collective-permute-start(f32[4,264,128]{2,1,0:T(8,128)S(1)} %get-tuple-element.28.own), channel_id=1, source_target_pairs={{0,1},{1,2},{2,3},{3,0},{4,5},{5,6},{6,7},{7,4},{8,9},{9,10},{10,1... | collective-permute-start | bytes 1622024 | tf_op jit(solution)/shard_map/ppermute | solution.py:704
  5.4 13.9 %collective-permute-start.1 = (f32[4,264,128]{2,1,0:T(8,128)S(1)}, f32[4,264,128]{2,1,0:T(8,128)S(1)}, u32[]{:S(2)}, u32[]{:S(2)}) collective-permute-start(f32[4,264,128]{2,1,0:T(8,128)S(1)} %get-tuple-element.28.own), channel_id=1, source_target_pairs={{0,3},{1,0},{2,1},{3,2},{4,7},{5,4},{6,5},{7,6},{8,11},{9,8},{10,9... | collective-permute-start | bytes 1622024 | tf_op jit(solution)/shard_map/ppermute | solution.py:704
  19.0 19.5 %collective-permute-start.2 = (f32[2,264,128]{2,1,0:T(8,128)}, f32[2,264,128]{2,1,0:T(8,128)S(1)}, u32[]{:S(2)}, u32[]{:S(2)}) collective-permute-start(f32[2,264,128]{2,1,0:T(8,128)} %slice.56), channel_id=1, source_target_pairs={{0,1},{1,2},{2,3},{3,0},{4,5},{5,6},{6,7},{7,4},{8,9},{9,10},{10,1... | collective-permute-start | bytes 811016 | tf_op jit(solution)/shard_map/ppermute | solution.py:704
  20.0 18.5 %collective-permute-start.3 = (f32[2,264,128]{2,1,0:T(8,128)}, f32[2,264,128]{2,1,0:T(8,128)S(1)}, u32[]{:S(2)}, u32[]{:S(2)}) collective-permute-start(f32[2,264,128]{2,1,0:T(8,128)} %slice.57), channel_id=1, source_target_pairs={{0,3},{1,0},{2,1},{3,2},{4,7},{5,4},{6,5},{7,6},{8,11},{9,8},{10,9... | collective-permute-start | bytes 811016 | tf_op jit(solution)/shard_map/ppermute | solution.py:704
  35.7 22.5 %collective-permute-start.8 = (f32[4,264,128]{2,1,0:T(8,128)}, f32[4,264,128]{2,1,0:T(8,128)S(1)}, u32[]{:S(2)}, u32[]{:S(2)}) collective-permute-start(f32[4,264,128]{2,1,0:T(8,128)} %get-tuple-element.42.own), channel_id=1, source_target_pairs={{0,1},{1,2},{2,3},{3,0},{4,5},{5,6},{6,7},{7,4},{8,9},{9,10},{10,1... | collective-permute-start | bytes 1622024 | tf_op jit(solution)/shard_map/ppermute | solution.py:704
  35.8 22.5 %collective-permute-start.9 = (f32[4,264,128]{2,1,0:T(8,128)}, f32[4,264,128]{2,1,0:T(8,128)S(1)}, u32[]{:S(2)}, u32[]{:S(2)}) collective-permute-start(f32[4,264,128]{2,1,0:T(8,128)} %get-tuple-element.42.own), channel_id=1, source_target_pairs={{0,3},{1,0},{2,1},{3,2},{4,7},{5,4},{6,5},{7,6},{8,11},{9,8},{10,9... | collective-permute-start | bytes 1622024 | tf_op jit(solution)/shard_map/ppermute | solution.py:704
  47.2 29.4 %all-to-all-start = ((f32[32,8,8,128]{3,2,1,0:T(8,128)}), f32[32,8,8,128]{3,2,1,0:T(8,128)S(1)}, u32[]{:S(2)}, u32[]{:S(2)}) async-start(f32[32,8,8,128]{3,2,1,0:T(8,128)} %legendre_sums.2), calls=%async_computation | async-start | bytes 2097152 | tf_op jit(solution)/shard_map/all_to_all | solution.py:732
  58.3 9.1 %collective-permute-start.10 = (f32[2,264,128]{2,1,0:T(8,128)S(1)}, f32[2,264,128]{2,1,0:T(8,128)S(1)}, u32[]{:S(2)}, u32[]{:S(2)}) collective-permute-start(f32[2,264,128]{2,1,0:T(8,128)S(1)} %slice.58), channel_id=1, source_target_pairs={{0,1},{1,2},{2,3},{3,0},{4,5},{5,6},{6,7},{7,4},{8,9},{9,10},{10,1... | collective-permute-start | bytes 811016 | tf_op jit(solution)/shard_map/ppermute | solution.py:704
  58.4 9.0 %collective-permute-start.11 = (f32[2,264,128]{2,1,0:T(8,128)S(1)}, f32[2,264,128]{2,1,0:T(8,128)S(1)}, u32[]{:S(2)}, u32[]{:S(2)}) collective-permute-start(f32[2,264,128]{2,1,0:T(8,128)S(1)} %slice.59), channel_id=1, source_target_pairs={{0,3},{1,0},{2,1},{3,2},{4,7},{5,4},{6,5},{7,6},{8,11},{9,8},{10,9... | collective-permute-start | bytes 811016 | tf_op jit(solution)/shard_map/ppermute | solution.py:704
  76.6 18.5 %copy-start.6 = (s32[512]{0:T(512)S(1)}, s32[512]{0:T(512)}, u32[]{:S(2)}) copy-start(s32[512]{0:T(512)} %param.9) | copy-start | bytes 6148
  76.6 36.7 %all-to-all-start.2 = ((f32[32,8,8,128]{3,2,1,0:T(8,128)}), f32[32,8,8,128]{3,2,1,0:T(8,128)S(1)}, u32[]{:S(2)}, u32[]{:S(2)}) async-start(f32[32,8,8,128]{3,2,1,0:T(8,128)} %legendre_sums.3), calls=%async_computation.2 | async-start | bytes 2097152 | tf_op jit(solution)/shard_map/all_to_all | solution.py:732
  88.1 40.6 %collective-permute-start.12 = (f32[12,2,4,2048]{3,2,1,0:T(4,128)}, f32[12,2,4,2048]{3,2,1,0:T(4,128)S(1)}, u32[]{:S(2)}, u32[]{:S(2)}) collective-permute-start(f32[12,2,4,2048]{3,2,1,0:T(4,128)} %get-tuple-element.55), channel_id=1, source_target_pairs={{0,1},{1,2},{2,3},{3,4},{4,5},{5,6},{6,7},{7,8},{8,9},{9,10},{10,1... | collective-permute-start | bytes 2359304 | tf_op jit(solution)/shard_map/ppermute | solution.py:712
  90.1 38.7 %collective-permute-start.13 = (f32[12,2,4,2048]{3,2,1,0:T(4,128)}, f32[12,2,4,2048]{3,2,1,0:T(4,128)}, u32[]{:S(2)}, u32[]{:S(2)}) collective-permute-start(f32[12,2,4,2048]{3,2,1,0:T(4,128)} %get-tuple-element.54), channel_id=1, source_target_pairs={{1,0},{2,1},{3,2},{4,3},{5,4},{6,5},{7,6},{8,7},{9,8},{10,9},{11,1... | collective-permute-start | bytes 2359304 | tf_op jit(solution)/shard_map/ppermute | solution.py:713
  102.3 26.3 %copy-start.8 = (f32[12,2]{0,1:T(2,128)S(1)}, f32[12,2]{0,1:T(2,128)}, u32[]{:S(2)}) copy-start(f32[12,2]{0,1:T(2,128)} %param.11) | copy-start | bytes 292
  111.3 0.7 copy-start.2
  112.0 0.7 copy-start.4
  112.6 0.6 copy-start.5
  113.3 39.9 %all-to-all-start.1 = ((f32[32,8,8,128]{3,2,1,0:T(8,128)}), f32[32,8,8,128]{3,2,1,0:T(8,128)S(1)}, u32[]{:S(2)}, u32[]{:S(2)}) async-start(f32[32,8,8,128]{3,2,1,0:T(8,128)} %bitcast.5), calls=%async_computation.1 | async-start | bytes 2097152 | tf_op jit(solution)/shard_map/all_to_all | solution.py:732
  121.6 8.6 %collective-permute-start.14 = (f32[4,4,2048]{2,1,0:T(4,128)}, f32[4,4,2048]{2,1,0:T(4,128)}, u32[]{:S(2)}, u32[]{:S(2)}) collective-permute-start(f32[4,4,2048]{2,1,0:T(4,128)} %copy-done.5), channel_id=1, source_target_pairs={{0,1},{1,2},{2,3},{3,4},{4,5},{5,6},{6,7},{7,8},{8,9},{9,10},{10,1... | collective-permute-start | bytes 393224 | tf_op jit(solution)/shard_map/ppermute | solution.py:712
  123.5 7.1 %collective-permute-start.15 = (f32[4,4,2048]{2,1,0:T(4,128)}, f32[4,4,2048]{2,1,0:T(4,128)}, u32[]{:S(2)}, u32[]{:S(2)}) collective-permute-start(f32[4,4,2048]{2,1,0:T(4,128)} %copy-done.4), channel_id=1, source_target_pairs={{1,0},{2,1},{3,2},{4,3},{5,4},{6,5},{7,6},{8,7},{9,8},{10,9},{11,1... | collective-permute-start | bytes 393224 | tf_op jit(solution)/shard_map/ppermute | solution.py:713
  130.6 1.4 copy-start
  132.0 0.9 copy-start.3
  144.4 17.6 %copy-start.7 = (f32[1,256]{1,0:T(1,128)S(1)}, f32[1,256]{1,0:T(1,128)}, u32[]{:S(2)}) copy-start(f32[1,256]{1,0:T(1,128)} %param.8) | copy-start | bytes 3076
  153.2 36.7 %all-to-all-start.3 = ((f32[32,8,8,128]{3,2,1,0:T(8,128)}), f32[32,8,8,128]{3,2,1,0:T(8,128)S(1)}, u32[]{:S(2)}, u32[]{:S(2)}) async-start(f32[32,8,8,128]{3,2,1,0:T(8,128)} %bitcast.9), calls=%async_computation.3 | async-start | bytes 2097152 | tf_op jit(solution)/shard_map/all_to_all | solution.py:732
  174.4 11.2 %collective-permute-start.6 = (f32[2,264,128]{2,1,0:T(8,128)S(1)}, f32[2,264,128]{2,1,0:T(8,128)S(1)}, u32[]{:S(2)}, u32[]{:S(2)}) collective-permute-start(f32[2,264,128]{2,1,0:T(8,128)S(1)} %get-tuple-element.41), channel_id=1, source_target_pairs={{0,3},{1,0},{2,1},{3,2},{4,7},{5,4},{6,5},{7,6},{8,11},{9,8},{10,9... | collective-permute-start | bytes 811016 | tf_op jit(solution)/shard_map/ppermute | solution.py:704
  180.0 21.5 %collective-permute-start.4 = (f32[2,264,128]{2,1,0:T(8,128)}, f32[2,264,128]{2,1,0:T(8,128)S(1)}, u32[]{:S(2)}, u32[]{:S(2)}) collective-permute-start(f32[2,264,128]{2,1,0:T(8,128)} %get-tuple-element.39), channel_id=1, source_target_pairs={{0,1},{1,2},{2,3},{3,0},{4,5},{5,6},{6,7},{7,4},{8,9},{9,10},{10,1... | collective-permute-start | bytes 811016 | tf_op jit(solution)/shard_map/ppermute | solution.py:704
  186.5 34.8 %collective-permute-start.7 = (f32[4,264,128]{2,1,0:T(8,128)}, f32[4,264,128]{2,1,0:T(8,128)S(1)}, u32[]{:S(2)}, u32[]{:S(2)}) collective-permute-start(f32[4,264,128]{2,1,0:T(8,128)} %pad_maximum_fusion.1), channel_id=1, source_target_pairs={{0,3},{1,0},{2,1},{3,2},{4,7},{5,4},{6,5},{7,6},{8,11},{9,8},{10,9... | collective-permute-start | bytes 1622024 | tf_op jit(solution)/shard_map/ppermute | solution.py:704
  201.4 6.7 %collective-permute-start.18 = (f32[2,264,128]{2,1,0:T(8,128)S(1)}, f32[2,264,128]{2,1,0:T(8,128)S(1)}, u32[]{:S(2)}, u32[]{:S(2)}) collective-permute-start(f32[2,264,128]{2,1,0:T(8,128)S(1)} %get-tuple-element.52), channel_id=1, source_target_pairs={{0,3},{1,0},{2,1},{3,2},{4,7},{5,4},{6,5},{7,6},{8,11},{9,8},{10,9... | collective-permute-start | bytes 811016 | tf_op jit(solution)/shard_map/ppermute | solution.py:704
  201.6 19.7 %collective-permute-start.5 = (f32[4,264,128]{2,1,0:T(8,128)S(1)}, f32[4,264,128]{2,1,0:T(8,128)S(1)}, u32[]{:S(2)}, u32[]{:S(2)}) collective-permute-start(f32[4,264,128]{2,1,0:T(8,128)S(1)} %pad_maximum_fusion), channel_id=1, source_target_pairs={{0,1},{1,2},{2,3},{3,0},{4,5},{5,6},{6,7},{7,4},{8,9},{9,10},{10,1... | collective-permute-start | bytes 1622024 | tf_op jit(solution)/shard_map/ppermute | solution.py:704
  203.1 18.0 %collective-permute-start.16 = (f32[2,264,128]{2,1,0:T(8,128)S(1)}, f32[2,264,128]{2,1,0:T(8,128)S(1)}, u32[]{:S(2)}, u32[]{:S(2)}) collective-permute-start(f32[2,264,128]{2,1,0:T(8,128)S(1)} %get-tuple-element.50), channel_id=1, source_target_pairs={{0,1},{1,2},{2,3},{3,0},{4,5},{5,6},{6,7},{7,4},{8,9},{9,10},{10,1... | collective-permute-start | bytes 811016 | tf_op jit(solution)/shard_map/ppermute | solution.py:704
  208.2 13.1 %collective-permute-start.19 = (f32[4,264,128]{2,1,0:T(8,128)S(1)}, f32[4,264,128]{2,1,0:T(8,128)S(1)}, u32[]{:S(2)}, u32[]{:S(2)}) collective-permute-start(f32[4,264,128]{2,1,0:T(8,128)S(1)} %pad_maximum_fusion.3), channel_id=1, source_target_pairs={{0,3},{1,0},{2,1},{3,2},{4,7},{5,4},{6,5},{7,6},{8,11},{9,8},{10,9... | collective-permute-start | bytes 1622024 | tf_op jit(solution)/shard_map/ppermute | solution.py:704
  221.2 12.9 %collective-permute-start.17 = (f32[4,264,128]{2,1,0:T(8,128)S(1)}, f32[4,264,128]{2,1,0:T(8,128)S(1)}, u32[]{:S(2)}, u32[]{:S(2)}) collective-permute-start(f32[4,264,128]{2,1,0:T(8,128)S(1)} %pad_maximum_fusion.2), channel_id=1, source_target_pairs={{0,1},{1,2},{2,3},{3,0},{4,5},{5,6},{6,7},{7,4},{8,9},{9,10},{10,1... | collective-permute-start | bytes 1622024 | tf_op jit(solution)/shard_map/ppermute | solution.py:704

commit v3 on v2

--- a/solution.py
+++ b/solution.py
@@ -1,3 +1,4 @@
+import functools
 import math
 
 import jax
@@ -77,7 +78,7 @@
     out, rows, cols, leg_hi, leg_lo, sem,
 ):
     tables = (hi_hbm, lo_hbm, leg_hi, leg_lo, sem)
-    start_tables(*tables)
+    start_tables(AHEAD, *tables)
 
     def body(step, carry):
         legendre_group(
@@ -104,7 +105,7 @@
     put(2, jnp.where(step < 2, far_a[jnp.minimum(step, 1)], far_b[jnp.maximum(step - 2, 0)]))
     cols[...] = rows[...].T
     for q in range(4):
-        next_tables(4 * step + q, *tables)
+        next_tables(4 * step + q, AHEAD, SLOTS, *tables)
     sums = []
     for q in range(4):
         lo_order = pairs[4 * step + q]
@@ -227,19 +228,19 @@
     )
 
 
-def start_tables(*refs):
-    for n in range(AHEAD):
+def start_tables(count, *refs):
+    for n in range(count):
         for copy in slot_tables(n, *refs):
             copy.start()
 
 
-def next_tables(n, *refs):
+def next_tables(n, ahead, end, *refs):
     for copy in slot_tables(n, *refs):
         copy.wait()
 
-    @pl.when(n + AHEAD < SLOTS)
+    @pl.when(n + ahead < end)
     def _():
-        for copy in slot_tables(n + AHEAD, *refs):
+        for copy in slot_tables(n + ahead, *refs):
             copy.start()
 
 
@@ -596,23 +597,24 @@
 
 
 def tendency_kernel(
-    pairs, place, recv, weight, hi_hbm, lo_hbm,
-    own, ahead, far_a, far_b, behind, res, leg_hi, leg_lo, sem,
+    half, pairs, place, recv, weight, hi_hbm, lo_hbm,
+    own, ahead, far, behind, res, leg_hi, leg_lo, sem,
 ):
-    tables = (hi_hbm, lo_hbm, leg_hi, leg_lo, sem)
-    start_tables(*tables)
+    slots = pl.ds(half * (SLOTS // 2), SLOTS // 2)
+    tables = (hi_hbm.at[slots], lo_hbm.at[slots], leg_hi, leg_lo, sem)
+    start_tables(4, *tables)
 
     def body(step, carry):
         tendency_group(
-            step, pairs, place, recv, weight, tables, own, ahead, far_a, far_b, behind, res
+            half, step, pairs, place, recv, weight, tables, own, ahead, far, behind, res
         )
         return carry
 
-    lax.fori_loop(0, 4, body, 0)
+    lax.fori_loop(0, 2, body, 0)
 
 
 def tendency_group(
-    step, pairs, place, recv, weight, tables, own, ahead, far_a, far_b, behind, res
+    half, step, pairs, place, recv, weight, tables, own, ahead, far, behind, res
 ):
     _, _, leg_hi, leg_lo, _ = tables
     d = place[0]
@@ -620,8 +622,8 @@
     rhs = []
     bound = jnp.zeros((1, 128), jnp.int32)
     for b in range(4):
-        lo_order = pairs[4 * step + b]
-        f = recv[:, 2 * step + b // 2].reshape(QLAT, 128) * weight[...]
+        lo_order = pairs[8 * half + 4 * step + b]
+        f = recv[:, 4 * half + 2 * step + b // 2].reshape(QLAT, 128) * weight[...]
         even = pltpu.roll(f, (32 * b - 64 * (b % 2)) % 128, 1)
         odd = pltpu.roll(f, (32 * b - 64 * (b % 2) - 32) % 128, 1)
         here = lane // 32 == b
@@ -632,7 +634,7 @@
         bound = jnp.where(here, M - lo_order, bound)
     rhs = jnp.concatenate([x for hi, lo in rhs for x in (hi, lo, hi)], axis=0)
     for b in range(4):
-        next_tables(4 * step + b, *tables)
+        next_tables(4 * step + b, 4, SLOTS // 2, *tables)
     for part in range(2):
         rows = slice(PART_ROWS * part, PART_ROWS * (part + 1))
         lhs = []
@@ -650,36 +652,31 @@
 
     own[step] = get(0)
     ahead[step] = get(1)
+    far[step] = get(2)
     behind[step] = get(3)
 
-    @pl.when(step < 2)
-    def _():
-        far_a[step] = get(2)
-
-    @pl.when(step >= 2)
-    def _():
-        far_b[step - 2] = get(2)
-
-
-def tendency_sums(pairs, place, recv, weight, leg_hi, leg_lo):
-    full = jax.ShapeDtypeStruct((4, ROWS, 128), F32)
+
+def tendency_sums(half, pairs, place, recv, weight, leg_hi, leg_lo):
     part = jax.ShapeDtypeStruct((2, ROWS, 128), F32)
     return pl.pallas_call(
-        tendency_kernel,
+        functools.partial(tendency_kernel, half),
         in_specs=[SCALARS] * 2 + [ON_CHIP] * 2 + [ANY] * 2,
-        out_specs=(ON_CHIP,) * 5,
-        out_shape=(full, full, part, part, full),
+        out_specs=(ON_CHIP,) * 4,
+        out_shape=(part,) * 4,
         scratch_shapes=[pltpu.VMEM((ALL_ROWS, 128), F32)] + LEG_SCRATCH,
         compiler_params=params(),
-        cost_estimate=cost(10),
+        cost_estimate=cost(6),
         name="tendency_sums",
     )(pairs, place, recv, weight, in_hbm(leg_hi), in_hbm(leg_lo))
 
 
-def unpack_kernel(a0, a1, a2, b0, b1, b2, out, scr):
-    for ch, refs in ((0, (a0, a1, a2)), (1, (b0, b1, b2))):
+def unpack_kernel(*refs):
+    *pieces, out, scr = refs
+    for ch in range(2):
         for g in range(4):
-            scr[0:ROWS, :] = refs[0][g] + refs[1][g] + refs[2][g]
+            first = 6 * ch + 3 * (g // 2)
+            own, ahead, behind = pieces[first : first + 3]
+            scr[0:ROWS, :] = own[g % 2] + ahead[g % 2] + behind[g % 2]
             value = scr[...].T
             for s in range(4):
                 for p in range(2):
@@ -720,12 +717,18 @@
     return right, left, shift(right[0:2], "pb", 1), shift(left[2:4], "pb", -1)
 
 
-def scatter_rows(own, ahead, far_a, far_b, behind):
-    via_a = shift(far_a, "pb", 1)
-    via_b = shift(far_b, "pb", -1)
-    ahead = jnp.concatenate([ahead[0:2] + via_a, ahead[2:4]], axis=0)
-    behind = jnp.concatenate([behind[0:2], behind[2:4] + via_b], axis=0)
-    return own, shift(ahead, "pb", 1), shift(behind, "pb", -1)
+def scatter_rows(recv, *args):
+    own_0, ahead_0, far_0, behind_0 = tendency_sums(0, *args[:2], recv, *args[2:])
+    via_0 = shift(far_0, "pb", 1)
+    behind_0 = shift(behind_0, "pb", -1)
+    own_1, ahead_1, far_1, behind_1 = tendency_sums(1, *args[:2], recv, *args[2:])
+    via_1 = shift(far_1, "pb", -1)
+    ahead_1 = shift(ahead_1, "pb", 1)
+    ahead_0 = ahead_0 + via_0
+    ahead_0 = shift(ahead_0, "pb", 1)
+    behind_1 = behind_1 + via_1
+    behind_1 = shift(behind_1, "pb", -1)
+    return own_0, ahead_0, behind_0, own_1, ahead_1, behind_1
 
 
 def exchange(x):
@@ -762,10 +765,8 @@
     )
     back_b = moist_stage(sent_b.reshape(QLAT, 8, 128), t_hi, t_lo, speed, heat)
     back_b = exchange(back_b.reshape(32, 8, 8, 128))
-    sums_a = tendency_sums(pairs, place, back_a, weight, leg_hi, leg_lo)
-    sums_a = scatter_rows(*sums_a)
-    sums_b = tendency_sums(pairs, place, back_b, weight, leg_hi, leg_lo)
-    sums_b = scatter_rows(*sums_b)
+    sums_a = scatter_rows(back_a, pairs, place, weight, leg_hi, leg_lo)
+    sums_b = scatter_rows(back_b, pairs, place, weight, leg_hi, leg_lo)
     summed = unpack((*sums_a, *sums_b))
     return (jnp.transpose(summed, (0, 2, 1)), new_tracers)
 

time: 239 us -> 237 us (level)
  waiting for transfers between devices: 54 us -> 43.1 us
  Pallas kernels: 92.7 us -> 98.6 us
    ppermute x16 -> x20, waiting for transfers between devices: 52.1 us -> 41.2 us  [shift(): return lax.ppermute(x, axis, [(i, (i + by) % n) for i in range(n)])]
    pallas_call x2 -> x4, Pallas kernels: 23.7 us -> 29.5 us  [tendency_sums(): pl.pallas_call(functools.partial(tendency_kernel, half), in_specs=[SCALAR...]
    ppermute x16 -> x20, starting transfers between devices: 24.3 us -> 26 us  [shift(): return lax.ppermute(x, axis, [(i, (i + by) % n) for i in range(n)])]
    unnamed x19 -> x27, local copies, waits for them, and re-layouts: 5.85 us -> 7.22 us
  transfers between devices with their start and end apart: 24 -> 28, of which waited for: 8 -> 9; matrix products, arithmetic and copies ran while one was open for 3% -> 4% of each run, Pallas kernels for 38% -> 41%
where the time goes in v3:
time: 237 us; the launch traced here: 235 us
  Pallas kernels  98.6 us (42%)
  starting transfers between devices  76.2 us (32%)
  waiting for transfers between devices  43.1 us (18%)
  local copies, waits for them, and re-layouts  13.6 us (6%)
    ppermute x20, waiting for transfers between devices, shift(): return lax.ppermute(x, axis, [(i, (i + by) % n) for i in range(n)])  41.2 us
    all_to_all x4, starting transfers between devices, exchange(): return lax.all_to_all(x, 'ma', 0, 0, tiled=True)  36.3 us
    pallas_call x4, Pallas kernels, tendency_sums(): pl.pallas_call(functools.partial(tendency_kernel, half), in_specs=[SCALAR...  29.5 us
    ppermute x20, starting transfers between devices, shift(): return lax.ppermute(x, axis, [(i, (i + by) % n) for i in range(n)])  26 us
    pallas_call x2, Pallas kernels, legendre_sums(): pl.pallas_call(legendre_kernel, in_specs=[SCALARS] * 2 + [ON_CHIP] * 5 +...  17.9 us
    pallas_call x1, Pallas kernels, prepare(): pl.pallas_call(prepare_kernel, in_specs=[ANY], out_specs=(ANY, ANY), out_...  12.6 us
    pallas_call x1, Pallas kernels, transport(): pl.pallas_call(advect_kernel, grid_spec=pltpu.PrefetchScalarGridSpec(num_...  11.4 us
    ppermute x2, starting transfers between devices, neighbours(): lax.ppermute(first, axes, [(b, a) for a, b in down])  10.1 us
  transfers between devices with their start and end apart: 28, of which 9 were waited for; matrix products, arithmetic and copies ran while one was open for 4% of the time, Pallas kernels for 41%

profile of v3, /device:TPU:1, one launch (start us, length us, event | category | flops | bytes accessed | tf_op | source)
XLA Modules:
  0.0 234.8 jit_solution(17957449158152565551)
XLA Ops:
  0.6 1.4 copy-done.1
  2.0 1.3 pack.1
  3.3 2.0 collective-permute-start
  5.4 1.3 collective-permute-start.1
  6.6 11.6 %collective-permute-done.right = f32[4,264,128]{2,1,0:T(8,128)S(1)} collective-permute-done((f32[4,264,128]{2,1,0:T(8,128)S(1)}, f32[4,264,128]{2,1,0:T(8,128)S(1)}, u32[]{:S(2)}, u32[]{:S(2)}) %collective-permute-start) | collective-permute-done | bytes 540704 | tf_op jit(solution)/shard_map/ppermute | solution.py:701
  18.2 0.7 slice.24
  19.2 0.7 slice.25
  20.0 2.4 %collective-permute-start.3 = (f32[2,264,128]{2,1,0:T(8,128)}, f32[2,264,128]{2,1,0:T(8,128)S(1)}, u32[]{:S(2)}, u32[]{:S(2)}) collective-permute-start(f32[2,264,128]{2,1,0:T(8,128)} %slice.25), channel_id=1, source_target_pairs={{0,3},{1,0},{2,1},{3,2},{4,7},{5,4},{6,5},{7,6},{8,11},{9,8},{10,9... | collective-permute-start | bytes 811016 | tf_op jit(solution)/shard_map/ppermute | solution.py:701
  22.4 0.8 dynamic_slice.3.pairs
  23.1 12.6 %prepare.1 = (bf16[16,1056,256]{2,1,0:T(8,128)(2,1)}, bf16[16,1056,256]{2,1,0:T(8,128)(2,1)}) custom-call(f32[16,2112,128]{2,1,0:T(8,128)} %bitcast.15), custom_call_target="tpu_custom_call" | custom-call | flops 2750000128 | bytes 1048576 | tf_op jit(solution)/shard_map/prepare/pallas_call | solution.py:192
  35.8 2.7 %collective-permute-start.11 = (f32[4,264,128]{2,1,0:T(8,128)}, f32[4,264,128]{2,1,0:T(8,128)S(1)}, u32[]{:S(2)}, u32[]{:S(2)}) collective-permute-start(f32[4,264,128]{2,1,0:T(8,128)} %get-tuple-element.51.own), channel_id=1, source_target_pairs={{0,3},{1,0},{2,1},{3,2},{4,7},{5,4},{6,5},{7,6},{8,11},{9,8},{10,9... | collective-permute-start | bytes 1622024 | tf_op jit(solution)/shard_map/ppermute | solution.py:701
  38.4 8.7 %legendre_sums.2 = f32[32,8,8,128]{3,2,1,0:T(8,128)} custom-call(s32[16]{0:T(128)S(1)} %dynamic_slice.3.pairs, s32[1]{0:T(128)} %bitcast.place, f32[4,264,128]{2,1,0:T(8,128)S(1)} %get-tuple-element.34.own, f32[4,264,128]{2,1,0:T(8,128)S(1)} %collective-permute-done.right, f32[4,264,128]{2,1,0:T(8,128)S(1)} %collective-permute-done.1.left, ...), custom_call_target="tpu_custom_call" | custom-call | flops 2500000000 | bytes 1048576 | tf_op jit(solution)/shard_map/legendre_sums/pallas_call | solution.py:248
  47.1 11.0 %all-to-all-start = ((f32[32,8,8,128]{3,2,1,0:T(8,128)}), f32[32,8,8,128]{3,2,1,0:T(8,128)S(1)}, u32[]{:S(2)}, u32[]{:S(2)}) async-start(f32[32,8,8,128]{3,2,1,0:T(8,128)} %legendre_sums.2), calls=%async_computation | async-start | bytes 2097152 | tf_op jit(solution)/shard_map/all_to_all | solution.py:735
  58.3 2.7 %collective-permute-start.13 = (f32[2,264,128]{2,1,0:T(8,128)S(1)}, f32[2,264,128]{2,1,0:T(8,128)S(1)}, u32[]{:S(2)}, u32[]{:S(2)}) collective-permute-start(f32[2,264,128]{2,1,0:T(8,128)S(1)} %slice.27), channel_id=1, source_target_pairs={{0,3},{1,0},{2,1},{3,2},{4,7},{5,4},{6,5},{7,6},{8,11},{9,8},{10,9... | collective-permute-start | bytes 811016 | tf_op jit(solution)/shard_map/ppermute | solution.py:701
  61.1 6.2 %collective-permute-done.12.far_a = f32[2,264,128]{2,1,0:T(8,128)S(1)} collective-permute-done((f32[2,264,128]{2,1,0:T(8,128)S(1)}, f32[2,264,128]{2,1,0:T(8,128)S(1)}, u32[]{:S(2)}, u32[]{:S(2)}) %collective-permute-start.12) | collective-permute-done | bytes 270368 | tf_op jit(solution)/shard_map/ppermute | solution.py:701
  67.3 9.2 %legendre_sums.3 = f32[32,8,8,128]{3,2,1,0:T(8,128)} custom-call(s32[16]{0:T(128)S(1)} %dynamic_slice.3.pairs, s32[1]{0:T(128)} %bitcast.place, f32[4,264,128]{2,1,0:T(8,128)} %get-tuple-element.51.own, f32[4,264,128]{2,1,0:T(8,128)S(1)} %collective-permute-done.10.right, f32[4,264,128]{2,1,0:T(8,128)S(1)} %collective-permute-done.11.left, ...), custom_call_target="tpu_custom_call" | custom-call | flops 2500000000 | bytes 1048576 | tf_op jit(solution)/shard_map/legendre_sums/pallas_call | solution.py:248
  76.5 8.1 %all-to-all-start.2 = ((f32[32,8,8,128]{3,2,1,0:T(8,128)}), f32[32,8,8,128]{3,2,1,0:T(8,128)S(1)}, u32[]{:S(2)}, u32[]{:S(2)}) async-start(f32[32,8,8,128]{3,2,1,0:T(8,128)} %legendre_sums.3), calls=%async_computation.2 | async-start | bytes 2097152 | tf_op jit(solution)/shard_map/all_to_all | solution.py:735
  84.7 3.4 %fusion.2 = (f32[12,2,4,2048]{3,2,1,0:T(4,128)}, f32[12,2,4,2048]{3,2,1,0:T(4,128)}) fusion(f32[12,2,8,2048]{3,2,1,0:T(8,128)} %tracer.1), kind=kLoop, calls=%fused_computation.8 | loop fusion | bytes 3145728 | tf_op jit(solution)/shard_map/slice | solution.py:756
  88.1 1.9 collective-permute-start.14
  90.0 5.0 %collective-permute-start.15 = (f32[12,2,4,2048]{3,2,1,0:T(4,128)}, f32[12,2,4,2048]{3,2,1,0:T(4,128)}, u32[]{:S(2)}, u32[]{:S(2)}) collective-permute-start(f32[12,2,4,2048]{3,2,1,0:T(4,128)} %get-tuple-element.66), channel_id=1, source_target_pairs={{1,0},{2,1},{3,2},{4,3},{5,4},{6,5},{7,6},{8,7},{9,8},{10,9},{11,1... | collective-permute-start | bytes 2359304 | tf_op jit(solution)/shard_map/ppermute | solution.py:710
  95.8 6.5 %tables.1 = (bf16[8,256,1024]{2,1,0:T(8,128)(2,1)}, bf16[8,256,1024]{2,1,0:T(8,128)(2,1)}) custom-call(s32[4,256,128]{2,1,0:T(8,128)S(1)} %broadcast_in_dim.15.orders), custom_call_target="tpu_custom_call" | custom-call | flops 1250000000 | bytes 1048576 | tf_op jit(solution)/shard_map/tables/pallas_call | solution.py:320
  102.3 9.0 %wind_stage.1 = (f32[256,8,128]{2,1,0:T(8,128)}, f32[4,8,2048]{2,1,0:T(8,128)S(1)}, f32[4,4,2048]{2,1,0:T(4,128)S(1)}, f32[4,4,2048]{2,1,0:T(4,128)S(1)}, f32[64,2048]{1,0:T(8,128)S(1)}) custom-call(f32[256,8,128]{2,1,0:T(8,128)S(1)} %bitcast.12, bf16[8,256,1024]{2,1,0:T(8,128)(2,1)} %get-tuple-element.40.hi_hbm, bf16[8,256,1024]{2,1,0:T(8,128)(2,1)} %get-tuple-element.41.lo_hbm), custom_call_target="tpu_custom_call" | custom-call | flops 2500000000 | bytes 1048576 | tf_op jit(solution)/shard_map/wind_stage/pallas_call | solution.py:455
  113.3 8.3 %all-to-all-start.1 = ((f32[32,8,8,128]{3,2,1,0:T(8,128)}), f32[32,8,8,128]{3,2,1,0:T(8,128)S(1)}, u32[]{:S(2)}, u32[]{:S(2)}) async-start(f32[32,8,8,128]{3,2,1,0:T(8,128)} %bitcast.5), calls=%async_computation.1 | async-start | bytes 2097152 | tf_op jit(solution)/shard_map/all_to_all | solution.py:735
  121.6 1.9 collective-permute-start.16
  123.5 5.1 %collective-permute-start.17 = (f32[4,4,2048]{2,1,0:T(4,128)}, f32[4,4,2048]{2,1,0:T(4,128)}, u32[]{:S(2)}, u32[]{:S(2)}) collective-permute-start(f32[4,4,2048]{2,1,0:T(4,128)} %copy-done.8), channel_id=1, source_target_pairs={{1,0},{2,1},{3,2},{4,3},{5,4},{6,5},{7,6},{8,7},{9,8},{10,9},{11,1... | collective-permute-start | bytes 393224 | tf_op jit(solution)/shard_map/ppermute | solution.py:710
  128.7 1.5 collective-permute-done.16.wind_above
  130.6 1.4 copy-done
  132.0 0.9 copy-done.7
  133.0 11.4 %transport.1 = (f32[12,2,8,2048]{3,2,1,0:T(8,128)}, f32[16,64,128]{2,1,0:T(8,128)S(1)}) custom-call(f32[12,2]{1,0:T(8,128)S(1)} %copy.14.rate, s32[1]{0:T(128)} %bitcast.8.band, f32[12,2,8,2048]{3,2,1,0:T(8,128)S(1)} %copy-done, f32[12,2,4,2048]{3,2,1,0:T(4,128)S(1)} %collective-permute-done.14.above, f32[12,2,4,2048]{3,2,1,0:T(4,128)} %collective-permute-done.15.below, ...), custom_call_target="tpu_custom_call" | custom-call | flops 2500000000 | bytes 1048576 | tf_op jit(solution)/shard_map/transport/pallas_call | solution.py:574
  144.4 8.8 %moist_stage.1 = f32[256,8,128]{2,1,0:T(8,128)} custom-call(f32[256,8,128]{2,1,0:T(8,128)S(1)} %bitcast.13, bf16[8,256,1024]{2,1,0:T(8,128)(2,1)} %get-tuple-element.40.hi_hbm, bf16[8,256,1024]{2,1,0:T(8,128)(2,1)} %get-tuple-element.41.lo_hbm, f32[64,2048]{1,0:T(8,128)S(1)} %get-tuple-element.52.speed_ref, f32[16,64,128]{2,1,0:T(8,128)S(1)} %get-tuple-element.56.heat_ref), custom_call_target="tpu_custom_call" | custom-call | flops 2500000000 | bytes 1048576 | tf_op jit(solution)/shard_map/moist_stage/pallas_call | solution.py:473
  153.2 8.9 %all-to-all-start.3 = ((f32[32,8,8,128]{3,2,1,0:T(8,128)}), f32[32,8,8,128]{3,2,1,0:T(8,128)S(1)}, u32[]{:S(2)}, u32[]{:S(2)}) async-start(f32[32,8,8,128]{3,2,1,0:T(8,128)} %bitcast.9), calls=%async_computation.3 | async-start | bytes 2097152 | tf_op jit(solution)/shard_map/all_to_all | solution.py:735
  162.1 7.7 %tendency_sums.5 = (f32[2,264,128]{2,1,0:T(8,128)S(1)}, f32[2,264,128]{2,1,0:T(8,128)S(1)}, f32[2,264,128]{2,1,0:T(8,128)}, f32[2,264,128]{2,1,0:T(8,128)S(1)}) custom-call(s32[16]{0:T(128)S(1)} %dynamic_slice.3.pairs, s32[1]{0:T(128)} %bitcast.place, f32[32,8,8,128]{3,2,1,0:T(8,128)S(1)} %all-to-all-done.1.recv, f32[256,128]{1,0:T(8,128)S(1)} %broadcast_in_dim.17.weight, ...), custom_call_target="tpu_custom_call" | custom-call | flops 1500000000 | bytes 1048576 | tf_op jit(solution)/shard_map/tendency_sums/pallas_call | solution.py:661
  170.6 5.6 %collective-permute-start.8 = (f32[2,264,128]{2,1,0:T(8,128)}, f32[2,264,128]{2,1,0:T(8,128)}, u32[]{:S(2)}, u32[]{:S(2)}) collective-permute-start(f32[2,264,128]{2,1,0:T(8,128)} %get-tuple-element.50), channel_id=1, source_target_pairs={{0,3},{1,0},{2,1},{3,2},{4,7},{5,4},{6,5},{7,6},{8,11},{9,8},{10,9... | collective-permute-start | bytes 811016 | tf_op jit(solution)/shard_map/ppermute | solution.py:701
  176.2 7.7 %tendency_sums.4 = (f32[2,264,128]{2,1,0:T(8,128)S(1)}, f32[2,264,128]{2,1,0:T(8,128)S(1)}, f32[2,264,128]{2,1,0:T(8,128)}, f32[2,264,128]{2,1,0:T(8,128)S(1)}) custom-call(s32[16]{0:T(128)S(1)} %dynamic_slice.3.pairs, s32[1]{0:T(128)} %bitcast.place, f32[32,8,8,128]{3,2,1,0:T(8,128)S(1)} %all-to-all-done.1.recv, f32[256,128]{1,0:T(8,128)S(1)} %broadcast_in_dim.17.weight, ...), custom_call_target="tpu_custom_call" | custom-call | flops 1500000000 | bytes 1048576 | tf_op jit(solution)/shard_map/tendency_sums/pallas_call | solution.py:661
  184.6 7.0 %tendency_sums.7 = (f32[2,264,128]{2,1,0:T(8,128)S(1)}, f32[2,264,128]{2,1,0:T(8,128)S(1)}, f32[2,264,128]{2,1,0:T(8,128)S(1)}, f32[2,264,128]{2,1,0:T(8,128)S(1)}) custom-call(s32[16]{0:T(128)S(1)} %dynamic_slice.3.pairs, s32[1]{0:T(128)} %bitcast.place, f32[32,8,8,128]{3,2,1,0:T(8,128)S(1)} %all-to-all-done.3.recv, ...), custom_call_target="tpu_custom_call" | custom-call | flops 1500000000 | bytes 1048576 | tf_op jit(solution)/shard_map/tendency_sums/pallas_call | solution.py:661
  191.7 3.0 %collective-permute-start.22 = (f32[2,264,128]{2,1,0:T(8,128)S(1)}, f32[2,264,128]{2,1,0:T(8,128)S(1)}, u32[]{:S(2)}, u32[]{:S(2)}) collective-permute-start(f32[2,264,128]{2,1,0:T(8,128)S(1)} %get-tuple-element.64), channel_id=1, source_target_pairs={{0,3},{1,0},{2,1},{3,2},{4,7},{5,4},{6,5},{7,6},{8,11},{9,8},{10,9... | collective-permute-start | bytes 811016 | tf_op jit(solution)/shard_map/ppermute | solution.py:701
  194.7 7.0 %tendency_sums.6 = (f32[2,264,128]{2,1,0:T(8,128)S(1)}, f32[2,264,128]{2,1,0:T(8,128)S(1)}, f32[2,264,128]{2,1,0:T(8,128)S(1)}, f32[2,264,128]{2,1,0:T(8,128)S(1)}) custom-call(s32[16]{0:T(128)S(1)} %dynamic_slice.3.pairs, s32[1]{0:T(128)} %bitcast.place, f32[32,8,8,128]{3,2,1,0:T(8,128)S(1)} %all-to-all-done.3.recv, ...), custom_call_target="tpu_custom_call" | custom-call | flops 1500000000 | bytes 1048576 | tf_op jit(solution)/shard_map/tendency_sums/pallas_call | solution.py:661
  201.9 2.6 %collective-permute-start.6 = (f32[2,264,128]{2,1,0:T(8,128)S(1)}, f32[2,264,128]{2,1,0:T(8,128)S(1)}, u32[]{:S(2)}, u32[]{:S(2)}) collective-permute-start(f32[2,264,128]{2,1,0:T(8,128)S(1)} %copy-done.5), channel_id=1, source_target_pairs={{0,3},{1,0},{2,1},{3,2},{4,7},{5,4},{6,5},{7,6},{8,11},{9,8},{10,9... | collective-permute-start | bytes 811016 | tf_op jit(solution)/shard_map/ppermute | solution.py:701
  204.5 1.0 add.27
  205.5 1.4 collective-permute-start.9
  207.0 1.0 add.26
  208.2 1.8 collective-permute-done.18
  210.0 5.8 %collective-permute-done.7.refs_4_ = f32[2,264,128]{2,1,0:T(8,128)S(1)} collective-permute-done((f32[2,264,128]{2,1,0:T(8,128)S(1)}, f32[2,264,128]{2,1,0:T(8,128)S(1)}, u32[]{:S(2)}, u32[]{:S(2)}) %collective-permute-start.7) | collective-permute-done | bytes 270368 | tf_op jit(solution)/shard_map/ppermute | solution.py:701
  215.8 1.5 collective-permute-start.19
  217.3 4.2 %collective-permute-done.5.refs_1_ = f32[2,264,128]{2,1,0:T(8,128)S(1)} collective-permute-done((f32[2,264,128]{2,1,0:T(8,128)S(1)}, f32[2,264,128]{2,1,0:T(8,128)S(1)}, u32[]{:S(2)}, u32[]{:S(2)}) %collective-permute-start.5) | collective-permute-done | bytes 270368 | tf_op jit(solution)/shard_map/ppermute | solution.py:701
  221.5 5.8 %collective-permute-done.21.refs_10_ = f32[2,264,128]{2,1,0:T(8,128)S(1)} collective-permute-done((f32[2,264,128]{2,1,0:T(8,128)S(1)}, f32[2,264,128]{2,1,0:T(8,128)S(1)}, u32[]{:S(2)}, u32[]{:S(2)}) %collective-permute-start.21) | collective-permute-done | bytes 270368 | tf_op jit(solution)/shard_map/ppermute | solution.py:701
  227.3 5.8 %collective-permute-done.19.refs_7_ = f32[2,264,128]{2,1,0:T(8,128)S(1)} collective-permute-done((f32[2,264,128]{2,1,0:T(8,128)S(1)}, f32[2,264,128]{2,1,0:T(8,128)S(1)}, u32[]{:S(2)}, u32[]{:S(2)}) %collective-permute-start.19) | collective-permute-done | bytes 270368 | tf_op jit(solution)/shard_map/ppermute | solution.py:701
  233.1 1.7 unpack.1
  (67 shorter events, 5.5 us)
Async XLA Ops:
  0.6 1.4 copy-start.1
  3.3 14.9 %collective-permute-start = (f32[4,264,128]{2,1,0:T(8,128)S(1)}, f32[4,264,128]{2,1,0:T(8,128)S(1)}, u32[]{:S(2)}, u32[]{:S(2)}) collective-permute-start(f32[4,264,128]{2,1,0:T(8,128)S(1)} %get-tuple-element.34.own), channel_id=1, source_target_pairs={{0,1},{1,2},{2,3},{3,0},{4,5},{5,6},{6,7},{7,4},{8,9},{9,10},{10,1... | collective-permute-start | bytes 1622024 | tf_op jit(solution)/shard_map/ppermute | solution.py:701
  5.4 13.9 %collective-permute-start.1 = (f32[4,264,128]{2,1,0:T(8,128)S(1)}, f32[4,264,128]{2,1,0:T(8,128)S(1)}, u32[]{:S(2)}, u32[]{:S(2)}) collective-permute-start(f32[4,264,128]{2,1,0:T(8,128)S(1)} %get-tuple-element.34.own), channel_id=1, source_target_pairs={{0,3},{1,0},{2,1},{3,2},{4,7},{5,4},{6,5},{7,6},{8,11},{9,8},{10,9... | collective-permute-start | bytes 1622024 | tf_op jit(solution)/shard_map/ppermute | solution.py:701
  19.0 19.5 %collective-permute-start.2 = (f32[2,264,128]{2,1,0:T(8,128)}, f32[2,264,128]{2,1,0:T(8,128)S(1)}, u32[]{:S(2)}, u32[]{:S(2)}) collective-permute-start(f32[2,264,128]{2,1,0:T(8,128)} %slice.24), channel_id=1, source_target_pairs={{0,1},{1,2},{2,3},{3,0},{4,5},{5,6},{6,7},{7,4},{8,9},{9,10},{10,1... | collective-permute-start | bytes 811016 | tf_op jit(solution)/shard_map/ppermute | solution.py:701
  20.0 18.5 %collective-permute-start.3 = (f32[2,264,128]{2,1,0:T(8,128)}, f32[2,264,128]{2,1,0:T(8,128)S(1)}, u32[]{:S(2)}, u32[]{:S(2)}) collective-permute-start(f32[2,264,128]{2,1,0:T(8,128)} %slice.25), channel_id=1, source_target_pairs={{0,3},{1,0},{2,1},{3,2},{4,7},{5,4},{6,5},{7,6},{8,11},{9,8},{10,9... | collective-permute-start | bytes 811016 | tf_op jit(solution)/shard_map/ppermute | solution.py:701
  35.7 22.5 %collective-permute-start.10 = (f32[4,264,128]{2,1,0:T(8,128)}, f32[4,264,128]{2,1,0:T(8,128)S(1)}, u32[]{:S(2)}, u32[]{:S(2)}) collective-permute-start(f32[4,264,128]{2,1,0:T(8,128)} %get-tuple-element.51.own), channel_id=1, source_target_pairs={{0,1},{1,2},{2,3},{3,0},{4,5},{5,6},{6,7},{7,4},{8,9},{9,10},{10,1... | collective-permute-start | bytes 1622024 | tf_op jit(solution)/shard_map/ppermute | solution.py:701
  35.8 22.5 %collective-permute-start.11 = (f32[4,264,128]{2,1,0:T(8,128)}, f32[4,264,128]{2,1,0:T(8,128)S(1)}, u32[]{:S(2)}, u32[]{:S(2)}) collective-permute-start(f32[4,264,128]{2,1,0:T(8,128)} %get-tuple-element.51.own), channel_id=1, source_target_pairs={{0,3},{1,0},{2,1},{3,2},{4,7},{5,4},{6,5},{7,6},{8,11},{9,8},{10,9... | collective-permute-start | bytes 1622024 | tf_op jit(solution)/shard_map/ppermute | solution.py:701
  47.1 29.4 %all-to-all-start = ((f32[32,8,8,128]{3,2,1,0:T(8,128)}), f32[32,8,8,128]{3,2,1,0:T(8,128)S(1)}, u32[]{:S(2)}, u32[]{:S(2)}) async-start(f32[32,8,8,128]{3,2,1,0:T(8,128)} %legendre_sums.2), calls=%async_computation | async-start | bytes 2097152 | tf_op jit(solution)/shard_map/all_to_all | solution.py:735
  58.2 9.1 %collective-permute-start.12 = (f32[2,264,128]{2,1,0:T(8,128)S(1)}, f32[2,264,128]{2,1,0:T(8,128)S(1)}, u32[]{:S(2)}, u32[]{:S(2)}) collective-permute-start(f32[2,264,128]{2,1,0:T(8,128)S(1)} %slice.26), channel_id=1, source_target_pairs={{0,1},{1,2},{2,3},{3,0},{4,5},{5,6},{6,7},{7,4},{8,9},{9,10},{10,1... | collective-permute-start | bytes 811016 | tf_op jit(solution)/shard_map/ppermute | solution.py:701
  58.3 9.0 %collective-permute-start.13 = (f32[2,264,128]{2,1,0:T(8,128)S(1)}, f32[2,264,128]{2,1,0:T(8,128)S(1)}, u32[]{:S(2)}, u32[]{:S(2)}) collective-permute-start(f32[2,264,128]{2,1,0:T(8,128)S(1)} %slice.27), channel_id=1, source_target_pairs={{0,3},{1,0},{2,1},{3,2},{4,7},{5,4},{6,5},{7,6},{8,11},{9,8},{10,9... | collective-permute-start | bytes 811016 | tf_op jit(solution)/shard_map/ppermute | solution.py:701
  76.5 18.5 %copy-start.10 = (s32[512]{0:T(512)S(1)}, s32[512]{0:T(512)}, u32[]{:S(2)}) copy-start(s32[512]{0:T(512)} %param.9) | copy-start | bytes 6148
  76.5 36.7 %all-to-all-start.2 = ((f32[32,8,8,128]{3,2,1,0:T(8,128)}), f32[32,8,8,128]{3,2,1,0:T(8,128)S(1)}, u32[]{:S(2)}, u32[]{:S(2)}) async-start(f32[32,8,8,128]{3,2,1,0:T(8,128)} %legendre_sums.3), calls=%async_computation.2 | async-start | bytes 2097152 | tf_op jit(solution)/shard_map/all_to_all | solution.py:735
  88.1 40.6 %collective-permute-start.14 = (f32[12,2,4,2048]{3,2,1,0:T(4,128)}, f32[12,2,4,2048]{3,2,1,0:T(4,128)S(1)}, u32[]{:S(2)}, u32[]{:S(2)}) collective-permute-start(f32[12,2,4,2048]{3,2,1,0:T(4,128)} %get-tuple-element.67), channel_id=1, source_target_pairs={{0,1},{1,2},{2,3},{3,4},{4,5},{5,6},{6,7},{7,8},{8,9},{9,10},{10,1... | collective-permute-start | bytes 2359304 | tf_op jit(solution)/shard_map/ppermute | solution.py:709
  90.0 38.7 %collective-permute-start.15 = (f32[12,2,4,2048]{3,2,1,0:T(4,128)}, f32[12,2,4,2048]{3,2,1,0:T(4,128)}, u32[]{:S(2)}, u32[]{:S(2)}) collective-permute-start(f32[12,2,4,2048]{3,2,1,0:T(4,128)} %get-tuple-element.66), channel_id=1, source_target_pairs={{1,0},{2,1},{3,2},{4,3},{5,4},{6,5},{7,6},{8,7},{9,8},{10,9},{11,1... | collective-permute-start | bytes 2359304 | tf_op jit(solution)/shard_map/ppermute | solution.py:710
  102.3 26.3 %copy-start.12 = (f32[12,2]{0,1:T(2,128)S(1)}, f32[12,2]{0,1:T(2,128)}, u32[]{:S(2)}) copy-start(f32[12,2]{0,1:T(2,128)} %param.11) | copy-start | bytes 292
  111.3 0.7 copy-start.6
  112.0 0.6 copy-start.8
  112.6 0.6 copy-start.9
  113.3 39.9 %all-to-all-start.1 = ((f32[32,8,8,128]{3,2,1,0:T(8,128)}), f32[32,8,8,128]{3,2,1,0:T(8,128)S(1)}, u32[]{:S(2)}, u32[]{:S(2)}) async-start(f32[32,8,8,128]{3,2,1,0:T(8,128)} %bitcast.5), calls=%async_computation.1 | async-start | bytes 2097152 | tf_op jit(solution)/shard_map/all_to_all | solution.py:735
  121.6 8.6 %collective-permute-start.16 = (f32[4,4,2048]{2,1,0:T(4,128)}, f32[4,4,2048]{2,1,0:T(4,128)}, u32[]{:S(2)}, u32[]{:S(2)}) collective-permute-start(f32[4,4,2048]{2,1,0:T(4,128)} %copy-done.9), channel_id=1, source_target_pairs={{0,1},{1,2},{2,3},{3,4},{4,5},{5,6},{6,7},{7,8},{8,9},{9,10},{10,1... | collective-permute-start | bytes 393224 | tf_op jit(solution)/shard_map/ppermute | solution.py:709
  123.5 7.1 %collective-permute-start.17 = (f32[4,4,2048]{2,1,0:T(4,128)}, f32[4,4,2048]{2,1,0:T(4,128)}, u32[]{:S(2)}, u32[]{:S(2)}) collective-permute-start(f32[4,4,2048]{2,1,0:T(4,128)} %copy-done.8), channel_id=1, source_target_pairs={{1,0},{2,1},{3,2},{4,3},{5,4},{6,5},{7,6},{8,7},{9,8},{10,9},{11,1... | collective-permute-start | bytes 393224 | tf_op jit(solution)/shard_map/ppermute | solution.py:710
  130.6 1.4 copy-start
  132.0 0.9 copy-start.7
  144.4 17.7 %copy-start.11 = (f32[1,256]{1,0:T(1,128)S(1)}, f32[1,256]{1,0:T(1,128)}, u32[]{:S(2)}) copy-start(f32[1,256]{1,0:T(1,128)} %param.8) | copy-start | bytes 3076
  153.2 31.4 %all-to-all-start.3 = ((f32[32,8,8,128]{3,2,1,0:T(8,128)}), f32[32,8,8,128]{3,2,1,0:T(8,128)S(1)}, u32[]{:S(2)}, u32[]{:S(2)}) async-start(f32[32,8,8,128]{3,2,1,0:T(8,128)} %bitcast.9), calls=%async_computation.3 | async-start | bytes 2097152 | tf_op jit(solution)/shard_map/all_to_all | solution.py:735
  169.9 0.7 copy-start.2
  170.6 31.3 %collective-permute-start.8 = (f32[2,264,128]{2,1,0:T(8,128)}, f32[2,264,128]{2,1,0:T(8,128)}, u32[]{:S(2)}, u32[]{:S(2)}) collective-permute-start(f32[2,264,128]{2,1,0:T(8,128)} %get-tuple-element.50), channel_id=1, source_target_pairs={{0,3},{1,0},{2,1},{3,2},{4,7},{5,4},{6,5},{7,6},{8,11},{9,8},{10,9... | collective-permute-start | bytes 811016 | tf_op jit(solution)/shard_map/ppermute | solution.py:701
  183.9 0.7 copy-start.4
  184.6 20.9 %collective-permute-start.4 = (f32[2,264,128]{2,1,0:T(8,128)}, f32[2,264,128]{2,1,0:T(8,128)}, u32[]{:S(2)}, u32[]{:S(2)}) collective-permute-start(f32[2,264,128]{2,1,0:T(8,128)} %get-tuple-element.45), channel_id=1, source_target_pairs={{0,1},{1,2},{2,3},{3,0},{4,5},{5,6},{6,7},{7,4},{8,9},{9,10},{10,1... | collective-permute-start | bytes 811016 | tf_op jit(solution)/shard_map/ppermute | solution.py:701
  191.6 10.1 %copy-start.3 = (f32[2,264,128]{2,1,0:T(8,128)S(1)}, f32[2,264,128]{2,1,0:T(8,128)}, u32[]{:S(2)}) copy-start(f32[2,264,128]{2,1,0:T(8,128)} %copy-done.2) | copy-start | bytes 811012
  191.6 10.2 %copy-start.5 = (f32[2,264,128]{2,1,0:T(8,128)S(1)}, f32[2,264,128]{2,1,0:T(8,128)}, u32[]{:S(2)}) copy-start(f32[2,264,128]{2,1,0:T(8,128)} %copy-done.4) | copy-start | bytes 811012
  191.7 16.3 %collective-permute-start.22 = (f32[2,264,128]{2,1,0:T(8,128)S(1)}, f32[2,264,128]{2,1,0:T(8,128)S(1)}, u32[]{:S(2)}, u32[]{:S(2)}) collective-permute-start(f32[2,264,128]{2,1,0:T(8,128)S(1)} %get-tuple-element.64), channel_id=1, source_target_pairs={{0,3},{1,0},{2,1},{3,2},{4,7},{5,4},{6,5},{7,6},{8,11},{9,8},{10,9... | collective-permute-start | bytes 811016 | tf_op jit(solution)/shard_map/ppermute | solution.py:701
  201.7 8.2 %collective-permute-start.18 = (f32[2,264,128]{2,1,0:T(8,128)S(1)}, f32[2,264,128]{2,1,0:T(8,128)S(1)}, u32[]{:S(2)}, u32[]{:S(2)}) collective-permute-start(f32[2,264,128]{2,1,0:T(8,128)S(1)} %get-tuple-element.59), channel_id=1, source_target_pairs={{0,1},{1,2},{2,3},{3,0},{4,5},{5,6},{6,7},{7,4},{8,9},{9,10},{10,1... | collective-permute-start | bytes 811016 | tf_op jit(solution)/shard_map/ppermute | solution.py:701
  201.8 13.9 %collective-permute-start.7 = (f32[2,264,128]{2,1,0:T(8,128)S(1)}, f32[2,264,128]{2,1,0:T(8,128)S(1)}, u32[]{:S(2)}, u32[]{:S(2)}) collective-permute-start(f32[2,264,128]{2,1,0:T(8,128)S(1)} %copy-done.3), channel_id=1, source_target_pairs={{0,1},{1,2},{2,3},{3,0},{4,5},{5,6},{6,7},{7,4},{8,9},{9,10},{10,1... | collective-permute-start | bytes 811016 | tf_op jit(solution)/shard_map/ppermute | solution.py:701
  201.9 13.8 %collective-permute-start.6 = (f32[2,264,128]{2,1,0:T(8,128)S(1)}, f32[2,264,128]{2,1,0:T(8,128)S(1)}, u32[]{:S(2)}, u32[]{:S(2)}) collective-permute-start(f32[2,264,128]{2,1,0:T(8,128)S(1)} %copy-done.5), channel_id=1, source_target_pairs={{0,3},{1,0},{2,1},{3,2},{4,7},{5,4},{6,5},{7,6},{8,11},{9,8},{10,9... | collective-permute-start | bytes 811016 | tf_op jit(solution)/shard_map/ppermute | solution.py:701
  205.5 10.2 %collective-permute-start.9 = (f32[2,264,128]{2,1,0:T(8,128)S(1)}, f32[2,264,128]{2,1,0:T(8,128)S(1)}, u32[]{:S(2)}, u32[]{:S(2)}) collective-permute-start(f32[2,264,128]{2,1,0:T(8,128)S(1)} %add.27), channel_id=1, source_target_pairs={{0,3},{1,0},{2,1},{3,2},{4,7},{5,4},{6,5},{7,6},{8,11},{9,8},{10,9... | collective-permute-start | bytes 811016 | tf_op jit(solution)/shard_map/ppermute | solution.py:701
  208.0 13.5 %collective-permute-start.5 = (f32[2,264,128]{2,1,0:T(8,128)S(1)}, f32[2,264,128]{2,1,0:T(8,128)S(1)}, u32[]{:S(2)}, u32[]{:S(2)}) collective-permute-start(f32[2,264,128]{2,1,0:T(8,128)S(1)} %add.26), channel_id=1, source_target_pairs={{0,1},{1,2},{2,3},{3,0},{4,5},{5,6},{6,7},{7,4},{8,9},{9,10},{10,1... | collective-permute-start | bytes 811016 | tf_op jit(solution)/shard_map/ppermute | solution.py:701
  209.9 17.4 %collective-permute-start.21 = (f32[2,264,128]{2,1,0:T(8,128)S(1)}, f32[2,264,128]{2,1,0:T(8,128)S(1)}, u32[]{:S(2)}, u32[]{:S(2)}) collective-permute-start(f32[2,264,128]{2,1,0:T(8,128)S(1)} %get-tuple-element.62), channel_id=1, source_target_pairs={{0,1},{1,2},{2,3},{3,0},{4,5},{5,6},{6,7},{7,4},{8,9},{9,10},{10,1... | collective-permute-start | bytes 811016 | tf_op jit(solution)/shard_map/ppermute | solution.py:701
  215.7 11.6 %collective-permute-start.20 = (f32[2,264,128]{2,1,0:T(8,128)S(1)}, f32[2,264,128]{2,1,0:T(8,128)S(1)}, u32[]{:S(2)}, u32[]{:S(2)}) collective-permute-start(f32[2,264,128]{2,1,0:T(8,128)S(1)} %get-tuple-element.60), channel_id=1, source_target_pairs={{0,3},{1,0},{2,1},{3,2},{4,7},{5,4},{6,5},{7,6},{8,11},{9,8},{10,9... | collective-permute-start | bytes 811016 | tf_op jit(solution)/shard_map/ppermute | solution.py:701
  215.7 11.6 %collective-permute-start.23 = (f32[2,264,128]{2,1,0:T(8,128)S(1)}, f32[2,264,128]{2,1,0:T(8,128)S(1)}, u32[]{:S(2)}, u32[]{:S(2)}) collective-permute-start(f32[2,264,128]{2,1,0:T(8,128)S(1)} %add.30), channel_id=1, source_target_pairs={{0,3},{1,0},{2,1},{3,2},{4,7},{5,4},{6,5},{7,6},{8,11},{9,8},{10,9... | collective-permute-start | bytes 811016 | tf_op jit(solution)/shard_map/ppermute | solution.py:701
  215.8 17.4 %collective-permute-start.19 = (f32[2,264,128]{2,1,0:T(8,128)S(1)}, f32[2,264,128]{2,1,0:T(8,128)S(1)}, u32[]{:S(2)}, u32[]{:S(2)}) collective-permute-start(f32[2,264,128]{2,1,0:T(8,128)S(1)} %add.29), channel_id=1, source_target_pairs={{0,1},{1,2},{2,3},{3,0},{4,5},{5,6},{6,7},{7,4},{8,9},{9,10},{10,1... | collective-permute-start | bytes 811016 | tf_op jit(solution)/shard_map/ppermute | solution.py:701
